TPU v7x, 128 devices: a whole 4x4x4 slice. The times are simulated.
128 devices in a mesh: layer: 4 (over x), col: 32 (over z, y, core).
Axes of the slice: x: 4, y: 4, z: 4, core: 2. Of those that a mesh axis runs over, the one named last changes fastest.
Arguments:
- inputs: bfloat16 [4, 128, 4096], replicated, may hold values from -6 to 6
- w_input: bfloat16 [4, 4096, 4, 4096], P('layer', None, None, 'col'), may hold values from -0.09375 to 0.09375
- w_recur: bfloat16 [4, 4096, 4, 4096], P('layer', None, None, 'col'), may hold values from -0.09375 to 0.09375
- bias: float32 [4, 4, 4096], P('layer', None, 'col'), may hold values from -1 to 2
- h_start: bfloat16 [4, 128, 4096], P('layer', None, 'col'), may hold values from -3 to 3
- c_start: float32 [4, 128, 4096], P('layer', None, 'col'), may hold values from -6 to 6
Outputs:
- hidden_seq: bfloat16 [4, 4, 128, 4096], P('layer', None, None, 'col')
- cell_final: float32 [4, 128, 4096], P('layer', None, 'col')
All inputs are finite; a program needn't handle non-finite values.
Results may differ from a plain program's by a relative error of at most 0.0024.
Values may be sent and summed in bfloat16 or wider, within the bound.
No kernel may reach another device: no remote copies, remote signals or barrier semaphores. Data moves between devices by JAX's collectives and lax.ppermute only.
A program may use at most 64 MiB of HBM per device.

v0:
```python
import jax
import jax.numpy as jnp
from jax import lax
from jax.sharding import PartitionSpec as P


def copy_for_each(x, axis):
    copies = jnp.broadcast_to(x, (lax.axis_size(axis), *x.shape))
    return lax.all_to_all(copies, axis, split_axis=0, concat_axis=0, tiled=True)


def joined_along(parts, dim):
    parts = jnp.moveaxis(parts, 0, dim)
    lengths = parts.shape
    return parts.reshape(*lengths[:dim], lengths[dim] * lengths[dim + 1], *lengths[dim + 2 :])


def gather_directly(x, axis, dim):
    parts = copy_for_each(x, axis)
    return joined_along(parts, dim)


def passed_along(value, axis, steps):
    count = lax.axis_size(axis)
    first, last = (max(0, -steps), min(count, count - steps))
    return lax.ppermute(value, axis, [(source, source + steps) for source in range(first, last)])


def body(inputs, w_input, w_recur, bias, h_start, c_start):
    steps = inputs.shape[0]
    batch = inputs.shape[1]
    width = inputs.shape[2]
    local = w_input.shape[3]
    span = steps // 4
    count = steps // span
    groups = lax.axis_size("layer")
    rounds = count + groups - 1
    section = lax.axis_index("layer")
    weight_in = w_input[0].reshape(width, 4 * local)
    weight_rec = w_recur[0].reshape(width, 4 * local)
    offset = bias[0].reshape(4 * local)
    hidden_full = gather_directly(h_start[0], "col", 1)
    cell = c_start[0]
    sequence = jnp.zeros((steps, batch, local), jnp.bfloat16)
    arrived = jnp.zeros((span, batch, width), jnp.bfloat16)

    def advance(carry, z_in):
        hidden_prev, cell_prev = carry
        gates = z_in + jnp.dot(hidden_prev, weight_rec, preferred_element_type=jnp.float32)
        gates = gates.reshape(batch, 4, local)
        cell_new = jax.nn.sigmoid(gates[:, 1]) * cell_prev + jax.nn.sigmoid(gates[:, 0]) * jnp.tanh(
            gates[:, 2]
        )
        hidden_new = (jax.nn.sigmoid(gates[:, 3]) * jnp.tanh(cell_new)).astype(jnp.bfloat16)
        hidden_wide = gather_directly(hidden_new, "col", 1)
        return ((hidden_wide, cell_new), (hidden_new, hidden_wide))

    for turn in range(rounds):
        block_id = turn - section
        valid = jnp.logical_and(block_id >= 0, block_id < count)
        start = jnp.clip(block_id, 0, count - 1) * span
        own_block = lax.dynamic_slice_in_dim(inputs, start, span, 0)
        source = jnp.where(section == 0, own_block, arrived)
        projected = (
            jnp.dot(
                source.reshape(span * batch, width), weight_in, preferred_element_type=jnp.float32
            )
            + offset
        )
        projected = projected.reshape(span, batch, 4 * local)
        (hidden_next, cell_next), (shards, wides) = lax.scan(
            advance, (hidden_full, cell), projected
        )
        hidden_full = jnp.where(valid, hidden_next, hidden_full)
        cell = jnp.where(valid, cell_next, cell)
        sequence = jnp.where(
            valid, lax.dynamic_update_slice_in_dim(sequence, shards, start, 0), sequence
        )
        if turn + 1 < rounds:
            received = passed_along(shards, "layer", 1)
            arrived = gather_directly(received, "col", 2)
    return (sequence[None], cell[None])


def solution(mesh):
    in_specs = (
        P(),
        P("layer", None, None, "col"),
        P("layer", None, None, "col"),
        P("layer", None, "col"),
        P("layer", None, "col"),
        P("layer", None, "col"),
    )
    out_specs = (P("layer", None, None, "col"), P("layer", None, "col"))
    return jax.shard_map(body, mesh=mesh, in_specs=in_specs, out_specs=out_specs, check_vma=False)
```

profile of v0, /device:TPU:1, one launch (start us, length us, event | category | flops | bytes accessed | tf_op | source)
XLA Modules:
  0.0 362.8 jit_solution(10242357486044283308)
XLA Ops:
  2.7 9.6 %all-to-all-start = ((bf16[32,128,128]{1,2,0:T(8,128)(2,1)}), bf16[32,128,128]{1,2,0:T(8,128)(2,1)S(1)}, u32[]{:S(2)}, u32[]{:S(2)}) async-start(bf16[32,128,128]{1,2,0:T(8,128)(2,1)} %broadcast_in_dim.76), calls=%async_computation | async-start | bytes 2097152 | tf_op jit(solution)/shard_map/all_to_all | solution.py:9
  12.4 5.9 %constant_dynamic-slice_fusion.1 = (bf16[1,128,4096]{2,1,0:T(8,128)(2,1)}, bf16[1,128,4096]{2,1,0:T(8,128)(2,1)}, bf16[1,128,4096]{2,1,0:T(8,128)(2,1)}, bf16[1,...) fusion(bf16[4,128,4096]{2,1,0:T(8,128)(2,1)} %param.6, ...), kind=kLoop, calls=%fused_computation.168 | loop fusion | bytes 14680092 | tf_op jit(solution)/shard_map/dynamic_slice | solution.py:62
  20.6 4.0 %fusion.42 = f32[128,512]{1,0:T(8,128)} fusion(bf16[512,8,4,128]{3,2,1,0:T(4,128)(2,1)} %bitcast.548, bf16[1,128,4096]{1,2,0:T(8,128)(2,1)} %copy.154, pred[]{:T(512)S(6)} %eq.2, f32[512]{0:T(512)S(1)} %bitcast.555), kind=kOutput, calls=%fused_computation.42 | convolution fusion | flops 537460736 | bytes 5507073 | tf_op jit(solution)/shard_map/dot_general | solution.py:65
  24.5 4.9 %all-to-all-done = bf16[32,128,128]{1,2,0:T(8,128)(2,1)S(1)} async-done(((bf16[32,128,128]{1,2,0:T(8,128)(2,1)}), bf16[32,128,128]{1,2,0:T(8,128)(2,1)S(1)}, u32[]{:S(2)}, u32[]{:S(2)}) %all-to-all-start) | async-done | bytes 1048608 | tf_op jit(solution)/shard_map/all_to_all | solution.py:9
  36.3 4.6 %all-to-all-start.2 = ((bf16[32,128,128]{1,2,0:T(8,128)(2,1)}), bf16[32,128,128]{1,2,0:T(8,128)(2,1)}, u32[]{:S(2)}, u32[]{:S(2)}) async-start(bf16[32,128,128]{1,2,0:T(8,128)(2,1)} %broadcast_in_dim.78), calls=%async_computation.2 | async-start | bytes 2097152 | tf_op jit(solution)/shard_map/while/body/eval_jaxpr/all_to_all | solution.py:9
  42.3 3.1 collective-permute-start
  46.4 11.7 %all-to-all-done.2 = bf16[32,128,128]{1,2,0:T(8,128)(2,1)} async-done(((bf16[32,128,128]{1,2,0:T(8,128)(2,1)}), bf16[32,128,128]{1,2,0:T(8,128)(2,1)}, u32[]{:S(2)}, u32[]{:S(2)}) %all-to-all-start.2) | async-done | bytes 1048608 | tf_op jit(solution)/shard_map/while/body/eval_jaxpr/all_to_all | solution.py:9
  59.4 4.6 %all-to-all-start.1 = ((bf16[32,1,128,128]{3,2,1,0:T(8,128)(2,1)}), bf16[32,1,128,128]{3,2,1,0:T(8,128)(2,1)}, u32[]{:S(2)}, u32[]{:S(2)}) async-start(bf16[32,1,128,128]{3,2,1,0:T(8,128)(2,1)} %broadcast_in_dim.77), calls=%async_computation.1 | async-start | bytes 2097152 | tf_op jit(solution)/shard_map/all_to_all | solution.py:9
  66.8 14.5 %all-to-all-done.1 = bf16[32,1,128,128]{3,2,1,0:T(8,128)(2,1)} async-done(((bf16[32,1,128,128]{3,2,1,0:T(8,128)(2,1)}), bf16[32,1,128,128]{3,2,1,0:T(8,128)(2,1)}, u32[]{:S(2)}, u32[]{:S(2)}) %all-to-all-start.1) | async-done | bytes 1048608 | tf_op jit(solution)/shard_map/all_to_all | solution.py:9
  84.4 3.1 fusion.45
  96.7 4.6 %all-to-all-start.4 = ((bf16[32,128,128]{1,2,0:T(8,128)(2,1)}), bf16[32,128,128]{1,2,0:T(8,128)(2,1)}, u32[]{:S(2)}, u32[]{:S(2)}) async-start(bf16[32,128,128]{1,2,0:T(8,128)(2,1)} %broadcast_in_dim.80), calls=%async_computation.4 | async-start | bytes 2097152 | tf_op jit(solution)/shard_map/while/body/eval_jaxpr/all_to_all | solution.py:9
  105.8 12.7 %all-to-all-done.4 = bf16[32,128,128]{1,2,0:T(8,128)(2,1)} async-done(((bf16[32,128,128]{1,2,0:T(8,128)(2,1)}), bf16[32,128,128]{1,2,0:T(8,128)(2,1)}, u32[]{:S(2)}, u32[]{:S(2)}) %all-to-all-start.4) | async-done | bytes 1048608 | tf_op jit(solution)/shard_map/while/body/eval_jaxpr/all_to_all | solution.py:9
  119.8 4.6 %all-to-all-start.3 = ((bf16[32,1,128,128]{3,2,1,0:T(8,128)(2,1)}), bf16[32,1,128,128]{3,2,1,0:T(8,128)(2,1)}, u32[]{:S(2)}, u32[]{:S(2)}) async-start(bf16[32,1,128,128]{3,2,1,0:T(8,128)(2,1)} %broadcast_in_dim.79), calls=%async_computation.3 | async-start | bytes 2097152 | tf_op jit(solution)/shard_map/all_to_all | solution.py:9
  127.1 14.6 %all-to-all-done.3 = bf16[32,1,128,128]{3,2,1,0:T(8,128)(2,1)} async-done(((bf16[32,1,128,128]{3,2,1,0:T(8,128)(2,1)}), bf16[32,1,128,128]{3,2,1,0:T(8,128)(2,1)}, u32[]{:S(2)}, u32[]{:S(2)}) %all-to-all-start.3) | async-done | bytes 1048608 | tf_op jit(solution)/shard_map/all_to_all | solution.py:9
  144.8 3.0 fusion.48
  150.4 4.0 %all-to-all-start.6 = ((bf16[32,128,128]{1,2,0:T(8,128)(2,1)}), bf16[32,128,128]{1,2,0:T(8,128)(2,1)S(1)}, u32[]{:S(2)}, u32[]{:S(2)}) async-start(bf16[32,128,128]{1,2,0:T(8,128)(2,1)} %broadcast_in_dim.82), calls=%async_computation.6 | async-start | bytes 2097152 | tf_op jit(solution)/shard_map/while/body/eval_jaxpr/all_to_all | solution.py:9
  158.3 13.2 %all-to-all-done.6 = bf16[32,128,128]{1,2,0:T(8,128)(2,1)S(1)} async-done(((bf16[32,128,128]{1,2,0:T(8,128)(2,1)}), bf16[32,128,128]{1,2,0:T(8,128)(2,1)S(1)}, u32[]{:S(2)}, u32[]{:S(2)}) %all-to-all-start.6) | async-done | bytes 1048608 | tf_op jit(solution)/shard_map/while/body/eval_jaxpr/all_to_all | solution.py:9
  172.8 4.6 %all-to-all-start.5 = ((bf16[32,1,128,128]{3,2,1,0:T(8,128)(2,1)}), bf16[32,1,128,128]{3,2,1,0:T(8,128)(2,1)}, u32[]{:S(2)}, u32[]{:S(2)}) async-start(bf16[32,1,128,128]{3,2,1,0:T(8,128)(2,1)} %broadcast_in_dim.81), calls=%async_computation.5 | async-start | bytes 2097152 | tf_op jit(solution)/shard_map/all_to_all | solution.py:9
  178.9 15.8 %all-to-all-done.5 = bf16[32,1,128,128]{3,2,1,0:T(8,128)(2,1)} async-done(((bf16[32,1,128,128]{3,2,1,0:T(8,128)(2,1)}), bf16[32,1,128,128]{3,2,1,0:T(8,128)(2,1)}, u32[]{:S(2)}, u32[]{:S(2)}) %all-to-all-start.5) | async-done | bytes 1048608 | tf_op jit(solution)/shard_map/all_to_all | solution.py:9
  204.0 4.0 %all-to-all-start.8 = ((bf16[32,128,128]{1,2,0:T(8,128)(2,1)}), bf16[32,128,128]{1,2,0:T(8,128)(2,1)S(1)}, u32[]{:S(2)}, u32[]{:S(2)}) async-start(bf16[32,128,128]{1,2,0:T(8,128)(2,1)} %broadcast_in_dim.84), calls=%async_computation.8 | async-start | bytes 2097152 | tf_op jit(solution)/shard_map/while/body/eval_jaxpr/all_to_all | solution.py:9
  211.9 13.3 %all-to-all-done.8 = bf16[32,128,128]{1,2,0:T(8,128)(2,1)S(1)} async-done(((bf16[32,128,128]{1,2,0:T(8,128)(2,1)}), bf16[32,128,128]{1,2,0:T(8,128)(2,1)S(1)}, u32[]{:S(2)}, u32[]{:S(2)}) %all-to-all-start.8) | async-done | bytes 1048608 | tf_op jit(solution)/shard_map/while/body/eval_jaxpr/all_to_all | solution.py:9
  226.4 4.6 %all-to-all-start.7 = ((bf16[32,1,128,128]{3,2,1,0:T(8,128)(2,1)}), bf16[32,1,128,128]{3,2,1,0:T(8,128)(2,1)}, u32[]{:S(2)}, u32[]{:S(2)}) async-start(bf16[32,1,128,128]{3,2,1,0:T(8,128)(2,1)} %broadcast_in_dim.83), calls=%async_computation.7 | async-start | bytes 2097152 | tf_op jit(solution)/shard_map/all_to_all | solution.py:9
  232.5 15.8 %all-to-all-done.7 = bf16[32,1,128,128]{3,2,1,0:T(8,128)(2,1)} async-done(((bf16[32,1,128,128]{3,2,1,0:T(8,128)(2,1)}), bf16[32,1,128,128]{3,2,1,0:T(8,128)(2,1)}, u32[]{:S(2)}, u32[]{:S(2)}) %all-to-all-start.7) | async-done | bytes 1048608 | tf_op jit(solution)/shard_map/all_to_all | solution.py:9
  257.0 4.0 %all-to-all-start.10 = ((bf16[32,128,128]{1,2,0:T(8,128)(2,1)}), bf16[32,128,128]{1,2,0:T(8,128)(2,1)S(1)}, u32[]{:S(2)}, u32[]{:S(2)}) async-start(bf16[32,128,128]{1,2,0:T(8,128)(2,1)} %broadcast_in_dim.86), calls=%async_computation.10 | async-start | bytes 2097152 | tf_op jit(solution)/shard_map/while/body/eval_jaxpr/all_to_all | solution.py:9
  264.9 13.2 %all-to-all-done.10 = bf16[32,128,128]{1,2,0:T(8,128)(2,1)S(1)} async-done(((bf16[32,128,128]{1,2,0:T(8,128)(2,1)}), bf16[32,128,128]{1,2,0:T(8,128)(2,1)S(1)}, u32[]{:S(2)}, u32[]{:S(2)}) %all-to-all-start.10) | async-done | bytes 1048608 | tf_op jit(solution)/shard_map/while/body/eval_jaxpr/all_to_all | solution.py:9
  279.4 4.6 %all-to-all-start.9 = ((bf16[32,1,128,128]{3,2,1,0:T(8,128)(2,1)}), bf16[32,1,128,128]{3,2,1,0:T(8,128)(2,1)}, u32[]{:S(2)}, u32[]{:S(2)}) async-start(bf16[32,1,128,128]{3,2,1,0:T(8,128)(2,1)} %broadcast_in_dim.85), calls=%async_computation.9 | async-start | bytes 2097152 | tf_op jit(solution)/shard_map/all_to_all | solution.py:9
  285.5 15.8 %all-to-all-done.9 = bf16[32,1,128,128]{3,2,1,0:T(8,128)(2,1)} async-done(((bf16[32,1,128,128]{3,2,1,0:T(8,128)(2,1)}), bf16[32,1,128,128]{3,2,1,0:T(8,128)(2,1)}, u32[]{:S(2)}, u32[]{:S(2)}) %all-to-all-start.9) | async-done | bytes 1048608 | tf_op jit(solution)/shard_map/all_to_all | solution.py:9
  310.0 4.0 %all-to-all-start.12 = ((bf16[32,128,128]{1,2,0:T(8,128)(2,1)}), bf16[32,128,128]{1,2,0:T(8,128)(2,1)S(1)}, u32[]{:S(2)}, u32[]{:S(2)}) async-start(bf16[32,128,128]{1,2,0:T(8,128)(2,1)} %broadcast_in_dim.89), calls=%async_computation.12 | async-start | bytes 2097152 | tf_op jit(solution)/shard_map/while/body/eval_jaxpr/all_to_all | solution.py:9
  317.9 13.2 %all-to-all-done.12 = bf16[32,128,128]{1,2,0:T(8,128)(2,1)S(1)} async-done(((bf16[32,128,128]{1,2,0:T(8,128)(2,1)}), bf16[32,128,128]{1,2,0:T(8,128)(2,1)S(1)}, u32[]{:S(2)}, u32[]{:S(2)}) %all-to-all-start.12) | async-done | bytes 1048608 | tf_op jit(solution)/shard_map/while/body/eval_jaxpr/all_to_all | solution.py:9
  332.4 4.6 %all-to-all-start.11 = ((bf16[32,1,128,128]{3,2,1,0:T(8,128)(2,1)}), bf16[32,1,128,128]{3,2,1,0:T(8,128)(2,1)}, u32[]{:S(2)}, u32[]{:S(2)}) async-start(bf16[32,1,128,128]{3,2,1,0:T(8,128)(2,1)} %broadcast_in_dim.88), calls=%async_computation.11 | async-start | bytes 2097152 | tf_op jit(solution)/shard_map/all_to_all | solution.py:9
  341.1 13.1 %all-to-all-done.11 = bf16[32,1,128,128]{3,2,1,0:T(8,128)(2,1)} async-done(((bf16[32,1,128,128]{3,2,1,0:T(8,128)(2,1)}), bf16[32,1,128,128]{3,2,1,0:T(8,128)(2,1)}, u32[]{:S(2)}, u32[]{:S(2)}) %all-to-all-start.11) | async-done | bytes 1048608 | tf_op jit(solution)/shard_map/all_to_all | solution.py:9
  356.1 3.1 fusion.60
  (148 shorter events, 104.7 us)
Async XLA Ops:
  2.7 26.6 %all-to-all-start = ((bf16[32,128,128]{1,2,0:T(8,128)(2,1)}), bf16[32,128,128]{1,2,0:T(8,128)(2,1)S(1)}, u32[]{:S(2)}, u32[]{:S(2)}) async-start(bf16[32,128,128]{1,2,0:T(8,128)(2,1)} %broadcast_in_dim.76), calls=%async_computation | async-start | bytes 2097152 | tf_op jit(solution)/shard_map/all_to_all | solution.py:9
  12.4 8.2 %copy-start.25 = (f32[1,4,128]{2,1,0:T(4,128)S(1)}, f32[1,4,128]{2,1,0:T(4,128)}, u32[]{:S(2)}) copy-start(f32[1,4,128]{2,1,0:T(4,128)} %param.9) | copy-start | bytes 6148
  24.5 10.3 %copy-start.12 = (f32[1,128,128]{2,1,0:T(8,128)S(1)}, f32[1,128,128]{2,1,0:T(8,128)}, u32[]{:S(2)}) copy-start(f32[1,128,128]{2,1,0:T(8,128)} %param.11) | copy-start | bytes 196612
  34.9 66.4 %copy-start.13 = (f32[128,1,128]{2,0,1:T(8,128)}, f32[128,1,128]{2,0,1:T(8,128)S(1)}, u32[]{:S(2)}) copy-start(f32[128,1,128]{2,0,1:T(8,128)S(1)} %get-tuple-element.135) | copy-start | bytes 196612
  36.3 21.9 %all-to-all-start.2 = ((bf16[32,128,128]{1,2,0:T(8,128)(2,1)}), bf16[32,128,128]{1,2,0:T(8,128)(2,1)}, u32[]{:S(2)}, u32[]{:S(2)}) async-start(bf16[32,128,128]{1,2,0:T(8,128)(2,1)} %broadcast_in_dim.78), calls=%async_computation.2 | async-start | bytes 2097152 | tf_op jit(solution)/shard_map/while/body/eval_jaxpr/all_to_all | solution.py:9
  42.3 4.1 %collective-permute-start = (bf16[1,128,128]{2,1,0:T(8,128)(2,1)S(1)}, bf16[1,128,128]{2,1,0:T(8,128)(2,1)S(1)}, u32[]{:S(2)}, u32[]{:S(2)}) collective-permute-start(bf16[1,128,128]{2,1,0:T(8,128)(2,1)S(1)} %get-tuple-element.137), channel_id=1, source_target_pairs={{0,32},{32,64},{64,96},{1,33},{33,65},{65,97},{2,34},{34,66},{66,9... | collective-permute-start | bytes 98312 | tf_op jit(solution)/shard_map/ppermute | solution.py:26
  59.4 21.8 %all-to-all-start.1 = ((bf16[32,1,128,128]{3,2,1,0:T(8,128)(2,1)}), bf16[32,1,128,128]{3,2,1,0:T(8,128)(2,1)}, u32[]{:S(2)}, u32[]{:S(2)}) async-start(bf16[32,1,128,128]{3,2,1,0:T(8,128)(2,1)} %broadcast_in_dim.77), calls=%async_computation.1 | async-start | bytes 2097152 | tf_op jit(solution)/shard_map/all_to_all | solution.py:9
  82.9 4.6 %copy-start = (bf16[1,4096,4,128]{3,2,1,0:T(4,128)(2,1)S(1)}, bf16[1,4096,4,128]{3,2,1,0:T(4,128)(2,1)}, u32[]{:S(2)}) copy-start(bf16[1,4096,4,128]{3,2,1,0:T(4,128)(2,1)} %param.8) | copy-start | bytes 12582916
  89.0 35.4 %copy-start.9 = (bf16[1,128,4096]{2,1,0:T(8,128)(2,1)S(1)}, bf16[1,128,4096]{2,1,0:T(8,128)(2,1)}, u32[]{:S(2)}) copy-start(bf16[1,128,4096]{2,1,0:T(8,128)(2,1)} %get-tuple-element.148) | copy-start | bytes 3145732
  96.7 21.8 %all-to-all-start.4 = ((bf16[32,128,128]{1,2,0:T(8,128)(2,1)}), bf16[32,128,128]{1,2,0:T(8,128)(2,1)}, u32[]{:S(2)}, u32[]{:S(2)}) async-start(bf16[32,128,128]{1,2,0:T(8,128)(2,1)} %broadcast_in_dim.80), calls=%async_computation.4 | async-start | bytes 2097152 | tf_op jit(solution)/shard_map/while/body/eval_jaxpr/all_to_all | solution.py:9
  102.8 3.0 collective-permute-start.1
  119.8 21.9 %all-to-all-start.3 = ((bf16[32,1,128,128]{3,2,1,0:T(8,128)(2,1)}), bf16[32,1,128,128]{3,2,1,0:T(8,128)(2,1)}, u32[]{:S(2)}, u32[]{:S(2)}) async-start(bf16[32,1,128,128]{3,2,1,0:T(8,128)(2,1)} %broadcast_in_dim.79), calls=%async_computation.3 | async-start | bytes 2097152 | tf_op jit(solution)/shard_map/all_to_all | solution.py:9
  143.3 4.6 %copy-start.1 = (bf16[1,4096,4,128]{3,2,1,0:T(4,128)(2,1)S(1)}, bf16[1,4096,4,128]{3,2,1,0:T(4,128)(2,1)}, u32[]{:S(2)}) copy-start(bf16[1,4096,4,128]{3,2,1,0:T(4,128)(2,1)} %param.8) | copy-start | bytes 12582916
  150.4 21.2 %all-to-all-start.6 = ((bf16[32,128,128]{1,2,0:T(8,128)(2,1)}), bf16[32,128,128]{1,2,0:T(8,128)(2,1)S(1)}, u32[]{:S(2)}, u32[]{:S(2)}) async-start(bf16[32,128,128]{1,2,0:T(8,128)(2,1)} %broadcast_in_dim.82), calls=%async_computation.6 | async-start | bytes 2097152 | tf_op jit(solution)/shard_map/while/body/eval_jaxpr/all_to_all | solution.py:9
  156.1 2.3 collective-permute-start.2
  172.8 21.9 %all-to-all-start.5 = ((bf16[32,1,128,128]{3,2,1,0:T(8,128)(2,1)}), bf16[32,1,128,128]{3,2,1,0:T(8,128)(2,1)}, u32[]{:S(2)}, u32[]{:S(2)}) async-start(bf16[32,1,128,128]{3,2,1,0:T(8,128)(2,1)} %broadcast_in_dim.81), calls=%async_computation.5 | async-start | bytes 2097152 | tf_op jit(solution)/shard_map/all_to_all | solution.py:9
  196.3 4.5 %copy-start.2 = (bf16[1,4096,4,128]{3,2,1,0:T(4,128)(2,1)S(1)}, bf16[1,4096,4,128]{3,2,1,0:T(4,128)(2,1)}, u32[]{:S(2)}) copy-start(bf16[1,4096,4,128]{3,2,1,0:T(4,128)(2,1)} %param.8) | copy-start | bytes 12582916
  201.7 29.3 %copy-start.8 = (bf16[1,128,4096]{2,1,0:T(8,128)(2,1)S(1)}, bf16[1,128,4096]{2,1,0:T(8,128)(2,1)}, u32[]{:S(2)}) copy-start(bf16[1,128,4096]{2,1,0:T(8,128)(2,1)} %get-tuple-element.146) | copy-start | bytes 3145732
  204.0 21.1 %all-to-all-start.8 = ((bf16[32,128,128]{1,2,0:T(8,128)(2,1)}), bf16[32,128,128]{1,2,0:T(8,128)(2,1)S(1)}, u32[]{:S(2)}, u32[]{:S(2)}) async-start(bf16[32,128,128]{1,2,0:T(8,128)(2,1)} %broadcast_in_dim.84), calls=%async_computation.8 | async-start | bytes 2097152 | tf_op jit(solution)/shard_map/while/body/eval_jaxpr/all_to_all | solution.py:9
  209.6 2.3 collective-permute-start.3
  226.4 21.9 %all-to-all-start.7 = ((bf16[32,1,128,128]{3,2,1,0:T(8,128)(2,1)}), bf16[32,1,128,128]{3,2,1,0:T(8,128)(2,1)}, u32[]{:S(2)}, u32[]{:S(2)}) async-start(bf16[32,1,128,128]{3,2,1,0:T(8,128)(2,1)} %broadcast_in_dim.83), calls=%async_computation.7 | async-start | bytes 2097152 | tf_op jit(solution)/shard_map/all_to_all | solution.py:9
  249.9 4.5 %copy-start.3 = (bf16[1,4096,4,128]{3,2,1,0:T(4,128)(2,1)S(1)}, bf16[1,4096,4,128]{3,2,1,0:T(4,128)(2,1)}, u32[]{:S(2)}) copy-start(bf16[1,4096,4,128]{3,2,1,0:T(4,128)(2,1)} %param.8) | copy-start | bytes 12582916
  255.3 28.7 %copy-start.7 = (bf16[1,128,4096]{2,1,0:T(8,128)(2,1)S(1)}, bf16[1,128,4096]{2,1,0:T(8,128)(2,1)}, u32[]{:S(2)}) copy-start(bf16[1,128,4096]{2,1,0:T(8,128)(2,1)} %get-tuple-element.145) | copy-start | bytes 3145732
  257.0 21.1 %all-to-all-start.10 = ((bf16[32,128,128]{1,2,0:T(8,128)(2,1)}), bf16[32,128,128]{1,2,0:T(8,128)(2,1)S(1)}, u32[]{:S(2)}, u32[]{:S(2)}) async-start(bf16[32,128,128]{1,2,0:T(8,128)(2,1)} %broadcast_in_dim.86), calls=%async_computation.10 | async-start | bytes 2097152 | tf_op jit(solution)/shard_map/while/body/eval_jaxpr/all_to_all | solution.py:9
  262.6 2.3 collective-permute-start.4
  279.4 21.9 %all-to-all-start.9 = ((bf16[32,1,128,128]{3,2,1,0:T(8,128)(2,1)}), bf16[32,1,128,128]{3,2,1,0:T(8,128)(2,1)}, u32[]{:S(2)}, u32[]{:S(2)}) async-start(bf16[32,1,128,128]{3,2,1,0:T(8,128)(2,1)} %broadcast_in_dim.85), calls=%async_computation.9 | async-start | bytes 2097152 | tf_op jit(solution)/shard_map/all_to_all | solution.py:9
  302.8 4.5 %copy-start.4 = (bf16[1,4096,4,128]{3,2,1,0:T(4,128)(2,1)S(1)}, bf16[1,4096,4,128]{3,2,1,0:T(4,128)(2,1)}, u32[]{:S(2)}) copy-start(bf16[1,4096,4,128]{3,2,1,0:T(4,128)(2,1)} %param.8) | copy-start | bytes 12582916
  308.3 28.7 %copy-start.6 = (bf16[1,128,4096]{2,1,0:T(8,128)(2,1)S(1)}, bf16[1,128,4096]{2,1,0:T(8,128)(2,1)}, u32[]{:S(2)}) copy-start(bf16[1,128,4096]{2,1,0:T(8,128)(2,1)} %get-tuple-element.144) | copy-start | bytes 3145732
  310.0 21.1 %all-to-all-start.12 = ((bf16[32,128,128]{1,2,0:T(8,128)(2,1)}), bf16[32,128,128]{1,2,0:T(8,128)(2,1)S(1)}, u32[]{:S(2)}, u32[]{:S(2)}) async-start(bf16[32,128,128]{1,2,0:T(8,128)(2,1)} %broadcast_in_dim.89), calls=%async_computation.12 | async-start | bytes 2097152 | tf_op jit(solution)/shard_map/while/body/eval_jaxpr/all_to_all | solution.py:9
  315.6 2.3 collective-permute-start.5
  332.4 21.9 %all-to-all-start.11 = ((bf16[32,1,128,128]{3,2,1,0:T(8,128)(2,1)}), bf16[32,1,128,128]{3,2,1,0:T(8,128)(2,1)}, u32[]{:S(2)}, u32[]{:S(2)}) async-start(bf16[32,1,128,128]{3,2,1,0:T(8,128)(2,1)} %broadcast_in_dim.88), calls=%async_computation.11 | async-start | bytes 2097152 | tf_op jit(solution)/shard_map/all_to_all | solution.py:9
  338.3 17.5 %copy-start.10 = (bf16[1,128,4096]{1,2,0:T(8,128)(2,1)S(1)}, bf16[1,128,4096]{1,2,0:T(8,128)(2,1)}, u32[]{:S(2)}) copy-start(bf16[1,128,4096]{1,2,0:T(8,128)(2,1)} %copy.184) | copy-start | bytes 3145732
  (13 other events, 22.8 us)
where the time goes:
time: 365 us; the launch traced here: 363 us
  waiting for transfers between devices  178 us (49%)
  starting transfers between devices  72.8 us (20%)
  local copies, waits for them, and re-layouts  55.7 us (15%)
  matrix products  30.5 us (8%)
  other arithmetic  24.4 us (7%)
    all_to_all x13, waiting for transfers between devices, copy_for_each(): return lax.all_to_all(copies, axis, split_axis=0, concat_axis=0, tiled=True)  172 us
    all_to_all x13, starting transfers between devices, copy_for_each(): return lax.all_to_all(copies, axis, split_axis=0, concat_axis=0, tiled=True)  62.6 us
    dot_general x7, matrix products, body(): jnp.dot(source.reshape(span * batch, width), weight_in, preferred_element...  22.1 us
    broadcast_in_dim x13, local copies, waits for them, and re-layouts, copy_for_each(): copies = jnp.broadcast_to(x, (lax.axis_size(axis), *x.shape))  16.8 us
    unnamed x60, local copies, waits for them, and re-layouts  12.4 us
    ppermute x6, starting transfers between devices, passed_along(): lax.ppermute(value, axis, [(source, source + steps) for source in range(f...  10.2 us
    select_n x7, other arithmetic, body(): jnp.where(valid, lax.dynamic_update_slice_in_dim(sequence, shards, start,...  10 us
    all_to_all x6, local copies, waits for them, and re-layouts, copy_for_each(): return lax.all_to_all(copies, axis, split_axis=0, concat_axis=0, tiled=True)  9.68 us
  transfers between devices with their start and end apart: 19, of which 19 were waited for; matrix products, arithmetic and copies ran while one was open for 10% of the time, Pallas kernels for 0%

commit v1 on v0

v1 whole, which is shorter than its diff:
```python
import functools

import jax
import jax.numpy as jnp
from jax import lax
from jax.experimental import pallas as pl
from jax.experimental.pallas import tpu as pltpu
from jax.sharding import PartitionSpec as P


def in_vmem(count):
    return [pl.BlockSpec(memory_space=pltpu.VMEM)] * count


def product_kernel(depth, g_ref, w_ref, out_ref):
    blocks = g_ref.shape[0]
    wide = 256
    for n in range(out_ref.shape[1] // wide):
        cols = slice(n * wide, (n + 1) * wide)
        total = None
        for j in range(blocks):
            term = jnp.dot(
                g_ref[j], w_ref[j, :depth, cols], preferred_element_type=jnp.float32
            )
            total = term if total is None else total + term
        out_ref[:, cols] = total


def product(g, w):
    blocks, rows, depth = g.shape
    width = w.shape[2]
    return pl.pallas_call(
        functools.partial(product_kernel, depth),
        out_shape=jax.ShapeDtypeStruct((rows, width), jnp.float32),
        in_specs=in_vmem(2),
        out_specs=pl.BlockSpec(memory_space=pltpu.VMEM),
        cost_estimate=pl.CostEstimate(
            flops=2 * blocks * rows * depth * width,
            bytes_accessed=2 * blocks * depth * (rows + width) + 4 * rows * width,
            transcendentals=0,
        ),
        compiler_params=pltpu.CompilerParams(vmem_limit_bytes=16 << 20),
    )(g, w)


def body(inputs, w_input, w_recur, bias, h_start, c_start):
    steps, batch, width = inputs.shape
    unit = w_input.shape[3]
    layers = lax.axis_size("layer")
    devices = lax.axis_size("col")
    chips = devices // 2
    turns = steps + layers - 1
    layer = lax.axis_index("layer")
    core = lax.axis_index("col") % 2
    same_core = [[2 * chip + side for chip in range(chips)] for side in range(2)]
    partners = [(i, i ^ 1) for i in range(devices)]
    upward = [(i, i + 1) for i in range(layers - 1)]

    def across(x):
        return lax.ppermute(x, "col", partners)

    def gathered(x):
        copies = jnp.broadcast_to(x, (chips, *x.shape))
        return lax.all_to_all(copies, "col", 0, 0, tiled=True, axis_index_groups=same_core)

    start = gathered(h_start[0])

    def halves(w):
        w = w[0].reshape(chips, 2, unit, 4 * unit)
        keep = lax.dynamic_index_in_dim(w, core, 1, keepdims=False)
        away = lax.dynamic_index_in_dim(w, 1 - core, 1, keepdims=False)
        return keep, across(away)

    rec_keep, rec_send = halves(w_recur)
    in_keep, in_send = halves(w_input)
    w_keep = jnp.concatenate([rec_keep, in_keep], axis=1)
    w_send = jnp.concatenate([rec_send, in_send], axis=1)
    first = jnp.dot(
        inputs.reshape(steps * batch, width),
        w_input[0].reshape(width, 4 * unit),
        preferred_element_type=jnp.float32,
    ).reshape(steps, batch, 4 * unit)
    offset = bias[0].reshape(4 * unit)

    cell = c_start[0]
    hidden = h_start[0]
    kept = []
    blocks = start
    for turn in range(turns):
        leaving = across(product(blocks, w_send))
        staying = product(blocks, w_keep)
        z = staying + leaving + offset
        if turn < steps:
            z = z + jnp.where(layer == 0, first[turn], 0.0)
        i, f, g, o = (z[:, k * unit : (k + 1) * unit] for k in range(4))
        cell_new = jax.nn.sigmoid(f) * cell + jax.nn.sigmoid(i) * jnp.tanh(g)
        hidden_new = (jax.nn.sigmoid(o) * jnp.tanh(cell_new)).astype(jnp.bfloat16)
        valid = jnp.logical_and(turn >= layer, turn < layer + steps)
        cell = jnp.where(valid, cell_new, cell)
        hidden = jnp.where(valid, hidden_new, hidden)
        kept.append(hidden)
        if turn + 1 < turns:
            below = lax.ppermute(hidden, "layer", upward)
            blocks = gathered(jnp.concatenate([hidden, below], axis=1))
    sequence = lax.dynamic_slice_in_dim(jnp.stack(kept), layer, steps, 0)
    return sequence[None], cell[None]


def solution(mesh):
    in_specs = (
        P(),
        P("layer", None, None, "col"),
        P("layer", None, None, "col"),
        P("layer", None, "col"),
        P("layer", None, "col"),
        P("layer", None, "col"),
    )
    out_specs = (P("layer", None, None, "col"), P("layer", None, "col"))
    return jax.shard_map(body, mesh=mesh, in_specs=in_specs, out_specs=out_specs, check_vma=False)
```

time: 365 us -> 240 us (0.66)
  waiting for transfers between devices: 178 us -> 11 us
  blocking collectives: 0 us -> 112 us
  starting transfers between devices: 72.8 us -> 46.3 us
  matrix products: 30.5 us -> 5.54 us
  other arithmetic: 24.4 us -> 6.57 us
  Pallas kernels: 0 us -> 9.81 us
  local copies, waits for them, and re-layouts: 55.7 us -> 46.2 us
    all_to_all x13 -> x1, waiting for transfers between devices: 172 us -> 4.92 us  [gathered(): lax.all_to_all(copies, 'col', 0, 0, tiled=True, axis_index_groups=same_core)]
    all_to_all x0 -> x6, blocking collectives: none -> 112 us  [gathered(): lax.all_to_all(copies, 'col', 0, 0, tiled=True, axis_index_groups=same_core)]
    all_to_all x13 -> x1, starting transfers between devices: 62.6 us -> 7.88 us  [gathered(): lax.all_to_all(copies, 'col', 0, 0, tiled=True, axis_index_groups=same_core)]
    ppermute x6 -> x15, starting transfers between devices: 10.2 us -> 38.5 us  [the longest x6 21.7 us: body(): below = lax.ppermute(hidden, 'layer', upward)]
    dot_general x14 -> x1, matrix products: 30.5 us -> 5.54 us  [body(): jnp.dot(inputs.reshape(steps * batch, width), w_input[0].reshape(width, 4...]
    select_n x20 -> x0, other arithmetic: 22.5 us -> none  [the longest x7 10 us: body(): jnp.where(valid, lax.dynamic_update_slice_in_dim(sequence, shards, start,...]
    broadcast_in_dim x14 -> x8, local copies, waits for them, and re-layouts: 17.5 us -> 2.17 us  [the longest x7 1.5 us: gathered(): copies = jnp.broadcast_to(x, (chips, *x.shape))]
    another operation x0 -> x2, local copies, waits for them, and re-layouts: none -> 14.4 us  [halves(): w = w[0].reshape(chips, 2, unit, 4 * unit)]
  transfers between devices with their start and end apart: 19 -> 16, of which waited for: 19 -> 7; matrix products, arithmetic and copies ran while one was open for 10% -> 10% of each run, Pallas kernels for 0% -> 2%
where the time goes in v1:
time: 240 us; the launch traced here: 239 us
  blocking collectives  112 us (47%)
  starting transfers between devices  46.3 us (19%)
  local copies, waits for them, and re-layouts  46.2 us (19%)
  waiting for transfers between devices  11 us (5%)
  Pallas kernels  9.81 us (4%)
  other arithmetic  6.57 us (3%)
  matrix products  5.54 us (2%)
    all_to_all x6, blocking collectives, gathered(): lax.all_to_all(copies, 'col', 0, 0, tiled=True, axis_index_groups=same_core)  112 us
    ppermute x6, starting transfers between devices, body(): below = lax.ppermute(hidden, 'layer', upward)  21.7 us
    unnamed x41, local copies, waits for them, and re-layouts  19.2 us
    ppermute x9, starting transfers between devices, across(): return lax.ppermute(x, 'col', partners)  16.8 us
    another operation x2, local copies, waits for them, and re-layouts, halves(): w = w[0].reshape(chips, 2, unit, 4 * unit)  14.4 us
    pallas_call x14, Pallas kernels, product(): pl.pallas_call(functools.partial(product_kernel, depth), out_shape=jax.Sh...  9.81 us
    squeeze x2, local copies, waits for them, and re-layouts, halves(): away = lax.dynamic_index_in_dim(w, 1 - core, 1, keepdims=False)  8.66 us
    all_to_all x1, starting transfers between devices, gathered(): lax.all_to_all(copies, 'col', 0, 0, tiled=True, axis_index_groups=same_core)  7.88 us
  transfers between devices with their start and end apart: 16, of which 7 were waited for; matrix products, arithmetic and copies ran while one was open for 10% of the time, Pallas kernels for 2%

profile of v1, /device:TPU:1, one launch (start us, length us, event | category | flops | bytes accessed | tf_op | source)
XLA Modules:
  0.0 239.0 jit_solution(302588631566262047)
XLA Ops:
  0.6 7.2 %reshape_squeeze.9 = bf16[16,2,128,512]{3,2,1,0:T(8,128)(2,1)} reshape(bf16[1,4096,4,128]{3,2,1,0:T(4,128)(2,1)} %param.8) | data formatting | bytes 8388608 | tf_op jit(solution)/shard_map/reshape;squeeze | solution.py:69
  7.9 4.0 %dynamic-slice_bitcast_fusion.1 = (bf16[16,128,512]{2,1,0:T(8,128)(2,1)}, bf16[16,128,512]{2,1,0:T(8,128)(2,1)S(1)}) fusion(bf16[16,2,128,512]{3,2,1,0:T(8,128)(2,1)} %reshape_squeeze.9, s32[]{:T(128)S(6)} %select_n.116, s32[]{:T(128)S(6)} %select_n.115), kind=kLoop, calls=%fused_computation.5 | loop fusion | bytes 8388616 | tf_op jit(solution)/shard_map/jit(dynamic_index_in_dim)/squeeze | solution.py:71
  13.2 7.2 %reshape_squeeze.10 = bf16[16,2,128,512]{3,2,1,0:T(8,128)(2,1)} reshape(bf16[1,4096,4,128]{3,2,1,0:T(4,128)(2,1)} %param.7) | data formatting | bytes 8388608 | tf_op jit(solution)/shard_map/reshape;squeeze | solution.py:69
  20.4 4.7 %dynamic-slice_bitcast_fusion = (bf16[16,128,512]{2,1,0:T(8,128)(2,1)}, bf16[16,128,512]{2,1,0:T(8,128)(2,1)}) fusion(bf16[16,2,128,512]{3,2,1,0:T(8,128)(2,1)} %reshape_squeeze.10, s32[]{:T(128)S(6)} %select_n.116, s32[]{:T(128)S(6)} %select_n.115), kind=kLoop, calls=%fused_computation.4 | loop fusion | bytes 8388616 | tf_op jit(solution)/shard_map/jit(dynamic_index_in_dim)/squeeze | solution.py:71
  26.1 7.9 %all-to-all-start = ((bf16[16,128,128]{2,1,0:T(8,128)(2,1)}), bf16[16,128,128]{2,1,0:T(8,128)(2,1)S(1)}, u32[]{:S(2)}, u32[]{:S(2)}) async-start(bf16[16,128,128]{2,1,0:T(8,128)(2,1)} %broadcast_in_dim.34), calls=%async_computation | async-start | bytes 1048576 | tf_op jit(solution)/shard_map/all_to_all | solution.py:64
  39.6 4.9 %all-to-all-done.g_ref = bf16[16,128,128]{2,1,0:T(8,128)(2,1)S(1)} async-done(((bf16[16,128,128]{2,1,0:T(8,128)(2,1)}), bf16[16,128,128]{2,1,0:T(8,128)(2,1)S(1)}, u32[]{:S(2)}, u32[]{:S(2)}) %all-to-all-start) | async-done | bytes 524320 | tf_op jit(solution)/shard_map/all_to_all | solution.py:64
  44.5 2.2 copy-done.8
  49.4 5.5 %fusion = f32[512,512]{1,0:T(8,128)} fusion(bf16[512,4096]{1,0:T(8,128)(2,1)} %bitcast.59, bf16[512,8,4,128]{3,2,1,0:T(4,128)(2,1)S(1)} %bitcast.50), kind=kOutput, calls=%fused_computation | convolution fusion | flops 2147483648 | bytes 9437184 | tf_op jit(solution)/shard_map/dot_general | solution.py:78
  57.7 2.8 %fusion.6 = f32[128,512]{1,0:T(8,128)S(1)} fusion(f32[512,512]{1,0:T(8,128)} %fusion, f32[128,512]{1,0:T(8,128)S(1)} %shard_map.77, f32[128,512]{1,0:T(8,128)S(1)} %collective-permute-done.2, f32[512]{0:T(512)S(1)} %bitcast.52, pred[]{:T(512)S(6)} %eq.4), kind=kLoop, calls=%fused_computation.15 | loop fusion | flops 262144 | bytes 1050625 | tf_op jit(solution)/shard_map/add | solution.py:94
  60.6 3.1 %collective-permute-start.3 = (bf16[128,128]{1,0:T(8,128)(2,1)S(1)}, bf16[128,128]{1,0:T(8,128)(2,1)S(1)}, u32[]{:S(2)}, u32[]{:S(2)}) collective-permute-start(bf16[128,128]{1,0:T(8,128)(2,1)S(1)} %get-tuple-element.23), channel_id=1, source_target_pairs={{0,32},{32,64},{64,96},{1,33},{33,65},{65,97},{2,34},{34,66},{66,9... | collective-permute-start | bytes 98312 | tf_op jit(solution)/shard_map/ppermute | solution.py:103
  64.8 18.4 %all_to_all.35.g_ref = bf16[16,128,256]{2,1,0:T(8,128)(2,1)S(1)} all-to-all(bf16[16,128,256]{2,1,0:T(8,128)(2,1)S(1)} %broadcast_in_dim.36), channel_id=1, replica_groups={{0,2,4,6,8,10,12,14,16,18,20,22,24,26,28,30},{1,3,5,7,9,11,13,15,17,19,..., dimensions={0} | all-to-all | bytes 2097152 | tf_op jit(solution)/shard_map/all_to_all | solution.py:64
  83.9 3.0 %collective-permute-start.4 = (f32[128,512]{1,0:T(8,128)S(1)}, f32[128,512]{1,0:T(8,128)S(1)}, u32[]{:S(2)}, u32[]{:S(2)}) collective-permute-start(f32[128,512]{1,0:T(8,128)S(1)} %shard_map.80), channel_id=1, source_target_pairs={{0,1},{1,0},{2,3},{3,2},{4,5},{5,4},{6,7},{7,6},{8,9},{9,8},{10,11... | collective-permute-start | bytes 786440 | tf_op jit(solution)/shard_map/ppermute | solution.py:60
  86.9 2.2 copy-done.1
  90.1 3.5 %collective-permute-start.5 = (bf16[128,128]{1,0:T(8,128)(2,1)S(1)}, bf16[128,128]{1,0:T(8,128)(2,1)S(1)}, u32[]{:S(2)}, u32[]{:S(2)}) collective-permute-start(bf16[128,128]{1,0:T(8,128)(2,1)S(1)} %get-tuple-element.19), channel_id=1, source_target_pairs={{0,32},{32,64},{64,96},{1,33},{33,65},{65,97},{2,34},{34,66},{66,9... | collective-permute-start | bytes 98312 | tf_op jit(solution)/shard_map/ppermute | solution.py:103
  94.6 18.8 %all_to_all.36.g_ref = bf16[16,128,256]{2,1,0:T(8,128)(2,1)S(1)} all-to-all(bf16[16,128,256]{2,1,0:T(8,128)(2,1)S(1)} %broadcast_in_dim.37), channel_id=1, replica_groups={{0,2,4,6,8,10,12,14,16,18,20,22,24,26,28,30},{1,3,5,7,9,11,13,15,17,19,..., dimensions={0} | all-to-all | bytes 2097152 | tf_op jit(solution)/shard_map/all_to_all | solution.py:64
  116.2 2.2 copy-done.2
  119.3 3.8 %collective-permute-start.7 = (bf16[128,128]{1,0:T(8,128)(2,1)S(1)}, bf16[128,128]{1,0:T(8,128)(2,1)S(1)}, u32[]{:S(2)}, u32[]{:S(2)}) collective-permute-start(bf16[128,128]{1,0:T(8,128)(2,1)S(1)} %get-tuple-element.16), channel_id=1, source_target_pairs={{0,32},{32,64},{64,96},{1,33},{33,65},{65,97},{2,34},{34,66},{66,9... | collective-permute-start | bytes 98312 | tf_op jit(solution)/shard_map/ppermute | solution.py:103
  124.2 18.8 %all_to_all.37.g_ref = bf16[16,128,256]{2,1,0:T(8,128)(2,1)S(1)} all-to-all(bf16[16,128,256]{2,1,0:T(8,128)(2,1)S(1)} %broadcast_in_dim.38), channel_id=1, replica_groups={{0,2,4,6,8,10,12,14,16,18,20,22,24,26,28,30},{1,3,5,7,9,11,13,15,17,19,..., dimensions={0} | all-to-all | bytes 2097152 | tf_op jit(solution)/shard_map/all_to_all | solution.py:64
  143.7 2.0 collective-permute-start.8
  145.7 2.2 copy-done.3
  148.8 3.8 %collective-permute-start.9 = (bf16[128,128]{1,0:T(8,128)(2,1)S(1)}, bf16[128,128]{1,0:T(8,128)(2,1)S(1)}, u32[]{:S(2)}, u32[]{:S(2)}) collective-permute-start(bf16[128,128]{1,0:T(8,128)(2,1)S(1)} %get-tuple-element.12), channel_id=1, source_target_pairs={{0,32},{32,64},{64,96},{1,33},{33,65},{65,97},{2,34},{34,66},{66,9... | collective-permute-start | bytes 98312 | tf_op jit(solution)/shard_map/ppermute | solution.py:103
  153.7 18.8 %all_to_all.38.g_ref = bf16[16,128,256]{2,1,0:T(8,128)(2,1)S(1)} all-to-all(bf16[16,128,256]{2,1,0:T(8,128)(2,1)S(1)} %broadcast_in_dim.39), channel_id=1, replica_groups={{0,2,4,6,8,10,12,14,16,18,20,22,24,26,28,30},{1,3,5,7,9,11,13,15,17,19,..., dimensions={0} | all-to-all | bytes 2097152 | tf_op jit(solution)/shard_map/all_to_all | solution.py:64
  173.3 2.2 collective-permute-start.10
  175.5 2.2 copy-done.4
  178.6 3.8 %collective-permute-start.11 = (bf16[128,128]{1,0:T(8,128)(2,1)S(1)}, bf16[128,128]{1,0:T(8,128)(2,1)S(1)}, u32[]{:S(2)}, u32[]{:S(2)}) collective-permute-start(bf16[128,128]{1,0:T(8,128)(2,1)S(1)} %get-tuple-element.9), channel_id=1, source_target_pairs={{0,32},{32,64},{64,96},{1,33},{33,65},{65,97},{2,34},{34,66},{66,9... | collective-permute-start | bytes 98312 | tf_op jit(solution)/shard_map/ppermute | solution.py:103
  183.5 18.8 %all_to_all.39.g_ref = bf16[16,128,256]{2,1,0:T(8,128)(2,1)S(1)} all-to-all(bf16[16,128,256]{2,1,0:T(8,128)(2,1)S(1)} %broadcast_in_dim.40), channel_id=1, replica_groups={{0,2,4,6,8,10,12,14,16,18,20,22,24,26,28,30},{1,3,5,7,9,11,13,15,17,19,..., dimensions={0} | all-to-all | bytes 2097152 | tf_op jit(solution)/shard_map/all_to_all | solution.py:64
  203.0 2.1 collective-permute-start.12
  205.0 2.2 copy-done.5
  208.1 3.8 %collective-permute-start.13 = (bf16[128,128]{1,0:T(8,128)(2,1)S(1)}, bf16[128,128]{1,0:T(8,128)(2,1)S(1)}, u32[]{:S(2)}, u32[]{:S(2)}) collective-permute-start(bf16[128,128]{1,0:T(8,128)(2,1)S(1)} %get-tuple-element.5), channel_id=1, source_target_pairs={{0,32},{32,64},{64,96},{1,33},{33,65},{65,97},{2,34},{34,66},{66,9... | collective-permute-start | bytes 98312 | tf_op jit(solution)/shard_map/ppermute | solution.py:103
  213.0 18.8 %all_to_all.40.g_ref = bf16[16,128,256]{2,1,0:T(8,128)(2,1)S(1)} all-to-all(bf16[16,128,256]{2,1,0:T(8,128)(2,1)S(1)} %broadcast_in_dim.41), channel_id=1, replica_groups={{0,2,4,6,8,10,12,14,16,18,20,22,24,26,28,30},{1,3,5,7,9,11,13,15,17,19,..., dimensions={0} | all-to-all | bytes 2097152 | tf_op jit(solution)/shard_map/all_to_all | solution.py:64
  232.5 2.0 collective-permute-start.14
  234.6 2.2 copy-done.6
  (97 shorter events, 32.9 us)
Async XLA Ops:
  11.8 22.1 %collective-permute-start = (bf16[16,128,512]{2,1,0:T(8,128)(2,1)}, bf16[16,128,512]{2,1,0:T(8,128)(2,1)}, u32[]{:S(2)}, u32[]{:S(2)}) collective-permute-start(bf16[16,128,512]{2,1,0:T(8,128)(2,1)} %get-tuple-element.27), channel_id=1, source_target_pairs={{0,1},{1,0},{2,3},{3,2},{4,5},{5,4},{6,7},{7,6},{8,9},{9,8},{10,11... | collective-permute-start | bytes 6291464 | tf_op jit(solution)/shard_map/ppermute | solution.py:60
  20.4 4.7 %copy-start.18 = (bf16[1,128,128]{2,1,0:T(8,128)(2,1)S(1)}, bf16[1,128,128]{2,1,0:T(8,128)(2,1)}, u32[]{:S(2)}) copy-start(bf16[1,128,128]{2,1,0:T(8,128)(2,1)} %param.10) | copy-start | bytes 98308
  25.1 10.6 %collective-permute-start.1 = (bf16[16,128,512]{2,1,0:T(8,128)(2,1)}, bf16[16,128,512]{2,1,0:T(8,128)(2,1)}, u32[]{:S(2)}, u32[]{:S(2)}) collective-permute-start(bf16[16,128,512]{2,1,0:T(8,128)(2,1)} %get-tuple-element.25), channel_id=1, source_target_pairs={{0,1},{1,0},{2,3},{3,2},{4,5},{5,4},{6,7},{7,6},{8,9},{9,8},{10,11... | collective-permute-start | bytes 6291464 | tf_op jit(solution)/shard_map/ppermute | solution.py:60
  26.1 18.5 %all-to-all-start = ((bf16[16,128,128]{2,1,0:T(8,128)(2,1)}), bf16[16,128,128]{2,1,0:T(8,128)(2,1)S(1)}, u32[]{:S(2)}, u32[]{:S(2)}) async-start(bf16[16,128,128]{2,1,0:T(8,128)(2,1)} %broadcast_in_dim.34), calls=%async_computation | async-start | bytes 1048576 | tf_op jit(solution)/shard_map/all_to_all | solution.py:64
  44.5 2.2 copy-start.8
  46.7 2.7 %copy-start.15 = (bf16[1,4096,4,128]{3,2,1,0:T(4,128)(2,1)S(1)}, bf16[1,4096,4,128]{3,2,1,0:T(4,128)(2,1)}, u32[]{:S(2)}) copy-start(bf16[1,4096,4,128]{3,2,1,0:T(4,128)(2,1)} %param.7) | copy-start | bytes 12582916
  47.4 10.2 %collective-permute-start.2 = (f32[128,512]{1,0:T(8,128)S(1)}, f32[128,512]{1,0:T(8,128)S(1)}, u32[]{:S(2)}, u32[]{:S(2)}) collective-permute-start(f32[128,512]{1,0:T(8,128)S(1)} %shard_map.78), channel_id=1, source_target_pairs={{0,1},{1,0},{2,3},{3,2},{4,5},{5,4},{6,7},{7,6},{8,9},{9,8},{10,11... | collective-permute-start | bytes 786440 | tf_op jit(solution)/shard_map/ppermute | solution.py:60
  56.9 26.3 %copy-start = (bf16[16,256,512]{2,1,0:T(8,128)(2,1)}, bf16[16,256,512]{2,1,0:T(8,128)(2,1)S(1)}, u32[]{:S(2)}) copy-start(bf16[16,256,512]{2,1,0:T(8,128)(2,1)S(1)} %pad_maximum_fusion.w_ref) | copy-start | bytes 12582916
  57.0 3.5 %copy-start.17 = (f32[1,128,128]{2,1,0:T(8,128)S(1)}, f32[1,128,128]{2,1,0:T(8,128)}, u32[]{:S(2)}) copy-start(f32[1,128,128]{2,1,0:T(8,128)} %param.11) | copy-start | bytes 196612
  57.0 26.2 %copy-start.9 = (bf16[16,256,512]{2,1,0:T(8,128)(2,1)S(1)}, bf16[16,256,512]{2,1,0:T(8,128)(2,1)}, u32[]{:S(2)}) copy-start(bf16[16,256,512]{2,1,0:T(8,128)(2,1)} %copy-done.7) | copy-start | bytes 12582916
  60.6 4.1 %collective-permute-start.3 = (bf16[128,128]{1,0:T(8,128)(2,1)S(1)}, bf16[128,128]{1,0:T(8,128)(2,1)S(1)}, u32[]{:S(2)}, u32[]{:S(2)}) collective-permute-start(bf16[128,128]{1,0:T(8,128)(2,1)S(1)} %get-tuple-element.23), channel_id=1, source_target_pairs={{0,32},{32,64},{64,96},{1,33},{33,65},{65,97},{2,34},{34,66},{66,9... | collective-permute-start | bytes 98312 | tf_op jit(solution)/shard_map/ppermute | solution.py:103
  83.2 6.6 %copy-start.16 = (f32[512,512]{1,0:T(8,128)S(1)}, f32[512,512]{1,0:T(8,128)}, u32[]{:S(2)}) copy-start(f32[512,512]{1,0:T(8,128)} %fusion) | copy-start | bytes 3145732
  83.9 5.9 %collective-permute-start.4 = (f32[128,512]{1,0:T(8,128)S(1)}, f32[128,512]{1,0:T(8,128)S(1)}, u32[]{:S(2)}, u32[]{:S(2)}) collective-permute-start(f32[128,512]{1,0:T(8,128)S(1)} %shard_map.80), channel_id=1, source_target_pairs={{0,1},{1,0},{2,3},{3,2},{4,5},{5,4},{6,7},{7,6},{8,9},{9,8},{10,11... | collective-permute-start | bytes 786440 | tf_op jit(solution)/shard_map/ppermute | solution.py:60
  86.9 2.2 copy-start.1
  89.1 24.3 %copy-start.10 = (bf16[16,256,512]{2,1,0:T(8,128)(2,1)S(1)}, bf16[16,256,512]{2,1,0:T(8,128)(2,1)}, u32[]{:S(2)}) copy-start(bf16[16,256,512]{2,1,0:T(8,128)(2,1)} %copy-done.7) | copy-start | bytes 12582916
  90.1 4.5 %collective-permute-start.5 = (bf16[128,128]{1,0:T(8,128)(2,1)S(1)}, bf16[128,128]{1,0:T(8,128)(2,1)S(1)}, u32[]{:S(2)}, u32[]{:S(2)}) collective-permute-start(bf16[128,128]{1,0:T(8,128)(2,1)S(1)} %get-tuple-element.19), channel_id=1, source_target_pairs={{0,32},{32,64},{64,96},{1,33},{33,65},{65,97},{2,34},{34,66},{66,9... | collective-permute-start | bytes 98312 | tf_op jit(solution)/shard_map/ppermute | solution.py:103
  114.1 4.9 %collective-permute-start.6 = (f32[128,512]{1,0:T(8,128)S(1)}, f32[128,512]{1,0:T(8,128)S(1)}, u32[]{:S(2)}, u32[]{:S(2)}) collective-permute-start(f32[128,512]{1,0:T(8,128)S(1)} %shard_map.82), channel_id=1, source_target_pairs={{0,1},{1,0},{2,3},{3,2},{4,5},{5,4},{6,7},{7,6},{8,9},{9,8},{10,11... | collective-permute-start | bytes 786440 | tf_op jit(solution)/shard_map/ppermute | solution.py:60
  116.2 2.2 copy-start.2
  118.3 24.6 %copy-start.11 = (bf16[16,256,512]{2,1,0:T(8,128)(2,1)S(1)}, bf16[16,256,512]{2,1,0:T(8,128)(2,1)}, u32[]{:S(2)}) copy-start(bf16[16,256,512]{2,1,0:T(8,128)(2,1)} %copy-done.7) | copy-start | bytes 12582916
  119.3 4.8 %collective-permute-start.7 = (bf16[128,128]{1,0:T(8,128)(2,1)S(1)}, bf16[128,128]{1,0:T(8,128)(2,1)S(1)}, u32[]{:S(2)}, u32[]{:S(2)}) collective-permute-start(bf16[128,128]{1,0:T(8,128)(2,1)S(1)} %get-tuple-element.16), channel_id=1, source_target_pairs={{0,32},{32,64},{64,96},{1,33},{33,65},{65,97},{2,34},{34,66},{66,9... | collective-permute-start | bytes 98312 | tf_op jit(solution)/shard_map/ppermute | solution.py:103
  143.7 5.0 %collective-permute-start.8 = (f32[128,512]{1,0:T(8,128)S(1)}, f32[128,512]{1,0:T(8,128)S(1)}, u32[]{:S(2)}, u32[]{:S(2)}) collective-permute-start(f32[128,512]{1,0:T(8,128)S(1)} %shard_map.84), channel_id=1, source_target_pairs={{0,1},{1,0},{2,3},{3,2},{4,5},{5,4},{6,7},{7,6},{8,9},{9,8},{10,11... | collective-permute-start | bytes 786440 | tf_op jit(solution)/shard_map/ppermute | solution.py:60
  145.7 2.2 copy-start.3
  147.9 24.6 %copy-start.12 = (bf16[16,256,512]{2,1,0:T(8,128)(2,1)S(1)}, bf16[16,256,512]{2,1,0:T(8,128)(2,1)}, u32[]{:S(2)}) copy-start(bf16[16,256,512]{2,1,0:T(8,128)(2,1)} %copy-done.7) | copy-start | bytes 12582916
  148.8 4.8 %collective-permute-start.9 = (bf16[128,128]{1,0:T(8,128)(2,1)S(1)}, bf16[128,128]{1,0:T(8,128)(2,1)S(1)}, u32[]{:S(2)}, u32[]{:S(2)}) collective-permute-start(bf16[128,128]{1,0:T(8,128)(2,1)S(1)} %get-tuple-element.12), channel_id=1, source_target_pairs={{0,32},{32,64},{64,96},{1,33},{33,65},{65,97},{2,34},{34,66},{66,9... | collective-permute-start | bytes 98312 | tf_op jit(solution)/shard_map/ppermute | solution.py:103
  173.3 5.1 %collective-permute-start.10 = (f32[128,512]{1,0:T(8,128)S(1)}, f32[128,512]{1,0:T(8,128)S(1)}, u32[]{:S(2)}, u32[]{:S(2)}) collective-permute-start(f32[128,512]{1,0:T(8,128)S(1)} %shard_map.86), channel_id=1, source_target_pairs={{0,1},{1,0},{2,3},{3,2},{4,5},{5,4},{6,7},{7,6},{8,9},{9,8},{10,11... | collective-permute-start | bytes 786440 | tf_op jit(solution)/shard_map/ppermute | solution.py:60
  175.5 2.2 copy-start.4
  177.7 24.6 %copy-start.13 = (bf16[16,256,512]{2,1,0:T(8,128)(2,1)S(1)}, bf16[16,256,512]{2,1,0:T(8,128)(2,1)}, u32[]{:S(2)}) copy-start(bf16[16,256,512]{2,1,0:T(8,128)(2,1)} %copy-done.7) | copy-start | bytes 12582916
  178.6 4.8 %collective-permute-start.11 = (bf16[128,128]{1,0:T(8,128)(2,1)S(1)}, bf16[128,128]{1,0:T(8,128)(2,1)S(1)}, u32[]{:S(2)}, u32[]{:S(2)}) collective-permute-start(bf16[128,128]{1,0:T(8,128)(2,1)S(1)} %get-tuple-element.9), channel_id=1, source_target_pairs={{0,32},{32,64},{64,96},{1,33},{33,65},{65,97},{2,34},{34,66},{66,9... | collective-permute-start | bytes 98312 | tf_op jit(solution)/shard_map/ppermute | solution.py:103
  203.0 5.0 %collective-permute-start.12 = (f32[128,512]{1,0:T(8,128)S(1)}, f32[128,512]{1,0:T(8,128)S(1)}, u32[]{:S(2)}, u32[]{:S(2)}) collective-permute-start(f32[128,512]{1,0:T(8,128)S(1)} %shard_map.88), channel_id=1, source_target_pairs={{0,1},{1,0},{2,3},{3,2},{4,5},{5,4},{6,7},{7,6},{8,9},{9,8},{10,11... | collective-permute-start | bytes 786440 | tf_op jit(solution)/shard_map/ppermute | solution.py:60
  207.2 24.6 %copy-start.14 = (bf16[16,256,512]{2,1,0:T(8,128)(2,1)S(1)}, bf16[16,256,512]{2,1,0:T(8,128)(2,1)}, u32[]{:S(2)}) copy-start(bf16[16,256,512]{2,1,0:T(8,128)(2,1)} %copy-done.7) | copy-start | bytes 12582916
  208.1 4.8 %collective-permute-start.13 = (bf16[128,128]{1,0:T(8,128)(2,1)S(1)}, bf16[128,128]{1,0:T(8,128)(2,1)S(1)}, u32[]{:S(2)}, u32[]{:S(2)}) collective-permute-start(bf16[128,128]{1,0:T(8,128)(2,1)S(1)} %get-tuple-element.5), channel_id=1, source_target_pairs={{0,32},{32,64},{64,96},{1,33},{33,65},{65,97},{2,34},{34,66},{66,9... | collective-permute-start | bytes 98312 | tf_op jit(solution)/shard_map/ppermute | solution.py:103
  232.5 4.9 %collective-permute-start.14 = (f32[128,512]{1,0:T(8,128)S(1)}, f32[128,512]{1,0:T(8,128)S(1)}, u32[]{:S(2)}, u32[]{:S(2)}) collective-permute-start(f32[128,512]{1,0:T(8,128)S(1)} %shard_map.90), channel_id=1, source_target_pairs={{0,1},{1,0},{2,3},{3,2},{4,5},{5,4},{6,7},{7,6},{8,9},{9,8},{10,11... | collective-permute-start | bytes 786440 | tf_op jit(solution)/shard_map/ppermute | solution.py:60
  (4 other events, 7.2 us)

commit v2 on v1

v2 whole, which is shorter than its diff:
```python
import functools

import jax
import jax.numpy as jnp
from jax import lax
from jax.experimental import pallas as pl
from jax.experimental.pallas import tpu as pltpu
from jax.sharding import PartitionSpec as P

VMEM = pl.BlockSpec(memory_space=pltpu.VMEM)
SMEM = pl.BlockSpec(memory_space=pltpu.SMEM)
ANY = pl.BlockSpec(memory_space=pl.ANY)


def resident(x):
    return pltpu.with_memory_space_constraint(x, pltpu.VMEM)


def limits(mib):
    return pltpu.CompilerParams(vmem_limit_bytes=mib << 20)


def sort_kernel(other, info_ref, w_ref, out_ref):
    blocks, depth, wide = out_ref.shape
    unit = w_ref.shape[1]
    gates = wide // unit
    half = depth // 2
    rows = half * gates
    side = 1 - info_ref[1] if other else info_ref[1]
    to = lax.broadcasted_iota(jnp.int32, (rows, rows), 0)
    come = lax.broadcasted_iota(jnp.int32, (rows, rows), 1)
    order = come == gates * (to % half) + to // half
    order = order.astype(jnp.float32).astype(jnp.bfloat16)
    unroll = 8

    def some(i, carry):
        for u in range(unroll):
            j = i * unroll + u
            at = pl.multiple_of((2 * j + side) * 2 * rows, 2 * rows)
            both = jnp.concatenate(
                [w_ref[pl.ds(at, rows), :], w_ref[pl.ds(at + rows, rows), :]], axis=1
            )
            sorted_rows = jnp.dot(order, both, preferred_element_type=jnp.float32)
            sorted_rows = sorted_rows.astype(jnp.bfloat16)
            for h in range(2):
                for g in range(gates):
                    out_ref[j, h * half : (h + 1) * half, g * unit : (g + 1) * unit] = sorted_rows[
                        g * half : (g + 1) * half, h * unit : (h + 1) * unit
                    ]
        return carry

    lax.fori_loop(0, blocks // unroll, some, 0)


def sorted_side(info, w, blocks, other):
    depth, gates, unit = w.shape[0] // (2 * blocks), w.shape[1], w.shape[2]
    return pl.pallas_call(
        functools.partial(sort_kernel, other),
        out_shape=jax.ShapeDtypeStruct((blocks, depth, gates * unit), w.dtype),
        in_specs=[SMEM, VMEM],
        out_specs=VMEM,
        cost_estimate=pl.CostEstimate(
            flops=2_000_000_000, bytes_accessed=4 * blocks * depth * gates * unit, transcendentals=0
        ),
        compiler_params=limits(4),
    )(info, resident(w.reshape(-1, unit)))


def pick_kernel(info_ref, x_ref, out_ref, sems):
    blocks, unit = out_ref.shape[1], out_ref.shape[3]
    copies = []
    for j in range(blocks):
        at = pl.multiple_of((2 * j + info_ref[1]) * unit, unit)
        copies.append(
            pltpu.make_async_copy(x_ref.at[:, :, pl.ds(at, unit)], out_ref.at[:, j], sems.at[j])
        )
    for copy in copies:
        copy.start()
    for copy in copies:
        copy.wait()


def picked(info, x, blocks, unit):
    steps, batch, _ = x.shape
    return pl.pallas_call(
        pick_kernel,
        out_shape=jax.ShapeDtypeStruct((steps, blocks, batch, unit), x.dtype),
        in_specs=[SMEM, ANY],
        out_specs=VMEM,
        scratch_shapes=[pltpu.SemaphoreType.DMA((blocks,))],
        cost_estimate=pl.CostEstimate(
            flops=1_000_000_000, bytes_accessed=4 * x.size // 2, transcendentals=0
        ),
        compiler_params=limits(1),
    )(info, x)


def product_kernel(turn, stage, fed, info_ref, *refs):
    refs = list(refs)
    out_ref, w_in_ref, w_rec_ref = refs.pop(), refs.pop(), refs.pop()
    x_ref = refs.pop() if fed else None
    blocks, unit, width = w_rec_ref.shape
    bottom = info_ref[0] == 0

    def own(j):
        if stage == 0:
            return refs[0][j]
        if stage == 1:
            return jnp.where(bottom, refs[1][j], refs[0][j])
        return refs[0][j, :, :unit]

    def below(j):
        if stage == 0:
            came = jnp.zeros_like(x_ref[turn, j])
        elif stage == 1:
            came = refs[1][j]
        else:
            came = refs[0][j, :, unit:]
        return jnp.where(bottom, x_ref[turn, j], came) if fed else came

    wide = 256
    for n in range(width // wide):
        cols = slice(n * wide, (n + 1) * wide)
        total = None
        for block, w_ref in ((own, w_rec_ref), (below, w_in_ref)):
            for j in range(0, blocks, 2):
                left = jnp.concatenate([block(j), block(j + 1)], axis=1)
                right = w_ref[j : j + 2, :, cols].reshape(2 * unit, wide)
                term = jnp.dot(left, right, preferred_element_type=jnp.float32)
                total = term if total is None else total + term
        out_ref[:, cols] = total


def product(info, gathered, x, w_rec, w_in, turn, stage):
    blocks, unit, width = w_rec.shape
    batch = gathered[0].shape[1]
    args = [*gathered, *([] if x is None else [x]), w_rec, w_in]
    return pl.pallas_call(
        functools.partial(product_kernel, turn, stage, x is not None),
        out_shape=jax.ShapeDtypeStruct((batch, width), jnp.float32),
        in_specs=[SMEM, *[VMEM] * len(args)],
        out_specs=VMEM,
        cost_estimate=pl.CostEstimate(
            flops=4 * blocks * unit * batch * width,
            bytes_accessed=4 * blocks * unit * (batch + width) + 4 * batch * width,
            transcendentals=0,
        ),
        compiler_params=limits(4),
    )(info, *[resident(arg) for arg in args])


def gates_kernel(turn, steps, info_ref, here_ref, came_ref, bias_ref, cell_ref, hid_ref, cell_out, hid_out):
    unit = cell_ref.shape[1]
    layer = info_ref[0]
    valid = jnp.logical_and(turn >= layer, turn < layer + steps)

    def gate(k):
        cols = slice(k * unit, (k + 1) * unit)
        return here_ref[:, cols] + came_ref[:, cols] + bias_ref[k : k + 1, :]

    cell = cell_ref[...]
    cell_new = jax.nn.sigmoid(gate(1)) * cell + jax.nn.sigmoid(gate(0)) * jnp.tanh(gate(2))
    hidden_new = (jax.nn.sigmoid(gate(3)) * jnp.tanh(cell_new)).astype(hid_ref.dtype)
    cell_out[...] = jnp.where(valid, cell_new, cell)
    hid_out[...] = jnp.where(valid, hidden_new, hid_ref[...])


def gates(info, here, came, bias, cell, hidden, turn, steps):
    return pl.pallas_call(
        functools.partial(gates_kernel, turn, steps),
        out_shape=(
            jax.ShapeDtypeStruct(cell.shape, cell.dtype),
            jax.ShapeDtypeStruct(hidden.shape, hidden.dtype),
        ),
        in_specs=[SMEM, *[VMEM] * 5],
        out_specs=(VMEM, VMEM),
        cost_estimate=pl.CostEstimate(
            flops=20 * cell.size, bytes_accessed=40 * cell.size, transcendentals=5 * cell.size
        ),
        compiler_params=limits(2),
    )(info, *[resident(arg) for arg in (here, came, bias, cell, hidden)])


def spread_kernel(stage, info_ref, *refs):
    out_ref = refs[-1]
    unit = refs[0].shape[1]
    for j in range(out_ref.shape[0]):
        if stage == 0:
            out_ref[j] = refs[0][...]
        elif stage == 1:
            out_ref[j] = jnp.where(info_ref[0] == 0, refs[0][...], refs[1][...])
        else:
            out_ref[j, :, :unit] = refs[0][...]
            out_ref[j, :, unit:] = refs[1][...]


def spread(info, parts, stage, copies):
    batch, unit = parts[0].shape
    width = unit * (2 if stage == 2 else 1)
    return pl.pallas_call(
        functools.partial(spread_kernel, stage),
        out_shape=jax.ShapeDtypeStruct((copies, batch, width), parts[0].dtype),
        in_specs=[SMEM, *[VMEM] * len(parts)],
        out_specs=VMEM,
        cost_estimate=pl.CostEstimate(
            flops=batch * width, bytes_accessed=2 * copies * batch * width, transcendentals=0
        ),
        compiler_params=limits(2),
    )(info, *[resident(part) for part in parts])


def select_kernel(layers, info_ref, *refs):
    out_ref = refs[-1]
    for t in range(out_ref.shape[0]):
        value = refs[t][...]
        for l in range(1, layers):
            value = jnp.where(info_ref[0] == l, refs[t + l][...], value)
        out_ref[t] = value


def selected(info, kept, steps, layers):
    return pl.pallas_call(
        functools.partial(select_kernel, layers),
        out_shape=jax.ShapeDtypeStruct((steps, *kept[0].shape), kept[0].dtype),
        in_specs=[SMEM, *[VMEM] * len(kept)],
        out_specs=VMEM,
        compiler_params=limits(2),
    )(info, *[resident(value) for value in kept])


def body(inputs, w_input, w_recur, bias, h_start, c_start):
    steps, _, _ = inputs.shape
    unit = w_input.shape[3]
    layers = lax.axis_size("layer")
    devices = lax.axis_size("col")
    chips = devices // 2
    turns = steps + layers - 1
    layer = lax.axis_index("layer")
    core = lax.axis_index("col") & 1
    same_core = [[2 * chip + side for chip in range(chips)] for side in range(2)]
    partners = [(i, i ^ 1) for i in range(devices)]
    upward = [(i, i + 1) for i in range(layers - 1)]
    info = jnp.stack([layer, core])

    def across(x):
        return lax.ppermute(x, "col", partners)

    def gathered(parts, stage):
        copies = spread(info, parts, stage, chips)
        return lax.all_to_all(copies, "col", 0, 0, tiled=True, axis_index_groups=same_core)

    cell = c_start[0]
    hidden = h_start[0]
    start = gathered((hidden,), 0)
    rec_send = across(sorted_side(info, w_recur[0], chips, True))
    in_send = across(sorted_side(info, w_input[0], chips, True))
    rec_keep = sorted_side(info, w_recur[0], chips, False)
    in_keep = sorted_side(info, w_input[0], chips, False)
    x = picked(info, inputs, chips, unit)

    kept = []
    blocks = (start,)
    for turn in range(turns):
        stage = min(turn, 2)
        fed = x if turn < steps else None
        came = across(product(info, blocks, fed, rec_send, in_send, turn, stage))
        here = product(info, blocks, fed, rec_keep, in_keep, turn, stage)
        cell, hidden = gates(info, here, came, bias[0], cell, hidden, turn, steps)
        kept.append(hidden)
        if turn + 1 < turns:
            below = lax.ppermute(hidden, "layer", upward)
            blocks = (gathered((hidden, below), min(turn + 1, 2)),)
            if turn == 0:
                blocks = (start, *blocks)
    return selected(info, kept, steps, layers)[None], cell[None]


def solution(mesh):
    in_specs = (
        P(),
        P("layer", None, None, "col"),
        P("layer", None, None, "col"),
        P("layer", None, "col"),
        P("layer", None, "col"),
        P("layer", None, "col"),
    )
    out_specs = (P("layer", None, None, "col"), P("layer", None, "col"))
    return jax.shard_map(body, mesh=mesh, in_specs=in_specs, out_specs=out_specs, check_vma=False)
```

time: 240 us -> 223 us (0.929)
  local copies, waits for them, and re-layouts: 46.2 us -> 4.4 us
  Pallas kernels: 9.81 us -> 51.1 us
  other arithmetic: 6.57 us -> 0.08 us
  blocking collectives: 112 us -> 106 us
  matrix products: 5.54 us -> 0 us
    pallas_call x14 -> x34, Pallas kernels: 9.81 us -> 51.1 us  [the longest x14 29.6 us: product(): pl.pallas_call(functools.partial(product_kernel, turn, stage, x is not No...]
    unnamed x41 -> x16, local copies, waits for them, and re-layouts: 19.2 us -> 4.4 us
    another operation x2 -> x0, local copies, waits for them, and re-layouts: 14.4 us -> none  [halves(): w = w[0].reshape(chips, 2, unit, 4 * unit)]
    squeeze x2 -> x0, local copies, waits for them, and re-layouts: 8.66 us -> none  [halves(): away = lax.dynamic_index_in_dim(w, 1 - core, 1, keepdims=False)]
    all_to_all x6, blocking collectives: 112 us -> 106 us  [gathered(): lax.all_to_all(copies, 'col', 0, 0, tiled=True, axis_index_groups=same_core)]
    dot_general x1 -> x0, matrix products: 5.54 us -> none  [body(): jnp.dot(inputs.reshape(steps * batch, width), w_input[0].reshape(width, 4...]
    add x7 -> x0, other arithmetic: 3.14 us -> none  [the longest x4 3.02 us: body(): z = z + jnp.where(layer == 0, first[turn], 0.0)]
  transfers between devices with their start and end apart: 16 -> 16, of which waited for: 7 -> 7; matrix products, arithmetic and copies ran while one was open for 10% -> 0% of each run, Pallas kernels for 2% -> 8%
where the time goes in v2:
time: 223 us; the launch traced here: 222 us
  blocking collectives  106 us (48%)
  Pallas kernels  51.1 us (23%)
  starting transfers between devices  46.8 us (21%)
  waiting for transfers between devices  13.2 us (6%)
  local copies, waits for them, and re-layouts  4.4 us (2%)
    all_to_all x6, blocking collectives, gathered(): lax.all_to_all(copies, 'col', 0, 0, tiled=True, axis_index_groups=same_core)  106 us
    pallas_call x14, Pallas kernels, product(): pl.pallas_call(functools.partial(product_kernel, turn, stage, x is not No...  29.6 us
    ppermute x6, starting transfers between devices, body(): below = lax.ppermute(hidden, 'layer', upward)  21.5 us
    ppermute x9, starting transfers between devices, across(): return lax.ppermute(x, 'col', partners)  17.4 us
    pallas_call x4, Pallas kernels, sorted_side(): pl.pallas_call(functools.partial(sort_kernel, other), out_shape=jax.Shape...  8.65 us
    all_to_all x1, starting transfers between devices, gathered(): lax.all_to_all(copies, 'col', 0, 0, tiled=True, axis_index_groups=same_core)  7.88 us
    all_to_all x1, waiting for transfers between devices, gathered(): lax.all_to_all(copies, 'col', 0, 0, tiled=True, axis_index_groups=same_core)  7.1 us
    ppermute x6, waiting for transfers between devices, body(): below = lax.ppermute(hidden, 'layer', upward)  6.03 us
  transfers between devices with their start and end apart: 16, of which 7 were waited for; matrix products, arithmetic and copies ran while one was open for 0% of the time, Pallas kernels for 8%

profile of v2, /device:TPU:1, one launch (start us, length us, event | category | flops | bytes accessed | tf_op | source)
XLA Modules:
  0.0 222.1 jit_solution(5806411308229126096)
XLA Ops:
  0.7 2.2 copy-done.4
  2.9 2.8 %shard_map.82 = bf16[16,128,512]{2,1,0:T(8,128)(2,1)} custom-call(s32[2]{0:T(128)S(1)} %pad_add_fusion.info_ref, bf16[16384,128]{1,0:T(8,128)(2,1)S(1)} %bitcast.19), custom_call_target="tpu_custom_call" | custom-call | flops 2000000000 | bytes 4194304 | tf_op jit(solution)/shard_map/pallas_call | solution.py:57
  7.1 2.9 %shard_map.83 = bf16[16,128,512]{2,1,0:T(8,128)(2,1)} custom-call(s32[2]{0:T(128)S(1)} %pad_add_fusion.info_ref, bf16[16384,128]{1,0:T(8,128)(2,1)S(1)} %bitcast.21), custom_call_target="tpu_custom_call" | custom-call | flops 2000000000 | bytes 4194304 | tf_op jit(solution)/shard_map/pallas_call | solution.py:57
  11.5 7.9 %all-to-all-start = ((bf16[16,128,128]{2,1,0:T(8,128)(2,1)}), bf16[16,128,128]{2,1,0:T(8,128)(2,1)S(1)}, u32[]{:S(2)}, u32[]{:S(2)}) async-start(bf16[16,128,128]{2,1,0:T(8,128)(2,1)} %shard_map.77), calls=%async_computation | async-start | bytes 1048576 | tf_op jit(solution)/shard_map/all_to_all | solution.py:250
  19.4 2.2 copy-done
  22.8 7.1 %all-to-all-done.refs_0_ = bf16[16,128,128]{2,1,0:T(8,128)(2,1)S(1)} async-done(((bf16[16,128,128]{2,1,0:T(8,128)(2,1)}), bf16[16,128,128]{2,1,0:T(8,128)(2,1)S(1)}, u32[]{:S(2)}, u32[]{:S(2)}) %all-to-all-start) | async-done | bytes 524320 | tf_op jit(solution)/shard_map/all_to_all | solution.py:250
  30.0 3.1 %shard_map.84 = f32[128,512]{1,0:T(8,128)S(1)} custom-call(s32[2]{0:T(128)S(1)} %pad_add_fusion.info_ref, bf16[16,128,128]{2,1,0:T(8,128)(2,1)S(1)} %all-to-all-done.refs_0_, bf16[4,16,128,128]{3,2,1,0:T(8,128)(2,1)S(1)} %shard_map.78.refs_1_.refs_2_, bf16[16,128,512]{2,1,0:T(8,128)(2,1)} %collective-permute-done.refs_2_.refs_3_.refs_1_, ...), custom_call_target="tpu_custom_call" | custom-call | flops 536870912 | bytes 5505024 | tf_op jit(solution)/shard_map/pallas_call | solution.py:138
  33.1 2.0 collective-permute-start.2
  40.0 3.1 %collective-permute-start.3 = (bf16[128,128]{1,0:T(8,128)(2,1)S(1)}, bf16[128,128]{1,0:T(8,128)(2,1)S(1)}, u32[]{:S(2)}, u32[]{:S(2)}) collective-permute-start(bf16[128,128]{1,0:T(8,128)(2,1)S(1)} %get-tuple-element.16.refs_0_.hid_ref), channel_id=1, source_target_pairs={{0,32},{32,64},{64,96},{1,33},{33,65},{65,97},{2,34},{34,66},{66,9... | collective-permute-start | bytes 98312 | tf_op jit(solution)/shard_map/ppermute | solution.py:271
  44.7 12.8 %all_to_all.35.refs_1_ = bf16[16,128,128]{2,1,0:T(8,128)(2,1)S(1)} all-to-all(bf16[16,128,128]{2,1,0:T(8,128)(2,1)S(1)} %shard_map.86), channel_id=1, replica_groups={{0,2,4,6,8,10,12,14,16,18,20,22,24,26,28,30},{1,3,5,7,9,11,13,15,17,19,..., dimensions={0} | all-to-all | bytes 1048576 | tf_op jit(solution)/shard_map/all_to_all | solution.py:250
  57.4 3.0 %shard_map.88 = f32[128,512]{1,0:T(8,128)S(1)} custom-call(s32[2]{0:T(128)S(1)} %pad_add_fusion.info_ref, bf16[16,128,128]{2,1,0:T(8,128)(2,1)S(1)} %all-to-all-done.refs_0_, bf16[16,128,128]{2,1,0:T(8,128)(2,1)S(1)} %all_to_all.35.refs_1_, bf16[4,16,128,128]{3,2,1,0:T(8,128)(2,1)S(1)} %shard_map.78.refs_1_.refs_2_, ...), custom_call_target="tpu_custom_call" | custom-call | flops 536870912 | bytes 5505024 | tf_op jit(solution)/shard_map/pallas_call | solution.py:138
  60.4 2.6 %collective-permute-start.4 = (f32[128,512]{1,0:T(8,128)S(1)}, f32[128,512]{1,0:T(8,128)S(1)}, u32[]{:S(2)}, u32[]{:S(2)}) collective-permute-start(f32[128,512]{1,0:T(8,128)S(1)} %shard_map.88), channel_id=1, source_target_pairs={{0,1},{1,0},{2,3},{3,2},{4,5},{5,4},{6,7},{7,6},{8,9},{9,8},{10,11... | collective-permute-start | bytes 786440 | tf_op jit(solution)/shard_map/ppermute | solution.py:246
  64.9 3.7 %collective-permute-start.5 = (bf16[128,128]{1,0:T(8,128)(2,1)S(1)}, bf16[128,128]{1,0:T(8,128)(2,1)S(1)}, u32[]{:S(2)}, u32[]{:S(2)}) collective-permute-start(bf16[128,128]{1,0:T(8,128)(2,1)S(1)} %get-tuple-element.18.refs_0_.hid_ref.refs_1_), channel_id=1, source_target_pairs={{0,32},{32,64},{64,96},{1,33},{33,65},{65,97},{2,34},{34,66},{66,9... | collective-permute-start | bytes 98312 | tf_op jit(solution)/shard_map/ppermute | solution.py:271
  70.3 18.6 %all_to_all.36.refs_0_ = bf16[16,128,256]{2,1,0:T(8,128)(2,1)S(1)} all-to-all(bf16[16,128,256]{2,1,0:T(8,128)(2,1)S(1)} %shard_map.90), channel_id=1, replica_groups={{0,2,4,6,8,10,12,14,16,18,20,22,24,26,28,30},{1,3,5,7,9,11,13,15,17,19,..., dimensions={0} | all-to-all | bytes 2097152 | tf_op jit(solution)/shard_map/all_to_all | solution.py:250
  88.9 2.9 %shard_map.92 = f32[128,512]{1,0:T(8,128)S(1)} custom-call(s32[2]{0:T(128)S(1)} %pad_add_fusion.info_ref, bf16[16,128,256]{2,1,0:T(8,128)(2,1)S(1)} %all_to_all.36.refs_0_, bf16[4,16,128,128]{3,2,1,0:T(8,128)(2,1)S(1)} %shard_map.78.refs_1_.refs_2_, bf16[16,128,512]{2,1,0:T(8,128)(2,1)} %collective-permute-done.refs_2_.refs_3_.refs_1_, ...), custom_call_target="tpu_custom_call" | custom-call | flops 536870912 | bytes 5505024 | tf_op jit(solution)/shard_map/pallas_call | solution.py:138
  91.9 2.2 collective-permute-start.6
  96.0 3.7 %collective-permute-start.7 = (bf16[128,128]{1,0:T(8,128)(2,1)S(1)}, bf16[128,128]{1,0:T(8,128)(2,1)S(1)}, u32[]{:S(2)}, u32[]{:S(2)}) collective-permute-start(bf16[128,128]{1,0:T(8,128)(2,1)S(1)} %get-tuple-element.20.refs_0_.hid_ref.refs_2_), channel_id=1, source_target_pairs={{0,32},{32,64},{64,96},{1,33},{33,65},{65,97},{2,34},{34,66},{66,9... | collective-permute-start | bytes 98312 | tf_op jit(solution)/shard_map/ppermute | solution.py:271
  101.3 18.6 %all_to_all.37.refs_0_ = bf16[16,128,256]{2,1,0:T(8,128)(2,1)S(1)} all-to-all(bf16[16,128,256]{2,1,0:T(8,128)(2,1)S(1)} %shard_map.94), channel_id=1, replica_groups={{0,2,4,6,8,10,12,14,16,18,20,22,24,26,28,30},{1,3,5,7,9,11,13,15,17,19,..., dimensions={0} | all-to-all | bytes 2097152 | tf_op jit(solution)/shard_map/all_to_all | solution.py:250
  119.9 2.9 %shard_map.96 = f32[128,512]{1,0:T(8,128)S(1)} custom-call(s32[2]{0:T(128)S(1)} %pad_add_fusion.info_ref, bf16[16,128,256]{2,1,0:T(8,128)(2,1)S(1)} %all_to_all.37.refs_0_, bf16[4,16,128,128]{3,2,1,0:T(8,128)(2,1)S(1)} %shard_map.78.refs_1_.refs_2_, bf16[16,128,512]{2,1,0:T(8,128)(2,1)} %collective-permute-done.refs_2_.refs_3_.refs_1_, ...), custom_call_target="tpu_custom_call" | custom-call | flops 536870912 | bytes 5505024 | tf_op jit(solution)/shard_map/pallas_call | solution.py:138
  122.8 2.3 %collective-permute-start.8 = (f32[128,512]{1,0:T(8,128)S(1)}, f32[128,512]{1,0:T(8,128)S(1)}, u32[]{:S(2)}, u32[]{:S(2)}) collective-permute-start(f32[128,512]{1,0:T(8,128)S(1)} %shard_map.96), channel_id=1, source_target_pairs={{0,1},{1,0},{2,3},{3,2},{4,5},{5,4},{6,7},{7,6},{8,9},{9,8},{10,11... | collective-permute-start | bytes 786440 | tf_op jit(solution)/shard_map/ppermute | solution.py:246
  127.0 3.7 %collective-permute-start.9 = (bf16[128,128]{1,0:T(8,128)(2,1)S(1)}, bf16[128,128]{1,0:T(8,128)(2,1)S(1)}, u32[]{:S(2)}, u32[]{:S(2)}) collective-permute-start(bf16[128,128]{1,0:T(8,128)(2,1)S(1)} %get-tuple-element.22.refs_0_.hid_ref.refs_3_), channel_id=1, source_target_pairs={{0,32},{32,64},{64,96},{1,33},{33,65},{65,97},{2,34},{34,66},{66,9... | collective-permute-start | bytes 98312 | tf_op jit(solution)/shard_map/ppermute | solution.py:271
  132.4 18.6 %all_to_all.38.refs_0_ = bf16[16,128,256]{2,1,0:T(8,128)(2,1)S(1)} all-to-all(bf16[16,128,256]{2,1,0:T(8,128)(2,1)S(1)} %shard_map.98), channel_id=1, replica_groups={{0,2,4,6,8,10,12,14,16,18,20,22,24,26,28,30},{1,3,5,7,9,11,13,15,17,19,..., dimensions={0} | all-to-all | bytes 2097152 | tf_op jit(solution)/shard_map/all_to_all | solution.py:250
  150.9 2.9 %shard_map.100 = f32[128,512]{1,0:T(8,128)S(1)} custom-call(s32[2]{0:T(128)S(1)} %pad_add_fusion.info_ref, bf16[16,128,256]{2,1,0:T(8,128)(2,1)S(1)} %all_to_all.38.refs_0_, bf16[16,128,512]{2,1,0:T(8,128)(2,1)} %collective-permute-done.refs_2_.refs_3_.refs_1_, bf16[16,128,512]{2,1,0:T(8,128)(2,1)} %collective-permute-done.1.refs_3_.refs_4_.refs_2_), custom_call_target="tpu_custom_call" | custom-call | flops 536870912 | bytes 5505024 | tf_op jit(solution)/shard_map/pallas_call | solution.py:138
  153.9 2.5 %collective-permute-start.10 = (f32[128,512]{1,0:T(8,128)S(1)}, f32[128,512]{1,0:T(8,128)S(1)}, u32[]{:S(2)}, u32[]{:S(2)}) collective-permute-start(f32[128,512]{1,0:T(8,128)S(1)} %shard_map.100), channel_id=1, source_target_pairs={{0,1},{1,0},{2,3},{3,2},{4,5},{5,4},{6,7},{7,6},{8,9},{9,8},{10,11... | collective-permute-start | bytes 786440 | tf_op jit(solution)/shard_map/ppermute | solution.py:246
  158.2 3.7 %collective-permute-start.11 = (bf16[128,128]{1,0:T(8,128)(2,1)S(1)}, bf16[128,128]{1,0:T(8,128)(2,1)S(1)}, u32[]{:S(2)}, u32[]{:S(2)}) collective-permute-start(bf16[128,128]{1,0:T(8,128)(2,1)S(1)} %get-tuple-element.24.refs_0_.hid_ref.refs_4_), channel_id=1, source_target_pairs={{0,32},{32,64},{64,96},{1,33},{33,65},{65,97},{2,34},{34,66},{66,9... | collective-permute-start | bytes 98312 | tf_op jit(solution)/shard_map/ppermute | solution.py:271
  163.6 18.5 %all_to_all.39.refs_0_ = bf16[16,128,256]{2,1,0:T(8,128)(2,1)S(1)} all-to-all(bf16[16,128,256]{2,1,0:T(8,128)(2,1)S(1)} %shard_map.102), channel_id=1, replica_groups={{0,2,4,6,8,10,12,14,16,18,20,22,24,26,28,30},{1,3,5,7,9,11,13,15,17,19,..., dimensions={0} | all-to-all | bytes 2097152 | tf_op jit(solution)/shard_map/all_to_all | solution.py:250
  182.1 2.9 %shard_map.104 = f32[128,512]{1,0:T(8,128)S(1)} custom-call(s32[2]{0:T(128)S(1)} %pad_add_fusion.info_ref, bf16[16,128,256]{2,1,0:T(8,128)(2,1)S(1)} %all_to_all.39.refs_0_, bf16[16,128,512]{2,1,0:T(8,128)(2,1)} %collective-permute-done.refs_2_.refs_3_.refs_1_, bf16[16,128,512]{2,1,0:T(8,128)(2,1)} %collective-permute-done.1.refs_3_.refs_4_.refs_2_), custom_call_target="tpu_custom_call" | custom-call | flops 536870912 | bytes 5505024 | tf_op jit(solution)/shard_map/pallas_call | solution.py:138
  185.0 2.3 %collective-permute-start.12 = (f32[128,512]{1,0:T(8,128)S(1)}, f32[128,512]{1,0:T(8,128)S(1)}, u32[]{:S(2)}, u32[]{:S(2)}) collective-permute-start(f32[128,512]{1,0:T(8,128)S(1)} %shard_map.104), channel_id=1, source_target_pairs={{0,1},{1,0},{2,3},{3,2},{4,5},{5,4},{6,7},{7,6},{8,9},{9,8},{10,11... | collective-permute-start | bytes 786440 | tf_op jit(solution)/shard_map/ppermute | solution.py:246
  189.2 3.7 %collective-permute-start.13 = (bf16[128,128]{1,0:T(8,128)(2,1)S(1)}, bf16[128,128]{1,0:T(8,128)(2,1)S(1)}, u32[]{:S(2)}, u32[]{:S(2)}) collective-permute-start(bf16[128,128]{1,0:T(8,128)(2,1)S(1)} %get-tuple-element.26.refs_0_.hid_ref.refs_5_), channel_id=1, source_target_pairs={{0,32},{32,64},{64,96},{1,33},{33,65},{65,97},{2,34},{34,66},{66,9... | collective-permute-start | bytes 98312 | tf_op jit(solution)/shard_map/ppermute | solution.py:271
  194.6 18.5 %all_to_all.40.refs_0_ = bf16[16,128,256]{2,1,0:T(8,128)(2,1)S(1)} all-to-all(bf16[16,128,256]{2,1,0:T(8,128)(2,1)S(1)} %shard_map.106), channel_id=1, replica_groups={{0,2,4,6,8,10,12,14,16,18,20,22,24,26,28,30},{1,3,5,7,9,11,13,15,17,19,..., dimensions={0} | all-to-all | bytes 2097152 | tf_op jit(solution)/shard_map/all_to_all | solution.py:250
  213.1 2.9 %shard_map.108 = f32[128,512]{1,0:T(8,128)S(1)} custom-call(s32[2]{0:T(128)S(1)} %pad_add_fusion.info_ref, bf16[16,128,256]{2,1,0:T(8,128)(2,1)S(1)} %all_to_all.40.refs_0_, bf16[16,128,512]{2,1,0:T(8,128)(2,1)} %collective-permute-done.refs_2_.refs_3_.refs_1_, bf16[16,128,512]{2,1,0:T(8,128)(2,1)} %collective-permute-done.1.refs_3_.refs_4_.refs_2_), custom_call_target="tpu_custom_call" | custom-call | flops 536870912 | bytes 5505024 | tf_op jit(solution)/shard_map/pallas_call | solution.py:138
  216.1 2.3 %collective-permute-start.14 = (f32[128,512]{1,0:T(8,128)S(1)}, f32[128,512]{1,0:T(8,128)S(1)}, u32[]{:S(2)}, u32[]{:S(2)}) collective-permute-start(f32[128,512]{1,0:T(8,128)S(1)} %shard_map.108), channel_id=1, source_target_pairs={{0,1},{1,0},{2,3},{3,2},{4,5},{5,4},{6,7},{7,6},{8,9},{9,8},{10,11... | collective-permute-start | bytes 786440 | tf_op jit(solution)/shard_map/ppermute | solution.py:246
  (57 shorter events, 32.2 us)
Async XLA Ops:
  0.7 2.2 copy-start.4
  2.9 4.2 %copy-start.6 = (bf16[1,4096,4,128]{3,2,1,0:T(4,128)(2,1)S(1)}, bf16[1,4096,4,128]{3,2,1,0:T(4,128)(2,1)}, u32[]{:S(2)}) copy-start(bf16[1,4096,4,128]{3,2,1,0:T(4,128)(2,1)} %param.7) | copy-start | bytes 12582916
  5.7 24.3 %collective-permute-start = (bf16[16,128,512]{2,1,0:T(8,128)(2,1)}, bf16[16,128,512]{2,1,0:T(8,128)(2,1)}, u32[]{:S(2)}, u32[]{:S(2)}) collective-permute-start(bf16[16,128,512]{2,1,0:T(8,128)(2,1)} %shard_map.82), channel_id=1, source_target_pairs={{0,1},{1,0},{2,3},{3,2},{4,5},{5,4},{6,7},{7,6},{8,9},{9,8},{10,11... | collective-permute-start | bytes 6291464 | tf_op jit(solution)/shard_map/ppermute | solution.py:246
  7.1 2.9 %copy-start.1 = (bf16[1,128,128]{2,1,0:T(8,128)(2,1)S(1)}, bf16[1,128,128]{2,1,0:T(8,128)(2,1)}, u32[]{:S(2)}) copy-start(bf16[1,128,128]{2,1,0:T(8,128)(2,1)} %param.10) | copy-start | bytes 98308
  10.0 20.0 %collective-permute-start.1 = (bf16[16,128,512]{2,1,0:T(8,128)(2,1)}, bf16[16,128,512]{2,1,0:T(8,128)(2,1)}, u32[]{:S(2)}, u32[]{:S(2)}) collective-permute-start(bf16[16,128,512]{2,1,0:T(8,128)(2,1)} %shard_map.83), channel_id=1, source_target_pairs={{0,1},{1,0},{2,3},{3,2},{4,5},{5,4},{6,7},{7,6},{8,9},{9,8},{10,11... | collective-permute-start | bytes 6291464 | tf_op jit(solution)/shard_map/ppermute | solution.py:246
  11.5 18.5 %all-to-all-start = ((bf16[16,128,128]{2,1,0:T(8,128)(2,1)}), bf16[16,128,128]{2,1,0:T(8,128)(2,1)S(1)}, u32[]{:S(2)}, u32[]{:S(2)}) async-start(bf16[16,128,128]{2,1,0:T(8,128)(2,1)} %shard_map.77), calls=%async_computation | async-start | bytes 1048576 | tf_op jit(solution)/shard_map/all_to_all | solution.py:250
  19.3 2.2 copy-start
  29.9 5.1 %copy-start.5 = (bf16[1,4096,4,128]{3,2,1,0:T(4,128)(2,1)S(1)}, bf16[1,4096,4,128]{3,2,1,0:T(4,128)(2,1)}, u32[]{:S(2)}) copy-start(bf16[1,4096,4,128]{3,2,1,0:T(4,128)(2,1)} %param.8) | copy-start | bytes 12582916
  33.0 3.5 %copy-start.7 = (bf16[1,4096,4,128]{3,2,1,0:T(4,128)(2,1)S(1)}, bf16[1,4096,4,128]{3,2,1,0:T(4,128)(2,1)}, u32[]{:S(2)}) copy-start(bf16[1,4096,4,128]{3,2,1,0:T(4,128)(2,1)} %param.7) | copy-start | bytes 12582916
  33.1 6.3 %collective-permute-start.2 = (f32[128,512]{1,0:T(8,128)S(1)}, f32[128,512]{1,0:T(8,128)S(1)}, u32[]{:S(2)}, u32[]{:S(2)}) collective-permute-start(f32[128,512]{1,0:T(8,128)S(1)} %shard_map.84), channel_id=1, source_target_pairs={{0,1},{1,0},{2,3},{3,2},{4,5},{5,4},{6,7},{7,6},{8,9},{9,8},{10,11... | collective-permute-start | bytes 786440 | tf_op jit(solution)/shard_map/ppermute | solution.py:246
  38.0 1.3 copy-start.2
  38.1 1.3 copy-start.3
  40.0 4.1 %collective-permute-start.3 = (bf16[128,128]{1,0:T(8,128)(2,1)S(1)}, bf16[128,128]{1,0:T(8,128)(2,1)S(1)}, u32[]{:S(2)}, u32[]{:S(2)}) collective-permute-start(bf16[128,128]{1,0:T(8,128)(2,1)S(1)} %get-tuple-element.16.refs_0_.hid_ref), channel_id=1, source_target_pairs={{0,32},{32,64},{64,96},{1,33},{33,65},{65,97},{2,34},{34,66},{66,9... | collective-permute-start | bytes 98312 | tf_op jit(solution)/shard_map/ppermute | solution.py:271
  60.4 3.9 %collective-permute-start.4 = (f32[128,512]{1,0:T(8,128)S(1)}, f32[128,512]{1,0:T(8,128)S(1)}, u32[]{:S(2)}, u32[]{:S(2)}) collective-permute-start(f32[128,512]{1,0:T(8,128)S(1)} %shard_map.88), channel_id=1, source_target_pairs={{0,1},{1,0},{2,3},{3,2},{4,5},{5,4},{6,7},{7,6},{8,9},{9,8},{10,11... | collective-permute-start | bytes 786440 | tf_op jit(solution)/shard_map/ppermute | solution.py:246
  64.9 4.7 %collective-permute-start.5 = (bf16[128,128]{1,0:T(8,128)(2,1)S(1)}, bf16[128,128]{1,0:T(8,128)(2,1)S(1)}, u32[]{:S(2)}, u32[]{:S(2)}) collective-permute-start(bf16[128,128]{1,0:T(8,128)(2,1)S(1)} %get-tuple-element.18.refs_0_.hid_ref.refs_1_), channel_id=1, source_target_pairs={{0,32},{32,64},{64,96},{1,33},{33,65},{65,97},{2,34},{34,66},{66,9... | collective-permute-start | bytes 98312 | tf_op jit(solution)/shard_map/ppermute | solution.py:271
  91.9 3.5 %collective-permute-start.6 = (f32[128,512]{1,0:T(8,128)S(1)}, f32[128,512]{1,0:T(8,128)S(1)}, u32[]{:S(2)}, u32[]{:S(2)}) collective-permute-start(f32[128,512]{1,0:T(8,128)S(1)} %shard_map.92), channel_id=1, source_target_pairs={{0,1},{1,0},{2,3},{3,2},{4,5},{5,4},{6,7},{7,6},{8,9},{9,8},{10,11... | collective-permute-start | bytes 786440 | tf_op jit(solution)/shard_map/ppermute | solution.py:246
  96.0 4.7 %collective-permute-start.7 = (bf16[128,128]{1,0:T(8,128)(2,1)S(1)}, bf16[128,128]{1,0:T(8,128)(2,1)S(1)}, u32[]{:S(2)}, u32[]{:S(2)}) collective-permute-start(bf16[128,128]{1,0:T(8,128)(2,1)S(1)} %get-tuple-element.20.refs_0_.hid_ref.refs_2_), channel_id=1, source_target_pairs={{0,32},{32,64},{64,96},{1,33},{33,65},{65,97},{2,34},{34,66},{66,9... | collective-permute-start | bytes 98312 | tf_op jit(solution)/shard_map/ppermute | solution.py:271
  122.8 3.6 %collective-permute-start.8 = (f32[128,512]{1,0:T(8,128)S(1)}, f32[128,512]{1,0:T(8,128)S(1)}, u32[]{:S(2)}, u32[]{:S(2)}) collective-permute-start(f32[128,512]{1,0:T(8,128)S(1)} %shard_map.96), channel_id=1, source_target_pairs={{0,1},{1,0},{2,3},{3,2},{4,5},{5,4},{6,7},{7,6},{8,9},{9,8},{10,11... | collective-permute-start | bytes 786440 | tf_op jit(solution)/shard_map/ppermute | solution.py:246
  127.0 4.7 %collective-permute-start.9 = (bf16[128,128]{1,0:T(8,128)(2,1)S(1)}, bf16[128,128]{1,0:T(8,128)(2,1)S(1)}, u32[]{:S(2)}, u32[]{:S(2)}) collective-permute-start(bf16[128,128]{1,0:T(8,128)(2,1)S(1)} %get-tuple-element.22.refs_0_.hid_ref.refs_3_), channel_id=1, source_target_pairs={{0,32},{32,64},{64,96},{1,33},{33,65},{65,97},{2,34},{34,66},{66,9... | collective-permute-start | bytes 98312 | tf_op jit(solution)/shard_map/ppermute | solution.py:271
  153.9 3.7 %collective-permute-start.10 = (f32[128,512]{1,0:T(8,128)S(1)}, f32[128,512]{1,0:T(8,128)S(1)}, u32[]{:S(2)}, u32[]{:S(2)}) collective-permute-start(f32[128,512]{1,0:T(8,128)S(1)} %shard_map.100), channel_id=1, source_target_pairs={{0,1},{1,0},{2,3},{3,2},{4,5},{5,4},{6,7},{7,6},{8,9},{9,8},{10,11... | collective-permute-start | bytes 786440 | tf_op jit(solution)/shard_map/ppermute | solution.py:246
  158.2 4.7 %collective-permute-start.11 = (bf16[128,128]{1,0:T(8,128)(2,1)S(1)}, bf16[128,128]{1,0:T(8,128)(2,1)S(1)}, u32[]{:S(2)}, u32[]{:S(2)}) collective-permute-start(bf16[128,128]{1,0:T(8,128)(2,1)S(1)} %get-tuple-element.24.refs_0_.hid_ref.refs_4_), channel_id=1, source_target_pairs={{0,32},{32,64},{64,96},{1,33},{33,65},{65,97},{2,34},{34,66},{66,9... | collective-permute-start | bytes 98312 | tf_op jit(solution)/shard_map/ppermute | solution.py:271
  185.0 3.5 %collective-permute-start.12 = (f32[128,512]{1,0:T(8,128)S(1)}, f32[128,512]{1,0:T(8,128)S(1)}, u32[]{:S(2)}, u32[]{:S(2)}) collective-permute-start(f32[128,512]{1,0:T(8,128)S(1)} %shard_map.104), channel_id=1, source_target_pairs={{0,1},{1,0},{2,3},{3,2},{4,5},{5,4},{6,7},{7,6},{8,9},{9,8},{10,11... | collective-permute-start | bytes 786440 | tf_op jit(solution)/shard_map/ppermute | solution.py:246
  189.2 4.7 %collective-permute-start.13 = (bf16[128,128]{1,0:T(8,128)(2,1)S(1)}, bf16[128,128]{1,0:T(8,128)(2,1)S(1)}, u32[]{:S(2)}, u32[]{:S(2)}) collective-permute-start(bf16[128,128]{1,0:T(8,128)(2,1)S(1)} %get-tuple-element.26.refs_0_.hid_ref.refs_5_), channel_id=1, source_target_pairs={{0,32},{32,64},{64,96},{1,33},{33,65},{65,97},{2,34},{34,66},{66,9... | collective-permute-start | bytes 98312 | tf_op jit(solution)/shard_map/ppermute | solution.py:271
  216.1 3.5 %collective-permute-start.14 = (f32[128,512]{1,0:T(8,128)S(1)}, f32[128,512]{1,0:T(8,128)S(1)}, u32[]{:S(2)}, u32[]{:S(2)}) collective-permute-start(f32[128,512]{1,0:T(8,128)S(1)} %shard_map.108), channel_id=1, source_target_pairs={{0,1},{1,0},{2,3},{3,2},{4,5},{5,4},{6,7},{7,6},{8,9},{9,8},{10,11... | collective-permute-start | bytes 786440 | tf_op jit(solution)/shard_map/ppermute | solution.py:246

commit v3 on v2

v3 whole, which is shorter than its diff:
```python
import functools

import jax
import jax.numpy as jnp
from jax import lax
from jax.experimental import pallas as pl
from jax.experimental.pallas import tpu as pltpu
from jax.sharding import PartitionSpec as P

VMEM = pl.BlockSpec(memory_space=pltpu.VMEM)
HBM = pl.BlockSpec(memory_space=pltpu.HBM)


def resident(x):
    return pltpu.with_memory_space_constraint(x, pltpu.VMEM)


def outside(x):
    return pltpu.with_memory_space_constraint(x, pltpu.HBM)


def limits(mib):
    return pltpu.CompilerParams(vmem_limit_bytes=mib << 20)


def sort_kernel(other, w_ref, out_ref, natural, ordered, in_sems, out_sems):
    blocks, depth, wide = ordered.shape
    unit = natural.shape[2]
    gates = wide // unit
    half = depth // 2
    rows = half * gates
    core = lax.axis_index("col") & 1
    side = 1 - core if other else core
    to = lax.broadcasted_iota(jnp.int32, (rows, rows), 0)
    come = lax.broadcasted_iota(jnp.int32, (rows, rows), 1)
    order = come == gates * (to % half) + to // half
    order = order.astype(jnp.float32).astype(jnp.bfloat16)
    parts = in_sems.shape[0]
    size = blocks // parts

    def incoming(part):
        chosen = pl.ds(part * size, size)
        return pltpu.make_async_copy(w_ref.at[chosen, side], natural.at[chosen], in_sems.at[part])

    def outgoing(part):
        chosen = pl.ds(part * size, size)
        return pltpu.make_async_copy(ordered.at[chosen], out_ref.at[chosen], out_sems.at[part])

    for part in range(parts):
        incoming(part).start()
    for part in range(parts):
        incoming(part).wait()
        for j in range(part * size, (part + 1) * size):
            both = jnp.concatenate([natural[j, :rows, :], natural[j, rows:, :]], axis=1)
            sorted_rows = jnp.dot(order, both, preferred_element_type=jnp.float32)
            sorted_rows = sorted_rows.astype(jnp.bfloat16)
            for h in range(2):
                for g in range(gates):
                    ordered[j, h * half : (h + 1) * half, g * unit : (g + 1) * unit] = sorted_rows[
                        g * half : (g + 1) * half, h * unit : (h + 1) * unit
                    ]
        outgoing(part).start()
    for part in range(parts):
        outgoing(part).wait()


def sorted_side(w, blocks, other):
    gates, unit = w.shape[1:]
    depth = w.shape[0] // (2 * blocks)
    wide = gates * unit
    parts = 4
    return pl.pallas_call(
        functools.partial(sort_kernel, other),
        out_shape=pltpu.HBM((blocks, depth, wide), w.dtype),
        in_specs=[HBM],
        out_specs=HBM,
        scratch_shapes=[
            pltpu.VMEM((blocks, depth * gates, unit), w.dtype),
            pltpu.VMEM((blocks, depth, wide), w.dtype),
            pltpu.SemaphoreType.DMA((parts,)),
            pltpu.SemaphoreType.DMA((parts,)),
        ],
        cost_estimate=pl.CostEstimate(
            flops=2_000_000_000, bytes_accessed=4 * blocks * depth * wide, transcendentals=0
        ),
        compiler_params=limits(8),
    )(outside(w.reshape(blocks, 2, depth * gates, unit)))


def pick_kernel(x_ref, out_ref, sems):
    blocks, unit = out_ref.shape[1], out_ref.shape[3]
    core = lax.axis_index("col") & 1
    copies = []
    for j in range(blocks):
        at = pl.multiple_of((2 * j + core) * unit, unit)
        copies.append(
            pltpu.make_async_copy(x_ref.at[:, :, pl.ds(at, unit)], out_ref.at[:, j], sems.at[j])
        )
    for copy in copies:
        copy.start()
    for copy in copies:
        copy.wait()


def picked(x, blocks, unit):
    steps, batch, _ = x.shape
    return pl.pallas_call(
        pick_kernel,
        out_shape=jax.ShapeDtypeStruct((steps, blocks, batch, unit), x.dtype),
        in_specs=[HBM],
        out_specs=VMEM,
        scratch_shapes=[pltpu.SemaphoreType.DMA((blocks,))],
        cost_estimate=pl.CostEstimate(
            flops=1_000_000_000, bytes_accessed=4 * x.size // 2, transcendentals=0
        ),
        compiler_params=limits(1),
    )(outside(x))


def fetch_kernel(count, *refs):
    sems = refs[-1]
    copies = [
        pltpu.make_async_copy(refs[i], refs[count + 1 + i], sems.at[i]) for i in range(count)
    ]
    for copy in copies:
        copy.start()
    for copy in copies:
        copy.wait()


def fetched(arrays, after):
    count = len(arrays)
    return pl.pallas_call(
        functools.partial(fetch_kernel, count),
        out_shape=tuple(jax.ShapeDtypeStruct(array.shape, array.dtype) for array in arrays),
        in_specs=[*[HBM] * count, pl.BlockSpec(memory_space=pl.ANY)],
        out_specs=tuple([VMEM] * count),
        scratch_shapes=[pltpu.SemaphoreType.DMA((count,))],
        compiler_params=limits(1),
    )(*[outside(array) for array in arrays], after)


def product_kernel(turn, stage, fed, *refs):
    refs = list(refs)
    out_ref, w_in_ref, w_rec_ref = refs.pop(), refs.pop(), refs.pop()
    x_ref = refs.pop() if fed else None
    blocks, unit, width = w_rec_ref.shape
    bottom = lax.axis_index("layer") == 0

    def own(j):
        if stage == 0:
            return refs[0][j]
        if stage == 1:
            return jnp.where(bottom, refs[1][j], refs[0][j])
        return refs[0][j, :, :unit]

    def below(j):
        if stage == 0:
            came = jnp.zeros_like(x_ref[turn, j])
        elif stage == 1:
            came = refs[1][j]
        else:
            came = refs[0][j, :, unit:]
        return jnp.where(bottom, x_ref[turn, j], came) if fed else came

    wide = 256
    for n in range(width // wide):
        cols = slice(n * wide, (n + 1) * wide)
        total = None
        for block, w_ref in ((own, w_rec_ref), (below, w_in_ref)):
            for j in range(0, blocks, 2):
                left = jnp.concatenate([block(j), block(j + 1)], axis=1)
                right = w_ref[j : j + 2, :, cols].reshape(2 * unit, wide)
                term = jnp.dot(left, right, preferred_element_type=jnp.float32)
                total = term if total is None else total + term
        out_ref[:, cols] = total


def product(gathered, x, w_rec, w_in, turn, stage):
    blocks, unit, width = w_rec.shape
    batch = gathered[0].shape[1]
    args = [*gathered, *([] if x is None else [x]), w_rec, w_in]
    return pl.pallas_call(
        functools.partial(product_kernel, turn, stage, x is not None),
        out_shape=jax.ShapeDtypeStruct((batch, width), jnp.float32),
        in_specs=[*[VMEM] * len(args)],
        out_specs=VMEM,
        cost_estimate=pl.CostEstimate(
            flops=4 * blocks * unit * batch * width,
            bytes_accessed=4 * blocks * unit * (batch + width) + 4 * batch * width,
            transcendentals=0,
        ),
        compiler_params=limits(4),
    )(*[resident(arg) for arg in args])


def gates_kernel(turn, steps, here_ref, came_ref, bias_ref, cell_ref, hid_ref, cell_out, hid_out):
    unit = cell_ref.shape[1]
    layer = lax.axis_index("layer")
    valid = jnp.logical_and(turn >= layer, turn < layer + steps)

    def gate(k):
        cols = slice(k * unit, (k + 1) * unit)
        return here_ref[:, cols] + came_ref[:, cols] + bias_ref[k : k + 1, :]

    cell = cell_ref[...]
    cell_new = jax.nn.sigmoid(gate(1)) * cell + jax.nn.sigmoid(gate(0)) * jnp.tanh(gate(2))
    hidden_new = (jax.nn.sigmoid(gate(3)) * jnp.tanh(cell_new)).astype(hid_ref.dtype)
    cell_out[...] = jnp.where(valid, cell_new, cell)
    hid_out[...] = jnp.where(valid, hidden_new, hid_ref[...])


def gates(here, came, bias, cell, hidden, turn, steps):
    return pl.pallas_call(
        functools.partial(gates_kernel, turn, steps),
        out_shape=(
            jax.ShapeDtypeStruct(cell.shape, cell.dtype),
            jax.ShapeDtypeStruct(hidden.shape, hidden.dtype),
        ),
        in_specs=[*[VMEM] * 5],
        out_specs=(VMEM, VMEM),
        cost_estimate=pl.CostEstimate(
            flops=20 * cell.size, bytes_accessed=40 * cell.size, transcendentals=5 * cell.size
        ),
        compiler_params=limits(2),
    )(*[resident(arg) for arg in (here, came, bias, cell, hidden)])


def spread_kernel(stage, *refs):
    out_ref = refs[-1]
    unit = refs[0].shape[1]
    layer = lax.axis_index("layer")
    for j in range(out_ref.shape[0]):
        if stage == 0:
            out_ref[j] = refs[0][...]
        elif stage == 1:
            out_ref[j] = jnp.where(layer == 0, refs[0][...], refs[1][...])
        else:
            out_ref[j, :, :unit] = refs[0][...]
            out_ref[j, :, unit:] = refs[1][...]


def spread(parts, stage, copies):
    batch, unit = parts[0].shape
    width = unit * (2 if stage == 2 else 1)
    return pl.pallas_call(
        functools.partial(spread_kernel, stage),
        out_shape=jax.ShapeDtypeStruct((copies, batch, width), parts[0].dtype),
        in_specs=[*[VMEM] * len(parts)],
        out_specs=VMEM,
        cost_estimate=pl.CostEstimate(
            flops=batch * width, bytes_accessed=2 * copies * batch * width, transcendentals=0
        ),
        compiler_params=limits(2),
    )(*[resident(part) for part in parts])


def select_kernel(layers, *refs):
    out_ref = refs[-1]
    layer = lax.axis_index("layer")
    for t in range(out_ref.shape[0]):
        value = refs[t][...]
        for l in range(1, layers):
            value = jnp.where(layer == l, refs[t + l][...], value)
        out_ref[t] = value


def selected(kept, steps, layers):
    return pl.pallas_call(
        functools.partial(select_kernel, layers),
        out_shape=jax.ShapeDtypeStruct((steps, *kept[0].shape), kept[0].dtype),
        in_specs=[*[VMEM] * len(kept)],
        out_specs=VMEM,
        compiler_params=limits(2),
    )(*[resident(value) for value in kept])


def body(inputs, w_input, w_recur, bias, h_start, c_start):
    steps, _, _ = inputs.shape
    unit = w_input.shape[3]
    layers = lax.axis_size("layer")
    devices = lax.axis_size("col")
    chips = devices // 2
    turns = steps + layers - 1
    same_core = [[2 * chip + side for chip in range(chips)] for side in range(2)]
    partners = [(i, i ^ 1) for i in range(devices)]
    upward = [(i, i + 1) for i in range(layers - 1)]

    def across(x):
        return lax.ppermute(x, "col", partners)

    def gathered(parts, stage):
        copies = spread(parts, stage, chips)
        return lax.all_to_all(copies, "col", 0, 0, tiled=True, axis_index_groups=same_core)

    cell = c_start[0]
    hidden = h_start[0]
    start = gathered((hidden,), 0)
    rec_send = across(sorted_side(w_recur[0], chips, True))
    in_send = across(sorted_side(w_input[0], chips, True))
    rec_keep = sorted_side(w_recur[0], chips, False)
    in_keep = sorted_side(w_input[0], chips, False)
    x = picked(inputs, chips, unit)
    rec_send, in_send, rec_keep, in_keep = fetched((rec_send, in_send, rec_keep, in_keep), start)

    kept = []
    blocks = (start,)
    for turn in range(turns):
        stage = min(turn, 2)
        fed = x if turn < steps else None
        came = across(product(blocks, fed, rec_send, in_send, turn, stage))
        here = product(blocks, fed, rec_keep, in_keep, turn, stage)
        cell, hidden = gates(here, came, bias[0], cell, hidden, turn, steps)
        kept.append(hidden)
        if turn + 1 < turns:
            below = lax.ppermute(hidden, "layer", upward)
            blocks = (gathered((hidden, below), min(turn + 1, 2)),)
            if turn == 0:
                blocks = (start, *blocks)
    return selected(kept, steps, layers)[None], cell[None]


def solution(mesh):
    in_specs = (
        P(),
        P("layer", None, None, "col"),
        P("layer", None, None, "col"),
        P("layer", None, "col"),
        P("layer", None, "col"),
        P("layer", None, "col"),
    )
    out_specs = (P("layer", None, None, "col"), P("layer", None, "col"))
    return jax.shard_map(body, mesh=mesh, in_specs=in_specs, out_specs=out_specs, check_vma=False)
```

time: 223 us -> 198 us (0.89)
  Pallas kernels: 51.1 us -> 31.3 us
  local copies, waits for them, and re-layouts: 4.4 us -> 0.01 us
    pallas_call x14, Pallas kernels: 29.6 us -> 9.88 us  [product(): pl.pallas_call(functools.partial(product_kernel, turn, stage, x is not No...]
    pallas_call x4 -> x5, Pallas kernels: 8.65 us -> 16.2 us  [the longest x4 12.6 us: sorted_side(): pl.pallas_call(functools.partial(sort_kernel, other), out_shape=pltpu.HBM...]
    all_to_all x1, waiting for transfers between devices: 7.1 us -> 2.44 us  [gathered(): lax.all_to_all(copies, 'col', 0, 0, tiled=True, axis_index_groups=same_core)]
    unnamed x16 -> x6, local copies, waits for them, and re-layouts: 4.4 us -> 0.01 us
    pallas_call x7, Pallas kernels: 4.83 us -> 1.04 us  [gates(): pl.pallas_call(functools.partial(gates_kernel, turn, steps), out_shape=(j...]
    pallas_call x7, Pallas kernels: 5.47 us -> 1.68 us  [spread(): pl.pallas_call(functools.partial(spread_kernel, stage), out_shape=jax.Sha...]
    ppermute x9, waiting for transfers between devices: 0.02 us -> 3.15 us  [across(): return lax.ppermute(x, 'col', partners)]
  transfers between devices with their start and end apart: 16 -> 16, of which waited for: 7 -> 14; matrix products, arithmetic and copies ran while one was open for 0% -> 0% of each run, Pallas kernels for 8% -> 9%
where the time goes in v3:
time: 198 us; the launch traced here: 197 us
  blocking collectives  106 us (54%)
  starting transfers between devices  47.5 us (24%)
  Pallas kernels  31.3 us (16%)
  waiting for transfers between devices  11.6 us (6%)
    all_to_all x6, blocking collectives, gathered(): lax.all_to_all(copies, 'col', 0, 0, tiled=True, axis_index_groups=same_core)  106 us
    ppermute x6, starting transfers between devices, body(): below = lax.ppermute(hidden, 'layer', upward)  21.7 us
    ppermute x9, starting transfers between devices, across(): return lax.ppermute(x, 'col', partners)  17.9 us
    pallas_call x4, Pallas kernels, sorted_side(): pl.pallas_call(functools.partial(sort_kernel, other), out_shape=pltpu.HBM...  12.6 us
    pallas_call x14, Pallas kernels, product(): pl.pallas_call(functools.partial(product_kernel, turn, stage, x is not No...  9.88 us
    all_to_all x1, starting transfers between devices, gathered(): lax.all_to_all(copies, 'col', 0, 0, tiled=True, axis_index_groups=same_core)  7.88 us
    ppermute x6, waiting for transfers between devices, body(): below = lax.ppermute(hidden, 'layer', upward)  6.03 us
  transfers between devices with their start and end apart: 16, of which 14 were waited for; matrix products, arithmetic and copies ran while one was open for 0% of the time, Pallas kernels for 9%

profile of v3, /device:TPU:1, one launch (start us, length us, event | category | flops | bytes accessed | tf_op | source)
XLA Modules:
  0.0 196.9 jit_solution(8142311012712686595)
XLA Ops:
  0.6 3.1 %shard_map.79 = bf16[16,128,512]{2,1,0:T(8,128)(2,1)} custom-call(bf16[16,2,512,128]{3,2,1,0:T(8,128)(2,1)} %bitcast.18), custom_call_target="tpu_custom_call" | custom-call | flops 2000000000 | bytes 4194304 | tf_op jit(solution)/shard_map/pallas_call | solution.py:72
  3.8 1.5 collective-permute-start
  5.2 3.2 %shard_map.80 = bf16[16,128,512]{2,1,0:T(8,128)(2,1)} custom-call(bf16[16,2,512,128]{3,2,1,0:T(8,128)(2,1)} %bitcast.20), custom_call_target="tpu_custom_call" | custom-call | flops 2000000000 | bytes 4194304 | tf_op jit(solution)/shard_map/pallas_call | solution.py:72
  9.5 7.9 %all-to-all-start = ((bf16[16,128,128]{2,1,0:T(8,128)(2,1)}), bf16[16,128,128]{2,1,0:T(8,128)(2,1)S(1)}, u32[]{:S(2)}, u32[]{:S(2)}) async-start(bf16[16,128,128]{2,1,0:T(8,128)(2,1)} %shard_map.77), calls=%async_computation | async-start | bytes 1048576 | tf_op jit(solution)/shard_map/all_to_all | solution.py:294
  17.3 1.8 shard_map.78.refs_1_.refs_2_
  19.2 3.2 %shard_map.81.refs_2_ = bf16[16,128,512]{2,1,0:T(8,128)(2,1)} custom-call(bf16[16,2,512,128]{3,2,1,0:T(8,128)(2,1)} %bitcast.19), custom_call_target="tpu_custom_call" | custom-call | flops 2000000000 | bytes 4194304 | tf_op jit(solution)/shard_map/pallas_call | solution.py:72
  22.4 3.2 %shard_map.82.refs_3_ = bf16[16,128,512]{2,1,0:T(8,128)(2,1)} custom-call(bf16[16,2,512,128]{3,2,1,0:T(8,128)(2,1)} %bitcast.21), custom_call_target="tpu_custom_call" | custom-call | flops 2000000000 | bytes 4194304 | tf_op jit(solution)/shard_map/pallas_call | solution.py:72
  25.5 2.4 %all-to-all-done.refs_4_.refs_0_ = bf16[16,128,128]{2,1,0:T(8,128)(2,1)S(1)} async-done(((bf16[16,128,128]{2,1,0:T(8,128)(2,1)}), bf16[16,128,128]{2,1,0:T(8,128)(2,1)S(1)}, u32[]{:S(2)}, u32[]{:S(2)}) %all-to-all-start) | async-done | bytes 524320 | tf_op jit(solution)/shard_map/all_to_all | solution.py:294
  28.0 3.5 %shard_map.83 = (bf16[16,128,512]{2,1,0:T(8,128)(2,1)S(1)}, bf16[16,128,512]{2,1,0:T(8,128)(2,1)S(1)}, bf16[16,128,512]{2,1,0:T(8,128)(2,1)S(1)}, bf16[16,128,512]{2,1,0:T(8,128)(2,1)S(1)}) custom-call(bf16[16,128,512]{2,1,0:T(8,128)(2,1)} %collective-permute-done.refs_0_, bf16[16,128,512]{2,1,0:T(8,128)(2,1)} %collective-permute-done.1.refs_1_, ...), custom_call_target="tpu_custom_call" | custom-call | tf_op jit(solution)/shard_map/pallas_call | solution.py:133
  32.2 2.0 collective-permute-start.2
  35.4 3.1 %collective-permute-start.3 = (bf16[128,128]{1,0:T(8,128)(2,1)S(1)}, bf16[128,128]{1,0:T(8,128)(2,1)S(1)}, u32[]{:S(2)}, u32[]{:S(2)}) collective-permute-start(bf16[128,128]{1,0:T(8,128)(2,1)S(1)} %get-tuple-element.24.refs_0_.hid_ref), channel_id=1, source_target_pairs={{0,32},{32,64},{64,96},{1,33},{33,65},{65,97},{2,34},{34,66},{66,9... | collective-permute-start | bytes 98312 | tf_op jit(solution)/shard_map/ppermute | solution.py:316
  38.5 1.0 collective-permute-done.3.refs_1_
  39.6 13.4 %all_to_all.35.refs_1_ = bf16[16,128,128]{2,1,0:T(8,128)(2,1)S(1)} all-to-all(bf16[16,128,128]{2,1,0:T(8,128)(2,1)S(1)} %shard_map.87), channel_id=1, replica_groups={{0,2,4,6,8,10,12,14,16,18,20,22,24,26,28,30},{1,3,5,7,9,11,13,15,17,19,..., dimensions={0} | all-to-all | bytes 1048576 | tf_op jit(solution)/shard_map/all_to_all | solution.py:294
  53.7 2.4 %collective-permute-start.4 = (f32[128,512]{1,0:T(8,128)S(1)}, f32[128,512]{1,0:T(8,128)S(1)}, u32[]{:S(2)}, u32[]{:S(2)}) collective-permute-start(f32[128,512]{1,0:T(8,128)S(1)} %shard_map.89), channel_id=1, source_target_pairs={{0,1},{1,0},{2,3},{3,2},{4,5},{5,4},{6,7},{7,6},{8,9},{9,8},{10,11... | collective-permute-start | bytes 786440 | tf_op jit(solution)/shard_map/ppermute | solution.py:290
  57.3 3.7 %collective-permute-start.5 = (bf16[128,128]{1,0:T(8,128)(2,1)S(1)}, bf16[128,128]{1,0:T(8,128)(2,1)S(1)}, u32[]{:S(2)}, u32[]{:S(2)}) collective-permute-start(bf16[128,128]{1,0:T(8,128)(2,1)S(1)} %get-tuple-element.26.refs_0_.hid_ref.refs_1_), channel_id=1, source_target_pairs={{0,32},{32,64},{64,96},{1,33},{33,65},{65,97},{2,34},{34,66},{66,9... | collective-permute-start | bytes 98312 | tf_op jit(solution)/shard_map/ppermute | solution.py:316
  61.0 1.0 collective-permute-done.5.refs_1_
  62.2 18.4 %all_to_all.36.refs_0_ = bf16[16,128,256]{2,1,0:T(8,128)(2,1)S(1)} all-to-all(bf16[16,128,256]{2,1,0:T(8,128)(2,1)S(1)} %shard_map.91), channel_id=1, replica_groups={{0,2,4,6,8,10,12,14,16,18,20,22,24,26,28,30},{1,3,5,7,9,11,13,15,17,19,..., dimensions={0} | all-to-all | bytes 2097152 | tf_op jit(solution)/shard_map/all_to_all | solution.py:294
  81.3 2.4 %collective-permute-start.6 = (f32[128,512]{1,0:T(8,128)S(1)}, f32[128,512]{1,0:T(8,128)S(1)}, u32[]{:S(2)}, u32[]{:S(2)}) collective-permute-start(f32[128,512]{1,0:T(8,128)S(1)} %shard_map.93), channel_id=1, source_target_pairs={{0,1},{1,0},{2,3},{3,2},{4,5},{5,4},{6,7},{7,6},{8,9},{9,8},{10,11... | collective-permute-start | bytes 786440 | tf_op jit(solution)/shard_map/ppermute | solution.py:290
  84.9 3.7 %collective-permute-start.7 = (bf16[128,128]{1,0:T(8,128)(2,1)S(1)}, bf16[128,128]{1,0:T(8,128)(2,1)S(1)}, u32[]{:S(2)}, u32[]{:S(2)}) collective-permute-start(bf16[128,128]{1,0:T(8,128)(2,1)S(1)} %get-tuple-element.28.refs_0_.hid_ref.refs_2_), channel_id=1, source_target_pairs={{0,32},{32,64},{64,96},{1,33},{33,65},{65,97},{2,34},{34,66},{66,9... | collective-permute-start | bytes 98312 | tf_op jit(solution)/shard_map/ppermute | solution.py:316
  88.6 1.0 collective-permute-done.7.refs_1_
  89.8 18.5 %all_to_all.37.refs_0_ = bf16[16,128,256]{2,1,0:T(8,128)(2,1)S(1)} all-to-all(bf16[16,128,256]{2,1,0:T(8,128)(2,1)S(1)} %shard_map.95), channel_id=1, replica_groups={{0,2,4,6,8,10,12,14,16,18,20,22,24,26,28,30},{1,3,5,7,9,11,13,15,17,19,..., dimensions={0} | all-to-all | bytes 2097152 | tf_op jit(solution)/shard_map/all_to_all | solution.py:294
  109.0 2.5 %collective-permute-start.8 = (f32[128,512]{1,0:T(8,128)S(1)}, f32[128,512]{1,0:T(8,128)S(1)}, u32[]{:S(2)}, u32[]{:S(2)}) collective-permute-start(f32[128,512]{1,0:T(8,128)S(1)} %shard_map.97), channel_id=1, source_target_pairs={{0,1},{1,0},{2,3},{3,2},{4,5},{5,4},{6,7},{7,6},{8,9},{9,8},{10,11... | collective-permute-start | bytes 786440 | tf_op jit(solution)/shard_map/ppermute | solution.py:290
  112.7 3.7 %collective-permute-start.9 = (bf16[128,128]{1,0:T(8,128)(2,1)S(1)}, bf16[128,128]{1,0:T(8,128)(2,1)S(1)}, u32[]{:S(2)}, u32[]{:S(2)}) collective-permute-start(bf16[128,128]{1,0:T(8,128)(2,1)S(1)} %get-tuple-element.30.refs_0_.hid_ref.refs_3_), channel_id=1, source_target_pairs={{0,32},{32,64},{64,96},{1,33},{33,65},{65,97},{2,34},{34,66},{66,9... | collective-permute-start | bytes 98312 | tf_op jit(solution)/shard_map/ppermute | solution.py:316
  116.5 1.0 collective-permute-done.9.refs_1_
  117.6 18.5 %all_to_all.38.refs_0_ = bf16[16,128,256]{2,1,0:T(8,128)(2,1)S(1)} all-to-all(bf16[16,128,256]{2,1,0:T(8,128)(2,1)S(1)} %shard_map.99), channel_id=1, replica_groups={{0,2,4,6,8,10,12,14,16,18,20,22,24,26,28,30},{1,3,5,7,9,11,13,15,17,19,..., dimensions={0} | all-to-all | bytes 2097152 | tf_op jit(solution)/shard_map/all_to_all | solution.py:294
  136.8 2.4 %collective-permute-start.10 = (f32[128,512]{1,0:T(8,128)S(1)}, f32[128,512]{1,0:T(8,128)S(1)}, u32[]{:S(2)}, u32[]{:S(2)}) collective-permute-start(f32[128,512]{1,0:T(8,128)S(1)} %shard_map.101), channel_id=1, source_target_pairs={{0,1},{1,0},{2,3},{3,2},{4,5},{5,4},{6,7},{7,6},{8,9},{9,8},{10,11... | collective-permute-start | bytes 786440 | tf_op jit(solution)/shard_map/ppermute | solution.py:290
  140.4 3.7 %collective-permute-start.11 = (bf16[128,128]{1,0:T(8,128)(2,1)S(1)}, bf16[128,128]{1,0:T(8,128)(2,1)S(1)}, u32[]{:S(2)}, u32[]{:S(2)}) collective-permute-start(bf16[128,128]{1,0:T(8,128)(2,1)S(1)} %get-tuple-element.32.refs_0_.hid_ref.refs_4_), channel_id=1, source_target_pairs={{0,32},{32,64},{64,96},{1,33},{33,65},{65,97},{2,34},{34,66},{66,9... | collective-permute-start | bytes 98312 | tf_op jit(solution)/shard_map/ppermute | solution.py:316
  145.2 18.5 %all_to_all.39.refs_0_ = bf16[16,128,256]{2,1,0:T(8,128)(2,1)S(1)} all-to-all(bf16[16,128,256]{2,1,0:T(8,128)(2,1)S(1)} %shard_map.103), channel_id=1, replica_groups={{0,2,4,6,8,10,12,14,16,18,20,22,24,26,28,30},{1,3,5,7,9,11,13,15,17,19,..., dimensions={0} | all-to-all | bytes 2097152 | tf_op jit(solution)/shard_map/all_to_all | solution.py:294
  164.4 2.3 %collective-permute-start.12 = (f32[128,512]{1,0:T(8,128)S(1)}, f32[128,512]{1,0:T(8,128)S(1)}, u32[]{:S(2)}, u32[]{:S(2)}) collective-permute-start(f32[128,512]{1,0:T(8,128)S(1)} %shard_map.105), channel_id=1, source_target_pairs={{0,1},{1,0},{2,3},{3,2},{4,5},{5,4},{6,7},{7,6},{8,9},{9,8},{10,11... | collective-permute-start | bytes 786440 | tf_op jit(solution)/shard_map/ppermute | solution.py:290
  168.0 3.7 %collective-permute-start.13 = (bf16[128,128]{1,0:T(8,128)(2,1)S(1)}, bf16[128,128]{1,0:T(8,128)(2,1)S(1)}, u32[]{:S(2)}, u32[]{:S(2)}) collective-permute-start(bf16[128,128]{1,0:T(8,128)(2,1)S(1)} %get-tuple-element.34.refs_0_.hid_ref.refs_5_), channel_id=1, source_target_pairs={{0,32},{32,64},{64,96},{1,33},{33,65},{65,97},{2,34},{34,66},{66,9... | collective-permute-start | bytes 98312 | tf_op jit(solution)/shard_map/ppermute | solution.py:316
  172.9 18.5 %all_to_all.40.refs_0_ = bf16[16,128,256]{2,1,0:T(8,128)(2,1)S(1)} all-to-all(bf16[16,128,256]{2,1,0:T(8,128)(2,1)S(1)} %shard_map.107), channel_id=1, replica_groups={{0,2,4,6,8,10,12,14,16,18,20,22,24,26,28,30},{1,3,5,7,9,11,13,15,17,19,..., dimensions={0} | all-to-all | bytes 2097152 | tf_op jit(solution)/shard_map/all_to_all | solution.py:294
  192.0 2.3 %collective-permute-start.14 = (f32[128,512]{1,0:T(8,128)S(1)}, f32[128,512]{1,0:T(8,128)S(1)}, u32[]{:S(2)}, u32[]{:S(2)}) collective-permute-start(f32[128,512]{1,0:T(8,128)S(1)} %shard_map.109), channel_id=1, source_target_pairs={{0,1},{1,0},{2,3},{3,2},{4,5},{5,4},{6,7},{7,6},{8,9},{9,8},{10,11... | collective-permute-start | bytes 786440 | tf_op jit(solution)/shard_map/ppermute | solution.py:290
  (47 shorter events, 18.6 us)
Async XLA Ops:
  3.8 24.2 %collective-permute-start = (bf16[16,128,512]{2,1,0:T(8,128)(2,1)}, bf16[16,128,512]{2,1,0:T(8,128)(2,1)}, u32[]{:S(2)}, u32[]{:S(2)}) collective-permute-start(bf16[16,128,512]{2,1,0:T(8,128)(2,1)} %shard_map.79), channel_id=1, source_target_pairs={{0,1},{1,0},{2,3},{3,2},{4,5},{5,4},{6,7},{7,6},{8,9},{9,8},{10,11... | collective-permute-start | bytes 6291464 | tf_op jit(solution)/shard_map/ppermute | solution.py:290
  5.2 3.3 %copy-start = (bf16[1,128,128]{2,1,0:T(8,128)(2,1)S(1)}, bf16[1,128,128]{2,1,0:T(8,128)(2,1)}, u32[]{:S(2)}) copy-start(bf16[1,128,128]{2,1,0:T(8,128)(2,1)} %param.10) | copy-start | bytes 98308
  8.4 19.5 %collective-permute-start.1 = (bf16[16,128,512]{2,1,0:T(8,128)(2,1)}, bf16[16,128,512]{2,1,0:T(8,128)(2,1)}, u32[]{:S(2)}, u32[]{:S(2)}) collective-permute-start(bf16[16,128,512]{2,1,0:T(8,128)(2,1)} %shard_map.80), channel_id=1, source_target_pairs={{0,1},{1,0},{2,3},{3,2},{4,5},{5,4},{6,7},{7,6},{8,9},{9,8},{10,11... | collective-permute-start | bytes 6291464 | tf_op jit(solution)/shard_map/ppermute | solution.py:290
  9.5 18.5 %all-to-all-start = ((bf16[16,128,128]{2,1,0:T(8,128)(2,1)}), bf16[16,128,128]{2,1,0:T(8,128)(2,1)S(1)}, u32[]{:S(2)}, u32[]{:S(2)}) async-start(bf16[16,128,128]{2,1,0:T(8,128)(2,1)} %shard_map.77), calls=%async_computation | async-start | bytes 1048576 | tf_op jit(solution)/shard_map/all_to_all | solution.py:294
  32.2 3.1 %collective-permute-start.2 = (f32[128,512]{1,0:T(8,128)S(1)}, f32[128,512]{1,0:T(8,128)S(1)}, u32[]{:S(2)}, u32[]{:S(2)}) collective-permute-start(f32[128,512]{1,0:T(8,128)S(1)} %shard_map.85), channel_id=1, source_target_pairs={{0,1},{1,0},{2,3},{3,2},{4,5},{5,4},{6,7},{7,6},{8,9},{9,8},{10,11... | collective-permute-start | bytes 786440 | tf_op jit(solution)/shard_map/ppermute | solution.py:290
  34.1 1.2 copy-start.1
  34.1 1.2 copy-start.2
  35.4 4.1 %collective-permute-start.3 = (bf16[128,128]{1,0:T(8,128)(2,1)S(1)}, bf16[128,128]{1,0:T(8,128)(2,1)S(1)}, u32[]{:S(2)}, u32[]{:S(2)}) collective-permute-start(bf16[128,128]{1,0:T(8,128)(2,1)S(1)} %get-tuple-element.24.refs_0_.hid_ref), channel_id=1, source_target_pairs={{0,32},{32,64},{64,96},{1,33},{33,65},{65,97},{2,34},{34,66},{66,9... | collective-permute-start | bytes 98312 | tf_op jit(solution)/shard_map/ppermute | solution.py:316
  53.7 3.6 %collective-permute-start.4 = (f32[128,512]{1,0:T(8,128)S(1)}, f32[128,512]{1,0:T(8,128)S(1)}, u32[]{:S(2)}, u32[]{:S(2)}) collective-permute-start(f32[128,512]{1,0:T(8,128)S(1)} %shard_map.89), channel_id=1, source_target_pairs={{0,1},{1,0},{2,3},{3,2},{4,5},{5,4},{6,7},{7,6},{8,9},{9,8},{10,11... | collective-permute-start | bytes 786440 | tf_op jit(solution)/shard_map/ppermute | solution.py:290
  57.3 4.7 %collective-permute-start.5 = (bf16[128,128]{1,0:T(8,128)(2,1)S(1)}, bf16[128,128]{1,0:T(8,128)(2,1)S(1)}, u32[]{:S(2)}, u32[]{:S(2)}) collective-permute-start(bf16[128,128]{1,0:T(8,128)(2,1)S(1)} %get-tuple-element.26.refs_0_.hid_ref.refs_1_), channel_id=1, source_target_pairs={{0,32},{32,64},{64,96},{1,33},{33,65},{65,97},{2,34},{34,66},{66,9... | collective-permute-start | bytes 98312 | tf_op jit(solution)/shard_map/ppermute | solution.py:316
  81.3 3.5 %collective-permute-start.6 = (f32[128,512]{1,0:T(8,128)S(1)}, f32[128,512]{1,0:T(8,128)S(1)}, u32[]{:S(2)}, u32[]{:S(2)}) collective-permute-start(f32[128,512]{1,0:T(8,128)S(1)} %shard_map.93), channel_id=1, source_target_pairs={{0,1},{1,0},{2,3},{3,2},{4,5},{5,4},{6,7},{7,6},{8,9},{9,8},{10,11... | collective-permute-start | bytes 786440 | tf_op jit(solution)/shard_map/ppermute | solution.py:290
  84.9 4.7 %collective-permute-start.7 = (bf16[128,128]{1,0:T(8,128)(2,1)S(1)}, bf16[128,128]{1,0:T(8,128)(2,1)S(1)}, u32[]{:S(2)}, u32[]{:S(2)}) collective-permute-start(bf16[128,128]{1,0:T(8,128)(2,1)S(1)} %get-tuple-element.28.refs_0_.hid_ref.refs_2_), channel_id=1, source_target_pairs={{0,32},{32,64},{64,96},{1,33},{33,65},{65,97},{2,34},{34,66},{66,9... | collective-permute-start | bytes 98312 | tf_op jit(solution)/shard_map/ppermute | solution.py:316
  109.0 3.7 %collective-permute-start.8 = (f32[128,512]{1,0:T(8,128)S(1)}, f32[128,512]{1,0:T(8,128)S(1)}, u32[]{:S(2)}, u32[]{:S(2)}) collective-permute-start(f32[128,512]{1,0:T(8,128)S(1)} %shard_map.97), channel_id=1, source_target_pairs={{0,1},{1,0},{2,3},{3,2},{4,5},{5,4},{6,7},{7,6},{8,9},{9,8},{10,11... | collective-permute-start | bytes 786440 | tf_op jit(solution)/shard_map/ppermute | solution.py:290
  112.7 4.7 %collective-permute-start.9 = (bf16[128,128]{1,0:T(8,128)(2,1)S(1)}, bf16[128,128]{1,0:T(8,128)(2,1)S(1)}, u32[]{:S(2)}, u32[]{:S(2)}) collective-permute-start(bf16[128,128]{1,0:T(8,128)(2,1)S(1)} %get-tuple-element.30.refs_0_.hid_ref.refs_3_), channel_id=1, source_target_pairs={{0,32},{32,64},{64,96},{1,33},{33,65},{65,97},{2,34},{34,66},{66,9... | collective-permute-start | bytes 98312 | tf_op jit(solution)/shard_map/ppermute | solution.py:316
  136.8 3.5 %collective-permute-start.10 = (f32[128,512]{1,0:T(8,128)S(1)}, f32[128,512]{1,0:T(8,128)S(1)}, u32[]{:S(2)}, u32[]{:S(2)}) collective-permute-start(f32[128,512]{1,0:T(8,128)S(1)} %shard_map.101), channel_id=1, source_target_pairs={{0,1},{1,0},{2,3},{3,2},{4,5},{5,4},{6,7},{7,6},{8,9},{9,8},{10,11... | collective-permute-start | bytes 786440 | tf_op jit(solution)/shard_map/ppermute | solution.py:290
  140.4 4.7 %collective-permute-start.11 = (bf16[128,128]{1,0:T(8,128)(2,1)S(1)}, bf16[128,128]{1,0:T(8,128)(2,1)S(1)}, u32[]{:S(2)}, u32[]{:S(2)}) collective-permute-start(bf16[128,128]{1,0:T(8,128)(2,1)S(1)} %get-tuple-element.32.refs_0_.hid_ref.refs_4_), channel_id=1, source_target_pairs={{0,32},{32,64},{64,96},{1,33},{33,65},{65,97},{2,34},{34,66},{66,9... | collective-permute-start | bytes 98312 | tf_op jit(solution)/shard_map/ppermute | solution.py:316
  164.4 3.5 %collective-permute-start.12 = (f32[128,512]{1,0:T(8,128)S(1)}, f32[128,512]{1,0:T(8,128)S(1)}, u32[]{:S(2)}, u32[]{:S(2)}) collective-permute-start(f32[128,512]{1,0:T(8,128)S(1)} %shard_map.105), channel_id=1, source_target_pairs={{0,1},{1,0},{2,3},{3,2},{4,5},{5,4},{6,7},{7,6},{8,9},{9,8},{10,11... | collective-permute-start | bytes 786440 | tf_op jit(solution)/shard_map/ppermute | solution.py:290
  168.0 4.8 %collective-permute-start.13 = (bf16[128,128]{1,0:T(8,128)(2,1)S(1)}, bf16[128,128]{1,0:T(8,128)(2,1)S(1)}, u32[]{:S(2)}, u32[]{:S(2)}) collective-permute-start(bf16[128,128]{1,0:T(8,128)(2,1)S(1)} %get-tuple-element.34.refs_0_.hid_ref.refs_5_), channel_id=1, source_target_pairs={{0,32},{32,64},{64,96},{1,33},{33,65},{65,97},{2,34},{34,66},{66,9... | collective-permute-start | bytes 98312 | tf_op jit(solution)/shard_map/ppermute | solution.py:316
  192.0 3.5 %collective-permute-start.14 = (f32[128,512]{1,0:T(8,128)S(1)}, f32[128,512]{1,0:T(8,128)S(1)}, u32[]{:S(2)}, u32[]{:S(2)}) collective-permute-start(f32[128,512]{1,0:T(8,128)S(1)} %shard_map.109), channel_id=1, source_target_pairs={{0,1},{1,0},{2,3},{3,2},{4,5},{5,4},{6,7},{7,6},{8,9},{9,8},{10,11... | collective-permute-start | bytes 786440 | tf_op jit(solution)/shard_map/ppermute | solution.py:290

commit v4 on v3

v4 whole, which is shorter than its diff:
```python
import functools

import jax
import jax.numpy as jnp
from jax import lax
from jax.experimental import pallas as pl
from jax.experimental.pallas import tpu as pltpu
from jax.sharding import PartitionSpec as P

VMEM = pl.BlockSpec(memory_space=pltpu.VMEM)
HBM = pl.BlockSpec(memory_space=pltpu.HBM)


def resident(x):
    return pltpu.with_memory_space_constraint(x, pltpu.VMEM)


def outside(x):
    return pltpu.with_memory_space_constraint(x, pltpu.HBM)


def limits(mib):
    return pltpu.CompilerParams(vmem_limit_bytes=mib << 20)


def own_side():
    return (lax.axis_index("col") & 1) == 0


def sort_kernel(away, in_ref, rec_ref, out_ref, natural, ordered, in_sems, out_sems):
    blocks, depth, wide = ordered.shape
    unit = natural.shape[2]
    gates = wide // unit
    rows = 2 * unit
    span = rows // gates
    to = lax.broadcasted_iota(jnp.int32, (rows, rows), 0)
    come = lax.broadcasted_iota(jnp.int32, (rows, rows), 1)
    order = come == gates * (to % span) + to // span
    order = order.astype(jnp.float32).astype(jnp.bfloat16)
    parts = in_sems.shape[0]
    size = blocks // parts
    from_input = own_side() if away else jnp.logical_not(own_side())

    def incoming(w_ref, part):
        chosen = pl.ds(part * size, size)
        return pltpu.make_async_copy(w_ref.at[chosen], natural.at[chosen], in_sems.at[part])

    def outgoing(part):
        chosen = pl.ds(part * size, size)
        return pltpu.make_async_copy(ordered.at[chosen], out_ref.at[chosen], out_sems.at[part])

    @pl.when(from_input)
    def _():
        for part in range(parts):
            incoming(in_ref, part).start()

    @pl.when(jnp.logical_not(from_input))
    def _():
        for part in range(parts):
            incoming(rec_ref, part).start()

    for part in range(parts):
        incoming(in_ref, part).wait()
        for j in range(part * size, (part + 1) * size):
            for q in range(0, depth // span, 2):
                both = jnp.concatenate(
                    [natural[j, (q + h) * rows : (q + h + 1) * rows, :] for h in range(2)], axis=1
                )
                moved = jnp.dot(order, both, preferred_element_type=jnp.float32)
                moved = moved.astype(jnp.bfloat16)
                for h in range(2):
                    at = (q + h) * span
                    for g in range(gates):
                        ordered[j, at : at + span, g * unit : (g + 1) * unit] = moved[
                            g * span : (g + 1) * span, h * unit : (h + 1) * unit
                        ]
        outgoing(part).start()
    for part in range(parts):
        outgoing(part).wait()


def sorted_weights(w_in, w_rec, blocks, away):
    gates, unit = w_in.shape[1:]
    depth = w_in.shape[0] // blocks
    wide = gates * unit
    parts = 4
    flat = (blocks, depth * gates, unit)
    return pl.pallas_call(
        functools.partial(sort_kernel, away),
        out_shape=pltpu.HBM((blocks, depth, wide), w_in.dtype),
        in_specs=[HBM, HBM],
        out_specs=HBM,
        scratch_shapes=[
            pltpu.VMEM(flat, w_in.dtype),
            pltpu.VMEM((blocks, depth, wide), w_in.dtype),
            pltpu.SemaphoreType.DMA((parts,)),
            pltpu.SemaphoreType.DMA((parts,)),
        ],
        cost_estimate=pl.CostEstimate(
            flops=4_000_000_000, bytes_accessed=4 * blocks * depth * wide, transcendentals=0
        ),
        compiler_params=limits(10),
    )(outside(w_in.reshape(flat)), outside(w_rec.reshape(flat)))


def fetch_kernel(count, *refs):
    sems = refs[-1]
    copies = [
        pltpu.make_async_copy(refs[i], refs[count + 1 + i], sems.at[i]) for i in range(count)
    ]
    for copy in copies:
        copy.start()
    for copy in copies:
        copy.wait()


def fetched(arrays, after):
    count = len(arrays)
    return pl.pallas_call(
        functools.partial(fetch_kernel, count),
        out_shape=tuple(jax.ShapeDtypeStruct(array.shape, array.dtype) for array in arrays),
        in_specs=[*[HBM] * count, pl.BlockSpec(memory_space=pl.ANY)],
        out_specs=tuple([VMEM] * count),
        scratch_shapes=[pltpu.SemaphoreType.DMA((count,))],
        compiler_params=limits(1),
    )(*[outside(array) for array in arrays], after)


def product_kernel(turn, fed, *refs):
    refs = list(refs)
    out_ref, w_ref = refs.pop(), refs.pop()
    x_ref = refs.pop() if fed else None
    blocks, depth, width = w_ref.shape
    bottom = jnp.logical_and(lax.axis_index("layer") == 0, jnp.logical_not(own_side()))

    def left(j):
        if len(refs) == 2:
            came = jnp.concatenate([refs[0][j], refs[1][j]], axis=1)
        else:
            came = refs[0][j]
        if fed:
            came = jnp.where(bottom, x_ref[turn, :, j * depth : (j + 1) * depth], came)
        return came

    wide = 256
    for n in range(width // wide):
        cols = slice(n * wide, (n + 1) * wide)
        total = None
        for j in range(blocks):
            term = jnp.dot(left(j), w_ref[j, :, cols], preferred_element_type=jnp.float32)
            total = term if total is None else total + term
        out_ref[:, cols] = total


def product(gathered, x, w, turn):
    blocks, depth, width = w.shape
    batch = gathered[0].shape[1]
    args = [*gathered, *([] if x is None else [x]), w]
    return pl.pallas_call(
        functools.partial(product_kernel, turn, x is not None),
        out_shape=jax.ShapeDtypeStruct((batch, width), jnp.float32),
        in_specs=[VMEM] * len(args),
        out_specs=VMEM,
        cost_estimate=pl.CostEstimate(
            flops=2 * blocks * depth * batch * width,
            bytes_accessed=2 * blocks * depth * (batch + width) + 4 * batch * width,
            transcendentals=0,
        ),
        compiler_params=limits(2),
    )(*[resident(arg) for arg in args])


def gates_kernel(turn, steps, layers, here_ref, came_ref, bias_ref, cell_ref, hid_ref, *refs):
    kept, (cell_out, hid_out) = refs[:-2], refs[-2:]
    unit = cell_ref.shape[1]
    layer = lax.axis_index("layer")
    valid = jnp.logical_and(turn >= layer, turn < layer + steps)

    def gate(k):
        cols = slice(k * unit, (k + 1) * unit)
        return here_ref[:, cols] + came_ref[:, cols] + bias_ref[k : k + 1, :]

    cell = cell_ref[...]
    cell_new = jax.nn.sigmoid(gate(1)) * cell + jax.nn.sigmoid(gate(0)) * jnp.tanh(gate(2))
    hidden_new = (jax.nn.sigmoid(gate(3)) * jnp.tanh(cell_new)).astype(hid_ref.dtype)
    hidden_new = jnp.where(valid, hidden_new, hid_ref[...])
    cell_out[...] = jnp.where(valid, cell_new, cell)
    if not kept:
        hid_out[...] = hidden_new
        return
    states = [*[ref[...] for ref in kept], hidden_new]
    for t in range(steps):
        value = states[t]
        for l in range(1, layers):
            value = jnp.where(layer == l, states[t + l], value)
        hid_out[t] = value


def gates(here, came, bias, cell, hidden, turn, steps, layers, kept=()):
    hid_shape = (steps, *hidden.shape) if kept else hidden.shape
    args = (here, came, bias, cell, hidden, *kept)
    return pl.pallas_call(
        functools.partial(gates_kernel, turn, steps, layers),
        out_shape=(
            jax.ShapeDtypeStruct(cell.shape, cell.dtype),
            jax.ShapeDtypeStruct(hid_shape, hidden.dtype),
        ),
        in_specs=[VMEM] * len(args),
        out_specs=(VMEM, VMEM),
        cost_estimate=pl.CostEstimate(
            flops=20 * cell.size, bytes_accessed=40 * cell.size, transcendentals=5 * cell.size
        ),
        compiler_params=limits(2),
    )(*[resident(arg) for arg in args])


def spread_kernel(*refs):
    out_ref = refs[-1]
    if len(refs) == 2:
        block = refs[0][...]
    else:
        hidden, first, second = (ref[...] for ref in refs[:3])
        block = jnp.concatenate(
            [jnp.where(own_side(), hidden, first), jnp.where(own_side(), first, second)], axis=1
        )
    for j in range(out_ref.shape[0]):
        out_ref[j] = block


def spread(parts, copies):
    batch, unit = parts[0].shape
    width = unit * (1 if len(parts) == 1 else 2)
    return pl.pallas_call(
        spread_kernel,
        out_shape=jax.ShapeDtypeStruct((copies, batch, width), parts[0].dtype),
        in_specs=[VMEM] * len(parts),
        out_specs=VMEM,
        cost_estimate=pl.CostEstimate(
            flops=batch * width, bytes_accessed=2 * copies * batch * width, transcendentals=0
        ),
        compiler_params=limits(2),
    )(*[resident(part) for part in parts])


def body(inputs, w_input, w_recur, bias, h_start, c_start):
    steps = inputs.shape[0]
    layers = lax.axis_size("layer")
    devices = lax.axis_size("col")
    chips = devices // 2
    turns = steps + layers - 1
    same_core = [[2 * chip + side for chip in range(chips)] for side in range(2)]
    partners = [(i, i ^ 1) for i in range(devices)]
    chip_bases = [(l, l * devices + 2 * chip) for l in range(layers) for chip in range(chips)]
    beside = [(base + 1, base) for _, base in chip_bases]
    upward = [(base, base + devices + 1) for l, base in chip_bases if l + 1 < layers]
    upward_too = [(base + 1, base + devices + 1) for l, base in chip_bases if l + 1 < layers]

    def across(x):
        return lax.ppermute(x, "col", partners)

    def gathered(*parts):
        copies = spread(parts, chips)
        return lax.all_to_all(copies, "col", 0, 0, tiled=True, axis_index_groups=same_core)

    cell = c_start[0]
    hidden = h_start[0]
    start = gathered(hidden)
    given = across(sorted_weights(w_input[0], w_recur[0], chips, True))
    w_here = sorted_weights(w_input[0], w_recur[0], chips, False)
    (w_there,) = fetched((given,), start)

    kept = []
    blocks = (start, across(start))
    for turn in range(turns):
        fed = inputs if turn < steps else None
        came = across(product(blocks, fed, w_there, turn))
        here = product(blocks, fed, w_here, turn)
        last = tuple(kept) if turn + 1 == turns else ()
        cell, hidden = gates(here, came, bias[0], cell, hidden, turn, steps, layers, last)
        kept.append(hidden)
        if turn + 1 < turns:
            first = lax.ppermute(hidden, ("layer", "col"), beside + upward)
            second = lax.ppermute(hidden, ("layer", "col"), upward_too)
            blocks = (gathered(hidden, first, second),)
    return hidden[None], cell[None]


def solution(mesh):
    in_specs = (
        P(),
        P("layer", None, None, "col"),
        P("layer", None, None, "col"),
        P("layer", None, "col"),
        P("layer", None, "col"),
        P("layer", None, "col"),
    )
    out_specs = (P("layer", None, None, "col"), P("layer", None, "col"))
    return jax.shard_map(body, mesh=mesh, in_specs=in_specs, out_specs=out_specs, check_vma=False)
```

time: 198 us -> 212 us (1.071)
  blocking collectives: 106 us -> 138 us
  starting transfers between devices: 47.5 us -> 36 us
  Pallas kernels: 31.3 us -> 22.4 us
  local copies, waits for them, and re-layouts: 0.01 us -> 5.13 us
  waiting for transfers between devices: 11.6 us -> 8.63 us
    all_to_all x6 -> x7, blocking collectives: 106 us -> 138 us  [gathered(): lax.all_to_all(copies, 'col', 0, 0, tiled=True, axis_index_groups=same_core)]
    ppermute x9, starting transfers between devices: 17.9 us -> 8.63 us  [across(): return lax.ppermute(x, 'col', partners)]
    all_to_all x1 -> x0, starting transfers between devices: 7.88 us -> none  [gathered(): lax.all_to_all(copies, 'col', 0, 0, tiled=True, axis_index_groups=same_core)]
    pallas_call x34 -> x30, Pallas kernels: 27.8 us -> 20.2 us  [the longest x14 10.3 us: product(): pl.pallas_call(functools.partial(product_kernel, turn, x is not None), ou...]
    ppermute x6 -> x12, starting transfers between devices: 21.7 us -> 27.4 us  [the longest x6 15.3 us: body(): second = lax.ppermute(hidden, ('layer', 'col'), upward_too)]
    unnamed x6 -> x14, local copies, waits for them, and re-layouts: 0.01 us -> 5.13 us
    all_to_all x1 -> x0, waiting for transfers between devices: 2.44 us -> none  [gathered(): lax.all_to_all(copies, 'col', 0, 0, tiled=True, axis_index_groups=same_core)]
    ppermute x6 -> x12, waiting for transfers between devices: 6.03 us -> 5.82 us  [the longest x6 4.97 us: body(): second = lax.ppermute(hidden, ('layer', 'col'), upward_too)]
  transfers between devices with their start and end apart: 16 -> 21, of which waited for: 14 -> 11; matrix products, arithmetic and copies ran while one was open for 0% -> 0% of each run, Pallas kernels for 9% -> 5%
where the time goes in v4:
time: 212 us; the launch traced here: 211 us
  blocking collectives  138 us (65%)
  starting transfers between devices  36 us (17%)
  Pallas kernels  22.4 us (11%)
  waiting for transfers between devices  8.63 us (4%)
  local copies, waits for them, and re-layouts  5.13 us (2%)
    all_to_all x7, blocking collectives, gathered(): lax.all_to_all(copies, 'col', 0, 0, tiled=True, axis_index_groups=same_core)  138 us
    ppermute x6, starting transfers between devices, body(): second = lax.ppermute(hidden, ('layer', 'col'), upward_too)  15.3 us
    ppermute x6, starting transfers between devices, body(): first = lax.ppermute(hidden, ('layer', 'col'), beside + upward)  12.1 us
    pallas_call x14, Pallas kernels, product(): pl.pallas_call(functools.partial(product_kernel, turn, x is not None), ou...  10.3 us
    ppermute x9, starting transfers between devices, across(): return lax.ppermute(x, 'col', partners)  8.63 us
    pallas_call x2, Pallas kernels, sorted_weights(): pl.pallas_call(functools.partial(sort_kernel, away), out_shape=pltpu.HBM(...  8.11 us
    unnamed x14, local copies, waits for them, and re-layouts  5.13 us
    ppermute x6, waiting for transfers between devices, body(): second = lax.ppermute(hidden, ('layer', 'col'), upward_too)  4.97 us
  transfers between devices with their start and end apart: 21, of which 11 were waited for; matrix products, arithmetic and copies ran while one was open for 0% of the time, Pallas kernels for 5%

profile of v4, /device:TPU:1, one launch (start us, length us, event | category | flops | bytes accessed | tf_op | source)
XLA Modules:
  0.0 211.2 jit_solution(14482517144719470887)
XLA Ops:
  0.6 4.1 %shard_map.80 = bf16[16,256,512]{2,1,0:T(8,128)(2,1)} custom-call(bf16[16,1024,128]{2,1,0:T(8,128)(2,1)} %bitcast.17, bf16[16,1024,128]{2,1,0:T(8,128)(2,1)} %bitcast.19), custom_call_target="tpu_custom_call" | custom-call | flops 4000000000 | bytes 8388608 | tf_op jit(solution)/shard_map/pallas_call | solution.py:88
  4.7 1.5 collective-permute-start.1
  6.3 18.7 %all_to_all.35.refs_0_.refs_1_ = bf16[16,128,128]{2,1,0:T(8,128)(2,1)S(1)} all-to-all(bf16[16,128,128]{2,1,0:T(8,128)(2,1)S(1)} %shard_map.77), channel_id=1, replica_groups={{0,2,4,6,8,10,12,14,16,18,20,22,24,26,28,30},{1,3,5,7,9,11,13,15,17,19,..., dimensions={0} | all-to-all | bytes 1048576 | tf_op jit(solution)/shard_map/all_to_all | solution.py:263
  25.0 1.5 collective-permute-start
  26.4 2.0 copy-done.6
  28.4 2.2 %shard_map.81.refs_3_.refs_2_.refs_1_ = bf16[16,256,512]{2,1,0:T(8,128)(2,1)S(1)} custom-call(bf16[16,256,512]{2,1,0:T(8,128)(2,1)} %copy-done.6, bf16[16,128,128]{2,1,0:T(8,128)(2,1)S(1)} %all_to_all.35.refs_0_.refs_1_), custom_call_target="tpu_custom_call" | custom-call | tf_op jit(solution)/shard_map/pallas_call | solution.py:119
  32.3 4.1 %shard_map.78.refs_3_.refs_2_.refs_1_ = bf16[16,256,512]{2,1,0:T(8,128)(2,1)} custom-call(bf16[16,1024,128]{2,1,0:T(8,128)(2,1)} %bitcast.18, bf16[16,1024,128]{2,1,0:T(8,128)(2,1)} %bitcast.20), custom_call_target="tpu_custom_call" | custom-call | flops 4000000000 | bytes 8388608 | tf_op jit(solution)/shard_map/pallas_call | solution.py:88
  36.4 2.2 %copy-done.1 = bf16[16,256,512]{2,1,0:T(8,128)(2,1)S(1)} copy-done((bf16[16,256,512]{2,1,0:T(8,128)(2,1)S(1)}, bf16[16,256,512]{2,1,0:T(8,128)(2,1)}, u32[]{:S(2)}) %copy-start.1) | copy-done | bytes 4194328
  39.5 1.9 collective-permute-start.3
  41.4 3.1 %collective-permute-start.4 = (bf16[128,128]{1,0:T(8,128)(2,1)S(1)}, bf16[128,128]{1,0:T(8,128)(2,1)S(1)}, u32[]{:S(2)}, u32[]{:S(2)}) collective-permute-start(bf16[128,128]{1,0:T(8,128)(2,1)S(1)} %get-tuple-element.16.refs_0_.hid_ref), channel_id=1, source_target_pairs={{1,33},{3,35},{5,37},{7,39},{9,41},{11,43},{13,45},{15,47},{17,49}... | collective-permute-start | bytes 98312 | tf_op jit(solution)/shard_map/ppermute | solution.py:283
  44.5 1.0 collective-permute-done.4.refs_2_
  45.6 20.0 %all_to_all.36.refs_0_ = bf16[16,128,256]{2,1,0:T(8,128)(2,1)S(1)} all-to-all(bf16[16,128,256]{2,1,0:T(8,128)(2,1)S(1)} %shard_map.84), channel_id=1, replica_groups={{0,2,4,6,8,10,12,14,16,18,20,22,24,26,28,30},{1,3,5,7,9,11,13,15,17,19,..., dimensions={0} | all-to-all | bytes 2097152 | tf_op jit(solution)/shard_map/all_to_all | solution.py:263
  68.6 2.3 %collective-permute-start.6 = (bf16[128,128]{1,0:T(8,128)(2,1)S(1)}, bf16[128,128]{1,0:T(8,128)(2,1)S(1)}, u32[]{:S(2)}, u32[]{:S(2)}) collective-permute-start(bf16[128,128]{1,0:T(8,128)(2,1)S(1)} %get-tuple-element.18.refs_0_.hid_ref.refs_1_), channel_id=1, source_target_pairs={{1,0},{3,2},{5,4},{7,6},{9,8},{11,10},{13,12},{15,14},{17,16},{19,... | collective-permute-start | bytes 98312 | tf_op jit(solution)/shard_map/ppermute | solution.py:282
  70.9 2.6 %collective-permute-start.7 = (bf16[128,128]{1,0:T(8,128)(2,1)S(1)}, bf16[128,128]{1,0:T(8,128)(2,1)S(1)}, u32[]{:S(2)}, u32[]{:S(2)}) collective-permute-start(bf16[128,128]{1,0:T(8,128)(2,1)S(1)} %get-tuple-element.18.refs_0_.hid_ref.refs_1_), channel_id=1, source_target_pairs={{1,33},{3,35},{5,37},{7,39},{9,41},{11,43},{13,45},{15,47},{17,49}... | collective-permute-start | bytes 98312 | tf_op jit(solution)/shard_map/ppermute | solution.py:283
  73.5 1.0 collective-permute-done.7.refs_2_
  74.6 19.8 %all_to_all.37.refs_0_ = bf16[16,128,256]{2,1,0:T(8,128)(2,1)S(1)} all-to-all(bf16[16,128,256]{2,1,0:T(8,128)(2,1)S(1)} %shard_map.88), channel_id=1, replica_groups={{0,2,4,6,8,10,12,14,16,18,20,22,24,26,28,30},{1,3,5,7,9,11,13,15,17,19,..., dimensions={0} | all-to-all | bytes 2097152 | tf_op jit(solution)/shard_map/all_to_all | solution.py:263
  96.9 2.8 %collective-permute-start.10 = (bf16[128,128]{1,0:T(8,128)(2,1)S(1)}, bf16[128,128]{1,0:T(8,128)(2,1)S(1)}, u32[]{:S(2)}, u32[]{:S(2)}) collective-permute-start(bf16[128,128]{1,0:T(8,128)(2,1)S(1)} %get-tuple-element.20.refs_0_.hid_ref.refs_2_), channel_id=1, source_target_pairs={{1,33},{3,35},{5,37},{7,39},{9,41},{11,43},{13,45},{15,47},{17,49}... | collective-permute-start | bytes 98312 | tf_op jit(solution)/shard_map/ppermute | solution.py:283
  99.7 1.3 collective-permute-start.9
  102.0 18.0 %all_to_all.38.refs_0_ = bf16[16,128,256]{2,1,0:T(8,128)(2,1)S(1)} all-to-all(bf16[16,128,256]{2,1,0:T(8,128)(2,1)S(1)} %shard_map.92), channel_id=1, replica_groups={{0,2,4,6,8,10,12,14,16,18,20,22,24,26,28,30},{1,3,5,7,9,11,13,15,17,19,..., dimensions={0} | all-to-all | bytes 2097152 | tf_op jit(solution)/shard_map/all_to_all | solution.py:263
  120.8 3.0 %collective-permute-start.11 = (f32[128,512]{1,0:T(8,128)S(1)}, f32[128,512]{1,0:T(8,128)S(1)}, u32[]{:S(2)}, u32[]{:S(2)}) collective-permute-start(f32[128,512]{1,0:T(8,128)S(1)} %shard_map.94), channel_id=1, source_target_pairs={{0,1},{1,0},{2,3},{3,2},{4,5},{5,4},{6,7},{7,6},{8,9},{9,8},{10,11... | collective-permute-start | bytes 786440 | tf_op jit(solution)/shard_map/ppermute | solution.py:259
  125.0 2.3 %collective-permute-start.12 = (bf16[128,128]{1,0:T(8,128)(2,1)S(1)}, bf16[128,128]{1,0:T(8,128)(2,1)S(1)}, u32[]{:S(2)}, u32[]{:S(2)}) collective-permute-start(bf16[128,128]{1,0:T(8,128)(2,1)S(1)} %get-tuple-element.22.refs_0_.hid_ref.refs_3_), channel_id=1, source_target_pairs={{1,0},{3,2},{5,4},{7,6},{9,8},{11,10},{13,12},{15,14},{17,16},{19,... | collective-permute-start | bytes 98312 | tf_op jit(solution)/shard_map/ppermute | solution.py:282
  127.3 3.6 %collective-permute-start.13 = (bf16[128,128]{1,0:T(8,128)(2,1)S(1)}, bf16[128,128]{1,0:T(8,128)(2,1)S(1)}, u32[]{:S(2)}, u32[]{:S(2)}) collective-permute-start(bf16[128,128]{1,0:T(8,128)(2,1)S(1)} %get-tuple-element.22.refs_0_.hid_ref.refs_3_), channel_id=1, source_target_pairs={{1,33},{3,35},{5,37},{7,39},{9,41},{11,43},{13,45},{15,47},{17,49}... | collective-permute-start | bytes 98312 | tf_op jit(solution)/shard_map/ppermute | solution.py:283
  130.9 1.0 collective-permute-done.13.refs_2_
  132.1 19.8 %all_to_all.39.refs_0_ = bf16[16,128,256]{2,1,0:T(8,128)(2,1)S(1)} all-to-all(bf16[16,128,256]{2,1,0:T(8,128)(2,1)S(1)} %shard_map.96), channel_id=1, replica_groups={{0,2,4,6,8,10,12,14,16,18,20,22,24,26,28,30},{1,3,5,7,9,11,13,15,17,19,..., dimensions={0} | all-to-all | bytes 2097152 | tf_op jit(solution)/shard_map/all_to_all | solution.py:263
  154.3 2.0 collective-permute-start.15
  156.3 1.9 collective-permute-start.16
  158.3 1.0 collective-permute-done.16.refs_2_
  159.4 20.2 %all_to_all.40.refs_0_ = bf16[16,128,256]{2,1,0:T(8,128)(2,1)S(1)} all-to-all(bf16[16,128,256]{2,1,0:T(8,128)(2,1)S(1)} %shard_map.100), channel_id=1, replica_groups={{0,2,4,6,8,10,12,14,16,18,20,22,24,26,28,30},{1,3,5,7,9,11,13,15,17,19,..., dimensions={0} | all-to-all | bytes 2097152 | tf_op jit(solution)/shard_map/all_to_all | solution.py:263
  182.0 2.3 %collective-permute-start.18 = (bf16[128,128]{1,0:T(8,128)(2,1)S(1)}, bf16[128,128]{1,0:T(8,128)(2,1)S(1)}, u32[]{:S(2)}, u32[]{:S(2)}) collective-permute-start(bf16[128,128]{1,0:T(8,128)(2,1)S(1)} %get-tuple-element.26.refs_0_.hid_ref.refs_5_), channel_id=1, source_target_pairs={{1,0},{3,2},{5,4},{7,6},{9,8},{11,10},{13,12},{15,14},{17,16},{19,... | collective-permute-start | bytes 98312 | tf_op jit(solution)/shard_map/ppermute | solution.py:282
  184.3 1.3 collective-permute-start.19
  185.6 1.0 collective-permute-done.19.refs_2_
  186.7 21.3 %all_to_all.41.refs_0_ = bf16[16,128,256]{2,1,0:T(8,128)(2,1)S(1)} all-to-all(bf16[16,128,256]{2,1,0:T(8,128)(2,1)S(1)} %shard_map.104), channel_id=1, replica_groups={{0,2,4,6,8,10,12,14,16,18,20,22,24,26,28,30},{1,3,5,7,9,11,13,15,17,19,..., dimensions={0} | all-to-all | bytes 2097152 | tf_op jit(solution)/shard_map/all_to_all | solution.py:263
  (62 shorter events, 19.5 us)
Async XLA Ops:
  0.6 5.5 %copy-start.3 = (bf16[1,128,128]{2,1,0:T(8,128)(2,1)S(1)}, bf16[1,128,128]{2,1,0:T(8,128)(2,1)}, u32[]{:S(2)}) copy-start(bf16[1,128,128]{2,1,0:T(8,128)(2,1)} %param.10) | copy-start | bytes 98308
  4.7 21.7 %collective-permute-start.1 = (bf16[16,256,512]{2,1,0:T(8,128)(2,1)}, bf16[16,256,512]{2,1,0:T(8,128)(2,1)S(1)}, u32[]{:S(2)}, u32[]{:S(2)}) collective-permute-start(bf16[16,256,512]{2,1,0:T(8,128)(2,1)} %shard_map.80), channel_id=1, source_target_pairs={{0,1},{1,0},{2,3},{3,2},{4,5},{5,4},{6,7},{7,6},{8,9},{9,8},{10,11... | collective-permute-start | bytes 12582920 | tf_op jit(solution)/shard_map/ppermute | solution.py:259
  25.0 5.6 %copy-start = (bf16[4,128,4096]{2,1,0:T(8,128)(2,1)S(1)}, bf16[4,128,4096]{2,1,0:T(8,128)(2,1)}, u32[]{:S(2)}) copy-start(bf16[4,128,4096]{2,1,0:T(8,128)(2,1)} %refs_1_.11) | copy-start | bytes 12582916
  25.0 5.6 %collective-permute-start = (bf16[16,128,128]{2,1,0:T(8,128)(2,1)S(1)}, bf16[16,128,128]{2,1,0:T(8,128)(2,1)S(1)}, u32[]{:S(2)}, u32[]{:S(2)}) collective-permute-start(bf16[16,128,128]{2,1,0:T(8,128)(2,1)S(1)} %all_to_all.35.refs_0_.refs_1_), channel_id=1, source_target_pairs={{0,1},{1,0},{2,3},{3,2},{4,5},{5,4},{6,7},{7,6},{8,9},{9,8},{10,11... | collective-permute-start | bytes 1572872 | tf_op jit(solution)/shard_map/ppermute | solution.py:259
  26.4 2.0 copy-start.6
  31.4 7.8 %collective-permute-start.2 = (f32[128,512]{1,0:T(8,128)S(1)}, f32[128,512]{1,0:T(8,128)S(1)}, u32[]{:S(2)}, u32[]{:S(2)}) collective-permute-start(f32[128,512]{1,0:T(8,128)S(1)} %shard_map.82), channel_id=1, source_target_pairs={{0,1},{1,0},{2,3},{3,2},{4,5},{5,4},{6,7},{7,6},{8,9},{9,8},{10,11... | collective-permute-start | bytes 786440 | tf_op jit(solution)/shard_map/ppermute | solution.py:259
  36.3 2.2 %copy-start.1 = (bf16[16,256,512]{2,1,0:T(8,128)(2,1)S(1)}, bf16[16,256,512]{2,1,0:T(8,128)(2,1)}, u32[]{:S(2)}) copy-start(bf16[16,256,512]{2,1,0:T(8,128)(2,1)} %shard_map.78.refs_3_.refs_2_.refs_1_) | copy-start | bytes 12582916
  38.5 0.7 copy-start.4
  38.5 0.9 copy-start.5
  39.5 5.1 %collective-permute-start.3 = (bf16[128,128]{1,0:T(8,128)(2,1)S(1)}, bf16[128,128]{1,0:T(8,128)(2,1)S(1)}, u32[]{:S(2)}, u32[]{:S(2)}) collective-permute-start(bf16[128,128]{1,0:T(8,128)(2,1)S(1)} %get-tuple-element.16.refs_0_.hid_ref), channel_id=1, source_target_pairs={{1,0},{3,2},{5,4},{7,6},{9,8},{11,10},{13,12},{15,14},{17,16},{19,... | collective-permute-start | bytes 98312 | tf_op jit(solution)/shard_map/ppermute | solution.py:282
  41.4 4.1 %collective-permute-start.4 = (bf16[128,128]{1,0:T(8,128)(2,1)S(1)}, bf16[128,128]{1,0:T(8,128)(2,1)S(1)}, u32[]{:S(2)}, u32[]{:S(2)}) collective-permute-start(bf16[128,128]{1,0:T(8,128)(2,1)S(1)} %get-tuple-element.16.refs_0_.hid_ref), channel_id=1, source_target_pairs={{1,33},{3,35},{5,37},{7,39},{9,41},{11,43},{13,45},{15,47},{17,49}... | collective-permute-start | bytes 98312 | tf_op jit(solution)/shard_map/ppermute | solution.py:283
  65.6 2.2 %copy-start.2 = (bf16[16,256,512]{2,1,0:T(8,128)(2,1)S(1)}, bf16[16,256,512]{2,1,0:T(8,128)(2,1)}, u32[]{:S(2)}) copy-start(bf16[16,256,512]{2,1,0:T(8,128)(2,1)} %shard_map.78.refs_3_.refs_2_.refs_1_) | copy-start | bytes 12582916
  66.5 2.0 collective-permute-start.5
  68.6 4.9 %collective-permute-start.6 = (bf16[128,128]{1,0:T(8,128)(2,1)S(1)}, bf16[128,128]{1,0:T(8,128)(2,1)S(1)}, u32[]{:S(2)}, u32[]{:S(2)}) collective-permute-start(bf16[128,128]{1,0:T(8,128)(2,1)S(1)} %get-tuple-element.18.refs_0_.hid_ref.refs_1_), channel_id=1, source_target_pairs={{1,0},{3,2},{5,4},{7,6},{9,8},{11,10},{13,12},{15,14},{17,16},{19,... | collective-permute-start | bytes 98312 | tf_op jit(solution)/shard_map/ppermute | solution.py:282
  70.9 3.6 %collective-permute-start.7 = (bf16[128,128]{1,0:T(8,128)(2,1)S(1)}, bf16[128,128]{1,0:T(8,128)(2,1)S(1)}, u32[]{:S(2)}, u32[]{:S(2)}) collective-permute-start(bf16[128,128]{1,0:T(8,128)(2,1)S(1)} %get-tuple-element.18.refs_0_.hid_ref.refs_1_), channel_id=1, source_target_pairs={{1,33},{3,35},{5,37},{7,39},{9,41},{11,43},{13,45},{15,47},{17,49}... | collective-permute-start | bytes 98312 | tf_op jit(solution)/shard_map/ppermute | solution.py:283
  95.2 1.6 collective-permute-start.8
  96.9 4.1 %collective-permute-start.10 = (bf16[128,128]{1,0:T(8,128)(2,1)S(1)}, bf16[128,128]{1,0:T(8,128)(2,1)S(1)}, u32[]{:S(2)}, u32[]{:S(2)}) collective-permute-start(bf16[128,128]{1,0:T(8,128)(2,1)S(1)} %get-tuple-element.20.refs_0_.hid_ref.refs_2_), channel_id=1, source_target_pairs={{1,33},{3,35},{5,37},{7,39},{9,41},{11,43},{13,45},{15,47},{17,49}... | collective-permute-start | bytes 98312 | tf_op jit(solution)/shard_map/ppermute | solution.py:283
  99.7 2.1 %collective-permute-start.9 = (bf16[128,128]{1,0:T(8,128)(2,1)S(1)}, bf16[128,128]{1,0:T(8,128)(2,1)S(1)}, u32[]{:S(2)}, u32[]{:S(2)}) collective-permute-start(bf16[128,128]{1,0:T(8,128)(2,1)S(1)} %get-tuple-element.20.refs_0_.hid_ref.refs_2_), channel_id=1, source_target_pairs={{1,0},{3,2},{5,4},{7,6},{9,8},{11,10},{13,12},{15,14},{17,16},{19,... | collective-permute-start | bytes 98312 | tf_op jit(solution)/shard_map/ppermute | solution.py:282
  120.8 4.2 %collective-permute-start.11 = (f32[128,512]{1,0:T(8,128)S(1)}, f32[128,512]{1,0:T(8,128)S(1)}, u32[]{:S(2)}, u32[]{:S(2)}) collective-permute-start(f32[128,512]{1,0:T(8,128)S(1)} %shard_map.94), channel_id=1, source_target_pairs={{0,1},{1,0},{2,3},{3,2},{4,5},{5,4},{6,7},{7,6},{8,9},{9,8},{10,11... | collective-permute-start | bytes 786440 | tf_op jit(solution)/shard_map/ppermute | solution.py:259
  125.0 5.9 %collective-permute-start.12 = (bf16[128,128]{1,0:T(8,128)(2,1)S(1)}, bf16[128,128]{1,0:T(8,128)(2,1)S(1)}, u32[]{:S(2)}, u32[]{:S(2)}) collective-permute-start(bf16[128,128]{1,0:T(8,128)(2,1)S(1)} %get-tuple-element.22.refs_0_.hid_ref.refs_3_), channel_id=1, source_target_pairs={{1,0},{3,2},{5,4},{7,6},{9,8},{11,10},{13,12},{15,14},{17,16},{19,... | collective-permute-start | bytes 98312 | tf_op jit(solution)/shard_map/ppermute | solution.py:282
  127.3 4.6 %collective-permute-start.13 = (bf16[128,128]{1,0:T(8,128)(2,1)S(1)}, bf16[128,128]{1,0:T(8,128)(2,1)S(1)}, u32[]{:S(2)}, u32[]{:S(2)}) collective-permute-start(bf16[128,128]{1,0:T(8,128)(2,1)S(1)} %get-tuple-element.22.refs_0_.hid_ref.refs_3_), channel_id=1, source_target_pairs={{1,33},{3,35},{5,37},{7,39},{9,41},{11,43},{13,45},{15,47},{17,49}... | collective-permute-start | bytes 98312 | tf_op jit(solution)/shard_map/ppermute | solution.py:283
  152.6 1.6 collective-permute-start.14
  154.3 4.0 %collective-permute-start.15 = (bf16[128,128]{1,0:T(8,128)(2,1)S(1)}, bf16[128,128]{1,0:T(8,128)(2,1)S(1)}, u32[]{:S(2)}, u32[]{:S(2)}) collective-permute-start(bf16[128,128]{1,0:T(8,128)(2,1)S(1)} %get-tuple-element.24.refs_0_.hid_ref.refs_4_), channel_id=1, source_target_pairs={{1,0},{3,2},{5,4},{7,6},{9,8},{11,10},{13,12},{15,14},{17,16},{19,... | collective-permute-start | bytes 98312 | tf_op jit(solution)/shard_map/ppermute | solution.py:282
  156.3 3.0 %collective-permute-start.16 = (bf16[128,128]{1,0:T(8,128)(2,1)S(1)}, bf16[128,128]{1,0:T(8,128)(2,1)S(1)}, u32[]{:S(2)}, u32[]{:S(2)}) collective-permute-start(bf16[128,128]{1,0:T(8,128)(2,1)S(1)} %get-tuple-element.24.refs_0_.hid_ref.refs_4_), channel_id=1, source_target_pairs={{1,33},{3,35},{5,37},{7,39},{9,41},{11,43},{13,45},{15,47},{17,49}... | collective-permute-start | bytes 98312 | tf_op jit(solution)/shard_map/ppermute | solution.py:283
  180.3 1.6 collective-permute-start.17
  182.0 3.6 %collective-permute-start.18 = (bf16[128,128]{1,0:T(8,128)(2,1)S(1)}, bf16[128,128]{1,0:T(8,128)(2,1)S(1)}, u32[]{:S(2)}, u32[]{:S(2)}) collective-permute-start(bf16[128,128]{1,0:T(8,128)(2,1)S(1)} %get-tuple-element.26.refs_0_.hid_ref.refs_5_), channel_id=1, source_target_pairs={{1,0},{3,2},{5,4},{7,6},{9,8},{11,10},{13,12},{15,14},{17,16},{19,... | collective-permute-start | bytes 98312 | tf_op jit(solution)/shard_map/ppermute | solution.py:282
  184.3 2.3 %collective-permute-start.19 = (bf16[128,128]{1,0:T(8,128)(2,1)S(1)}, bf16[128,128]{1,0:T(8,128)(2,1)S(1)}, u32[]{:S(2)}, u32[]{:S(2)}) collective-permute-start(bf16[128,128]{1,0:T(8,128)(2,1)S(1)} %get-tuple-element.26.refs_0_.hid_ref.refs_5_), channel_id=1, source_target_pairs={{1,33},{3,35},{5,37},{7,39},{9,41},{11,43},{13,45},{15,47},{17,49}... | collective-permute-start | bytes 98312 | tf_op jit(solution)/shard_map/ppermute | solution.py:283
  208.8 1.7 collective-permute-start.20

commit v5 on v3

v5 whole, which is shorter than its diff:
```python
import functools

import jax
import jax.numpy as jnp
from jax import lax
from jax.experimental import pallas as pl
from jax.experimental.pallas import tpu as pltpu
from jax.sharding import PartitionSpec as P

VMEM = pl.BlockSpec(memory_space=pltpu.VMEM)
HBM = pl.BlockSpec(memory_space=pltpu.HBM)


def resident(x):
    return pltpu.with_memory_space_constraint(x, pltpu.VMEM)


def outside(x):
    return pltpu.with_memory_space_constraint(x, pltpu.HBM)


def limits(mib):
    return pltpu.CompilerParams(vmem_limit_bytes=mib << 20)


def sort_kernel(w_ref, keep_ref, away_ref, natural, ordered, in_sems, out_sems):
    blocks, _, depth, wide = ordered.shape
    unit = natural.shape[3]
    gates = wide // unit
    half = depth // 2
    rows = half * gates
    core = lax.axis_index("col") & 1
    to = lax.broadcasted_iota(jnp.int32, (rows, rows), 0)
    come = lax.broadcasted_iota(jnp.int32, (rows, rows), 1)
    order = come == gates * (to % half) + to // half
    order = order.astype(jnp.float32).astype(jnp.bfloat16)
    parts = in_sems.shape[0]
    size = blocks // parts

    def incoming(part):
        chosen = pl.ds(part * size, size)
        return pltpu.make_async_copy(w_ref.at[chosen], natural.at[chosen], in_sems.at[part])

    def outgoing(part, away):
        chosen = pl.ds(part * size, size)
        side = 1 - core if away else core
        return pltpu.make_async_copy(
            ordered.at[chosen, side],
            (away_ref if away else keep_ref).at[chosen],
            out_sems.at[part, away],
        )

    for part in range(parts):
        incoming(part).start()
    for part in range(parts):
        incoming(part).wait()
        for j in range(part * size, (part + 1) * size):
            for side in range(2):
                both = jnp.concatenate(
                    [natural[j, side, :rows, :], natural[j, side, rows:, :]], axis=1
                )
                moved = jnp.dot(order, both, preferred_element_type=jnp.float32)
                moved = moved.astype(jnp.bfloat16)
                for h in range(2):
                    for g in range(gates):
                        ordered[j, side, h * half : (h + 1) * half, g * unit : (g + 1) * unit] = (
                            moved[g * half : (g + 1) * half, h * unit : (h + 1) * unit]
                        )
        for away in range(2):
            outgoing(part, away).start()
    for part in range(parts):
        for away in range(2):
            outgoing(part, away).wait()


def sorted_weights(w, blocks):
    gates, unit = w.shape[1:]
    depth = w.shape[0] // (2 * blocks)
    wide = gates * unit
    parts = 4
    return pl.pallas_call(
        sort_kernel,
        out_shape=tuple([pltpu.HBM((blocks, depth, wide), w.dtype)] * 2),
        in_specs=[HBM],
        out_specs=(HBM, HBM),
        scratch_shapes=[
            pltpu.VMEM((blocks, 2, depth * gates, unit), w.dtype),
            pltpu.VMEM((blocks, 2, depth, wide), w.dtype),
            pltpu.SemaphoreType.DMA((parts,)),
            pltpu.SemaphoreType.DMA((parts, 2)),
        ],
        cost_estimate=pl.CostEstimate(
            flops=4_000_000_000, bytes_accessed=8 * blocks * depth * wide, transcendentals=0
        ),
        compiler_params=limits(10),
    )(outside(w.reshape(blocks, 2, depth * gates, unit)))


def block_of(x_ref, turn, j, side, unit):
    at = pl.multiple_of((2 * j + side) * unit, unit)
    return x_ref[turn, :, pl.ds(at, unit)]


def first_kernel(own_ref, other_ref, x_ref, *refs):
    weights, (out_ref, *kept), (*away, x_held, sems, x_sem) = refs[:4], refs[4:7], refs[7:]
    blocks, unit, width = kept[0].shape
    core = lax.axis_index("col") & 1
    parts = sems.shape[1]
    size = blocks // parts
    places = (*kept, *away)

    def incoming(i, part):
        chosen = pl.ds(part * size, size)
        return pltpu.make_async_copy(
            weights[i].at[chosen], places[i].at[chosen], sems.at[i, part]
        )

    def left(i, j):
        if i == 0:
            return own_ref[j]
        if i == 2:
            return other_ref[j]
        return block_of(x_held, 0, j, core if i == 1 else 1 - core, unit)

    x_copy = pltpu.make_async_copy(x_ref.at[pl.ds(0, 1)], x_held, x_sem)
    for i in range(4):
        for part in range(parts):
            incoming(i, part).start()
        if i == 0:
            x_copy.start()
    wide = 256
    for i in range(4):
        if i == 1:
            x_copy.wait()
        for part in range(parts):
            incoming(i, part).wait()
            for n in range(width // wide):
                cols = slice(n * wide, (n + 1) * wide)
                total = None if i + part == 0 else out_ref[:, cols]
                for j in range(part * size, (part + 1) * size, 2):
                    pair = jnp.concatenate([left(i, j), left(i, j + 1)], axis=1)
                    right = places[i][j : j + 2, :, cols].reshape(2 * unit, wide)
                    term = jnp.dot(pair, right, preferred_element_type=jnp.float32)
                    total = term if total is None else total + term
                out_ref[:, cols] = total


def first_product(own, other, x, keeps, aways):
    blocks, unit, width = keeps[0].shape
    batch = own.shape[1]
    held = jax.ShapeDtypeStruct(keeps[0].shape, keeps[0].dtype)
    parts = 2
    return pl.pallas_call(
        first_kernel,
        out_shape=(jax.ShapeDtypeStruct((batch, width), jnp.float32), held, held),
        in_specs=[*[VMEM] * 2, *[HBM] * 5],
        out_specs=(VMEM, VMEM, VMEM),
        scratch_shapes=[
            pltpu.VMEM(keeps[0].shape, keeps[0].dtype),
            pltpu.VMEM(keeps[0].shape, keeps[0].dtype),
            pltpu.VMEM((1, *x.shape[1:]), x.dtype),
            pltpu.SemaphoreType.DMA((4, parts)),
            pltpu.SemaphoreType.DMA,
        ],
        cost_estimate=pl.CostEstimate(
            flops=8 * blocks * unit * batch * width,
            bytes_accessed=8 * blocks * unit * width,
            transcendentals=0,
        ),
        compiler_params=limits(7),
    )(resident(own), resident(other), *[outside(value) for value in (x, *keeps, *aways)])


def product_kernel(turn, stage, fed, *refs):
    refs = list(refs)
    out_ref, w_in_ref, w_rec_ref = refs.pop(), refs.pop(), refs.pop()
    x_ref = refs.pop() if fed else None
    blocks, unit, width = w_rec_ref.shape
    bottom = lax.axis_index("layer") == 0
    core = lax.axis_index("col") & 1

    def own(j):
        if stage == 1:
            return jnp.where(bottom, refs[1][j], refs[0][j])
        return refs[0][j, :, :unit]

    def below(j):
        came = refs[1][j] if stage == 1 else refs[0][j, :, unit:]
        return jnp.where(bottom, block_of(x_ref, turn, j, core, unit), came) if fed else came

    wide = 256
    for n in range(width // wide):
        cols = slice(n * wide, (n + 1) * wide)
        total = None
        for block, w_ref in ((own, w_rec_ref), (below, w_in_ref)):
            for j in range(0, blocks, 2):
                left = jnp.concatenate([block(j), block(j + 1)], axis=1)
                right = w_ref[j : j + 2, :, cols].reshape(2 * unit, wide)
                term = jnp.dot(left, right, preferred_element_type=jnp.float32)
                total = term if total is None else total + term
        out_ref[:, cols] = total


def product(gathered, x, w_rec, w_in, turn, stage):
    blocks, unit, width = w_rec.shape
    batch = gathered[0].shape[1]
    args = [*gathered, *([] if x is None else [x]), w_rec, w_in]
    return pl.pallas_call(
        functools.partial(product_kernel, turn, stage, x is not None),
        out_shape=jax.ShapeDtypeStruct((batch, width), jnp.float32),
        in_specs=[*[VMEM] * len(args)],
        out_specs=VMEM,
        cost_estimate=pl.CostEstimate(
            flops=4 * blocks * unit * batch * width,
            bytes_accessed=4 * blocks * unit * (batch + width) + 4 * batch * width,
            transcendentals=0,
        ),
        compiler_params=limits(4),
    )(*[resident(arg) for arg in args])


def gates_kernel(turn, steps, layers, parts, *refs):
    sums, (bias_ref, cell_ref, hid_ref) = refs[:parts], refs[parts : parts + 3]
    kept, (cell_out, hid_out) = refs[parts + 3 : -2], refs[-2:]
    unit = cell_ref.shape[1]
    layer = lax.axis_index("layer")
    valid = jnp.logical_and(turn >= layer, turn < layer + steps)

    def gate(k):
        cols = slice(k * unit, (k + 1) * unit)
        total = bias_ref[k : k + 1, :]
        for ref in sums:
            total = total + ref[:, cols]
        return total

    cell = cell_ref[...]
    cell_new = jax.nn.sigmoid(gate(1)) * cell + jax.nn.sigmoid(gate(0)) * jnp.tanh(gate(2))
    hidden_new = (jax.nn.sigmoid(gate(3)) * jnp.tanh(cell_new)).astype(hid_ref.dtype)
    hidden_new = jnp.where(valid, hidden_new, hid_ref[...])
    cell_out[...] = jnp.where(valid, cell_new, cell)
    if not kept:
        hid_out[...] = hidden_new
        return
    states = [*[ref[...] for ref in kept], hidden_new]
    for t in range(steps):
        value = states[t]
        for l in range(1, layers):
            value = jnp.where(layer == l, states[t + l], value)
        hid_out[t] = value


def gates(sums, bias, cell, hidden, turn, steps, layers, kept=()):
    hid_shape = (steps, *hidden.shape) if kept else hidden.shape
    args = (*sums, bias, cell, hidden, *kept)
    return pl.pallas_call(
        functools.partial(gates_kernel, turn, steps, layers, len(sums)),
        out_shape=(
            jax.ShapeDtypeStruct(cell.shape, cell.dtype),
            jax.ShapeDtypeStruct(hid_shape, hidden.dtype),
        ),
        in_specs=[VMEM] * len(args),
        out_specs=(VMEM, VMEM),
        cost_estimate=pl.CostEstimate(
            flops=20 * cell.size, bytes_accessed=40 * cell.size, transcendentals=5 * cell.size
        ),
        compiler_params=limits(2),
    )(*[resident(arg) for arg in args])


def spread_kernel(stage, *refs):
    out_ref = refs[-1]
    unit = refs[0].shape[1]
    layer = lax.axis_index("layer")
    for j in range(out_ref.shape[0]):
        if stage == 0:
            out_ref[j] = refs[0][...]
        elif stage == 1:
            out_ref[j] = jnp.where(layer == 0, refs[0][...], refs[1][...])
        else:
            out_ref[j, :, :unit] = refs[0][...]
            out_ref[j, :, unit:] = refs[1][...]


def spread(parts, stage, copies):
    batch, unit = parts[0].shape
    width = unit * (2 if stage == 2 else 1)
    return pl.pallas_call(
        functools.partial(spread_kernel, stage),
        out_shape=jax.ShapeDtypeStruct((copies, batch, width), parts[0].dtype),
        in_specs=[*[VMEM] * len(parts)],
        out_specs=VMEM,
        cost_estimate=pl.CostEstimate(
            flops=batch * width, bytes_accessed=2 * copies * batch * width, transcendentals=0
        ),
        compiler_params=limits(2),
    )(*[resident(part) for part in parts])


def body(inputs, w_input, w_recur, bias, h_start, c_start):
    steps, _, _ = inputs.shape
    layers = lax.axis_size("layer")
    devices = lax.axis_size("col")
    chips = devices // 2
    turns = steps + layers - 1
    same_core = [[2 * chip + side for chip in range(chips)] for side in range(2)]
    partners = [(i, i ^ 1) for i in range(devices)]
    upward = [(i, (i + 1) % layers) for i in range(layers)]

    def across(x):
        return lax.ppermute(x, "col", partners)

    def gathered(parts, stage):
        copies = spread(parts, stage, chips)
        return lax.all_to_all(copies, "col", 0, 0, tiled=True, axis_index_groups=same_core)

    cell = c_start[0]
    hidden = h_start[0]
    start = gathered((hidden,), 0)
    rec_keep, rec_away = sorted_weights(w_recur[0], chips)
    in_keep, in_away = sorted_weights(w_input[0], chips)
    other = across(start)
    *leaving, other = lax.optimization_barrier((rec_away, in_away, other))
    rec_send, in_send = (across(away) for away in leaving)

    kept = []
    for turn in range(turns):
        fed = inputs if turn < steps else None
        if turn == 0:
            z, rec_keep, in_keep = first_product(
                start, other, fed, (rec_keep, in_keep), (rec_away, in_away)
            )
            sums = (z,)
        else:
            stage = min(turn, 2)
            came = across(product(blocks, fed, rec_send, in_send, turn, stage))
            sums = (product(blocks, fed, rec_keep, in_keep, turn, stage), came)
        last = tuple(kept) if turn + 1 == turns else ()
        cell, hidden = gates(sums, bias[0], cell, hidden, turn, steps, layers, last)
        kept.append(hidden)
        if turn + 1 < turns:
            below = lax.ppermute(hidden, "layer", upward)
            blocks = (gathered((hidden, below), min(turn + 1, 2)),)
            if turn == 0:
                blocks = (start, *blocks)
    return hidden[None], cell[None]


def solution(mesh):
    in_specs = (
        P(),
        P("layer", None, None, "col"),
        P("layer", None, None, "col"),
        P("layer", None, "col"),
        P("layer", None, "col"),
        P("layer", None, "col"),
    )
    out_specs = (P("layer", None, None, "col"), P("layer", None, "col"))
    return jax.shard_map(body, mesh=mesh, in_specs=in_specs, out_specs=out_specs, check_vma=False)
```

time: 198 us -> 194 us (0.980)
  starting transfers between devices: 47.5 us -> 19.7 us
  blocking collectives: 106 us -> 123 us
  waiting for transfers between devices: 11.6 us -> 25.2 us
  Pallas kernels: 31.3 us -> 23.8 us
    ppermute x6, starting transfers between devices: 21.7 us -> 1.65 us  [body(): below = lax.ppermute(hidden, 'layer', upward)]
    all_to_all x6 -> x7, blocking collectives: 106 us -> 123 us  [gathered(): lax.all_to_all(copies, 'col', 0, 0, tiled=True, axis_index_groups=same_core)]
    ppermute x6, waiting for transfers between devices: 6.03 us -> 22.6 us  [body(): below = lax.ppermute(hidden, 'layer', upward)]
    all_to_all x1 -> x0, starting transfers between devices: 7.88 us -> none  [gathered(): lax.all_to_all(copies, 'col', 0, 0, tiled=True, axis_index_groups=same_core)]
    pallas_call x14 -> x10, Pallas kernels: 19.7 us -> 14.5 us  [the longest x2 8.4 us: sorted_weights(): pl.pallas_call(sort_kernel, out_shape=tuple([pltpu.HBM((blocks, depth, wi...]
    all_to_all x1 -> x0, waiting for transfers between devices: 2.44 us -> none  [gathered(): lax.all_to_all(copies, 'col', 0, 0, tiled=True, axis_index_groups=same_core)]
    pallas_call x14 -> x12, Pallas kernels: 9.88 us -> 8.55 us  [product(): pl.pallas_call(functools.partial(product_kernel, turn, stage, x is not No...]
  transfers between devices with their start and end apart: 16 -> 15, of which waited for: 14 -> 12; matrix products, arithmetic and copies ran while one was open for 0% -> 0% of each run, Pallas kernels for 9% -> 9%
where the time goes in v5:
time: 194 us
  blocking collectives  123 us (63%)
  waiting for transfers between devices  25.2 us (13%)
  Pallas kernels  23.8 us (12%)
  starting transfers between devices  19.7 us (10%)
    all_to_all x7, blocking collectives, gathered(): lax.all_to_all(copies, 'col', 0, 0, tiled=True, axis_index_groups=same_core)  123 us
    ppermute x6, waiting for transfers between devices, body(): below = lax.ppermute(hidden, 'layer', upward)  22.6 us
    ppermute x9, starting transfers between devices, across(): return lax.ppermute(x, 'col', partners)  18.1 us
    pallas_call x12, Pallas kernels, product(): pl.pallas_call(functools.partial(product_kernel, turn, stage, x is not No...  8.55 us
    pallas_call x2, Pallas kernels, sorted_weights(): pl.pallas_call(sort_kernel, out_shape=tuple([pltpu.HBM((blocks, depth, wi...  8.4 us
    pallas_call x1, Pallas kernels, first_product(): pl.pallas_call(first_kernel, out_shape=(jax.ShapeDtypeStruct((batch, widt...  4.96 us
  transfers between devices with their start and end apart: 15, of which 12 were waited for; matrix products, arithmetic and copies ran while one was open for 0% of the time, Pallas kernels for 9%

profile of v5, /device:TPU:1, one launch (start us, length us, event | category | flops | bytes accessed | tf_op | source)
XLA Modules:
  0.0 193.8 jit_solution(14592957113579626913)
XLA Ops:
  0.6 0.7 copy-done.1
  1.5 18.8 %all_to_all.35.own_ref.refs_0_ = bf16[16,128,128]{2,1,0:T(8,128)(2,1)S(1)} all-to-all(bf16[16,128,128]{2,1,0:T(8,128)(2,1)S(1)} %shard_map.77), channel_id=1, replica_groups={{0,2,4,6,8,10,12,14,16,18,20,22,24,26,28,30},{1,3,5,7,9,11,13,15,17,19,..., dimensions={0} | all-to-all | bytes 1048576 | tf_op jit(solution)/shard_map/all_to_all | solution.py:314
  20.3 2.1 %collective-permute-start = (bf16[16,128,128]{2,1,0:T(8,128)(2,1)S(1)}, bf16[16,128,128]{2,1,0:T(8,128)(2,1)S(1)}, u32[]{:S(2)}, u32[]{:S(2)}) collective-permute-start(bf16[16,128,128]{2,1,0:T(8,128)(2,1)S(1)} %all_to_all.35.own_ref.refs_0_), channel_id=1, source_target_pairs={{0,1},{1,0},{2,3},{3,2},{4,5},{5,4},{6,7},{7,6},{8,9},{9,8},{10,11... | collective-permute-start | bytes 1572872 | tf_op jit(solution)/shard_map/ppermute | solution.py:310
  22.3 4.2 %shard_map.79 = (bf16[16,128,512]{2,1,0:T(8,128)(2,1)}, bf16[16,128,512]{2,1,0:T(8,128)(2,1)}) custom-call(bf16[16,2,512,128]{3,2,1,0:T(8,128)(2,1)} %bitcast.17), custom_call_target="tpu_custom_call" | custom-call | flops 4000000000 | bytes 8388608 | tf_op jit(solution)/shard_map/pallas_call | solution.py:81
  26.5 4.2 %shard_map.78 = (bf16[16,128,512]{2,1,0:T(8,128)(2,1)}, bf16[16,128,512]{2,1,0:T(8,128)(2,1)}) custom-call(bf16[16,2,512,128]{3,2,1,0:T(8,128)(2,1)} %bitcast.18), custom_call_target="tpu_custom_call" | custom-call | flops 4000000000 | bytes 8388608 | tf_op jit(solution)/shard_map/pallas_call | solution.py:81
  31.4 5.0 %shard_map.80 = (f32[128,512]{1,0:T(8,128)S(1)}, bf16[16,128,512]{2,1,0:T(8,128)(2,1)S(1)}, bf16[16,128,512]{2,1,0:T(8,128)(2,1)S(1)}) custom-call(bf16[16,128,128]{2,1,0:T(8,128)(2,1)S(1)} %all_to_all.35.own_ref.refs_0_, bf16[16,128,128]{2,1,0:T(8,128)(2,1)S(1)} %collective-permute-done.other_ref, bf16[4,128,4096]{2,1,0:T(8,128)(2,1)} %refs_1_.7, ...), custom_call_target="tpu_custom_call" | custom-call | flops 1073741824 | bytes 8388608 | tf_op jit(solution)/shard_map/pallas_call | solution.py:153
  36.4 1.3 collective-permute-start.1
  37.7 2.8 %collective-permute-done.1.refs_1_ = bf16[128,128]{1,0:T(8,128)(2,1)S(1)} collective-permute-done((bf16[128,128]{1,0:T(8,128)(2,1)S(1)}, bf16[128,128]{1,0:T(8,128)(2,1)S(1)}, u32[]{:S(2)}, u32[]{:S(2)}) %collective-permute-start.1) | collective-permute-done | bytes 32800 | tf_op jit(solution)/shard_map/ppermute | solution.py:341
  40.6 12.8 %all_to_all.36.refs_1_ = bf16[16,128,128]{2,1,0:T(8,128)(2,1)S(1)} all-to-all(bf16[16,128,128]{2,1,0:T(8,128)(2,1)S(1)} %shard_map.82), channel_id=1, replica_groups={{0,2,4,6,8,10,12,14,16,18,20,22,24,26,28,30},{1,3,5,7,9,11,13,15,17,19,..., dimensions={0} | all-to-all | bytes 1048576 | tf_op jit(solution)/shard_map/all_to_all | solution.py:314
  53.4 0.7 shard_map.84
  54.1 2.4 %collective-permute-start.4 = (f32[128,512]{1,0:T(8,128)S(1)}, f32[128,512]{1,0:T(8,128)S(1)}, u32[]{:S(2)}, u32[]{:S(2)}) collective-permute-start(f32[128,512]{1,0:T(8,128)S(1)} %shard_map.84), channel_id=1, source_target_pairs={{0,1},{1,0},{2,3},{3,2},{4,5},{5,4},{6,7},{7,6},{8,9},{9,8},{10,11... | collective-permute-start | bytes 786440 | tf_op jit(solution)/shard_map/ppermute | solution.py:310
  56.6 0.7 shard_map.83.refs_0_
  57.9 4.0 %collective-permute-done.5.refs_1_ = bf16[128,128]{1,0:T(8,128)(2,1)S(1)} collective-permute-done((bf16[128,128]{1,0:T(8,128)(2,1)S(1)}, bf16[128,128]{1,0:T(8,128)(2,1)S(1)}, u32[]{:S(2)}, u32[]{:S(2)}) %collective-permute-start.5) | collective-permute-done | bytes 32800 | tf_op jit(solution)/shard_map/ppermute | solution.py:341
  62.0 18.3 %all_to_all.37.refs_0_ = bf16[16,128,256]{2,1,0:T(8,128)(2,1)S(1)} all-to-all(bf16[16,128,256]{2,1,0:T(8,128)(2,1)S(1)} %shard_map.86), channel_id=1, replica_groups={{0,2,4,6,8,10,12,14,16,18,20,22,24,26,28,30},{1,3,5,7,9,11,13,15,17,19,..., dimensions={0} | all-to-all | bytes 2097152 | tf_op jit(solution)/shard_map/all_to_all | solution.py:314
  80.3 0.7 shard_map.88
  81.0 2.6 %collective-permute-start.6 = (f32[128,512]{1,0:T(8,128)S(1)}, f32[128,512]{1,0:T(8,128)S(1)}, u32[]{:S(2)}, u32[]{:S(2)}) collective-permute-start(f32[128,512]{1,0:T(8,128)S(1)} %shard_map.88), channel_id=1, source_target_pairs={{0,1},{1,0},{2,3},{3,2},{4,5},{5,4},{6,7},{7,6},{8,9},{9,8},{10,11... | collective-permute-start | bytes 786440 | tf_op jit(solution)/shard_map/ppermute | solution.py:310
  83.6 0.7 shard_map.87.refs_0_
  85.0 4.0 %collective-permute-done.7.refs_1_ = bf16[128,128]{1,0:T(8,128)(2,1)S(1)} collective-permute-done((bf16[128,128]{1,0:T(8,128)(2,1)S(1)}, bf16[128,128]{1,0:T(8,128)(2,1)S(1)}, u32[]{:S(2)}, u32[]{:S(2)}) %collective-permute-start.7) | collective-permute-done | bytes 32800 | tf_op jit(solution)/shard_map/ppermute | solution.py:341
  89.1 18.3 %all_to_all.38.refs_0_ = bf16[16,128,256]{2,1,0:T(8,128)(2,1)S(1)} all-to-all(bf16[16,128,256]{2,1,0:T(8,128)(2,1)S(1)} %shard_map.90), channel_id=1, replica_groups={{0,2,4,6,8,10,12,14,16,18,20,22,24,26,28,30},{1,3,5,7,9,11,13,15,17,19,..., dimensions={0} | all-to-all | bytes 2097152 | tf_op jit(solution)/shard_map/all_to_all | solution.py:314
  107.4 0.7 shard_map.92
  108.1 2.7 %collective-permute-start.8 = (f32[128,512]{1,0:T(8,128)S(1)}, f32[128,512]{1,0:T(8,128)S(1)}, u32[]{:S(2)}, u32[]{:S(2)}) collective-permute-start(f32[128,512]{1,0:T(8,128)S(1)} %shard_map.92), channel_id=1, source_target_pairs={{0,1},{1,0},{2,3},{3,2},{4,5},{5,4},{6,7},{7,6},{8,9},{9,8},{10,11... | collective-permute-start | bytes 786440 | tf_op jit(solution)/shard_map/ppermute | solution.py:310
  110.8 0.7 shard_map.91.refs_0_
  112.1 4.0 %collective-permute-done.9.refs_1_ = bf16[128,128]{1,0:T(8,128)(2,1)S(1)} collective-permute-done((bf16[128,128]{1,0:T(8,128)(2,1)S(1)}, bf16[128,128]{1,0:T(8,128)(2,1)S(1)}, u32[]{:S(2)}, u32[]{:S(2)}) %collective-permute-start.9) | collective-permute-done | bytes 32800 | tf_op jit(solution)/shard_map/ppermute | solution.py:341
  116.3 18.4 %all_to_all.39.refs_0_ = bf16[16,128,256]{2,1,0:T(8,128)(2,1)S(1)} all-to-all(bf16[16,128,256]{2,1,0:T(8,128)(2,1)S(1)} %shard_map.94), channel_id=1, replica_groups={{0,2,4,6,8,10,12,14,16,18,20,22,24,26,28,30},{1,3,5,7,9,11,13,15,17,19,..., dimensions={0} | all-to-all | bytes 2097152 | tf_op jit(solution)/shard_map/all_to_all | solution.py:314
  135.3 2.5 %collective-permute-start.10 = (f32[128,512]{1,0:T(8,128)S(1)}, f32[128,512]{1,0:T(8,128)S(1)}, u32[]{:S(2)}, u32[]{:S(2)}) collective-permute-start(f32[128,512]{1,0:T(8,128)S(1)} %shard_map.96), channel_id=1, source_target_pairs={{0,1},{1,0},{2,3},{3,2},{4,5},{5,4},{6,7},{7,6},{8,9},{9,8},{10,11... | collective-permute-start | bytes 786440 | tf_op jit(solution)/shard_map/ppermute | solution.py:310
  139.2 4.0 %collective-permute-done.11.refs_1_ = bf16[128,128]{1,0:T(8,128)(2,1)S(1)} collective-permute-done((bf16[128,128]{1,0:T(8,128)(2,1)S(1)}, bf16[128,128]{1,0:T(8,128)(2,1)S(1)}, u32[]{:S(2)}, u32[]{:S(2)}) %collective-permute-start.11) | collective-permute-done | bytes 32800 | tf_op jit(solution)/shard_map/ppermute | solution.py:341
  143.3 18.4 %all_to_all.40.refs_0_ = bf16[16,128,256]{2,1,0:T(8,128)(2,1)S(1)} all-to-all(bf16[16,128,256]{2,1,0:T(8,128)(2,1)S(1)} %shard_map.98), channel_id=1, replica_groups={{0,2,4,6,8,10,12,14,16,18,20,22,24,26,28,30},{1,3,5,7,9,11,13,15,17,19,..., dimensions={0} | all-to-all | bytes 2097152 | tf_op jit(solution)/shard_map/all_to_all | solution.py:314
  162.3 2.5 %collective-permute-start.12 = (f32[128,512]{1,0:T(8,128)S(1)}, f32[128,512]{1,0:T(8,128)S(1)}, u32[]{:S(2)}, u32[]{:S(2)}) collective-permute-start(f32[128,512]{1,0:T(8,128)S(1)} %shard_map.100), channel_id=1, source_target_pairs={{0,1},{1,0},{2,3},{3,2},{4,5},{5,4},{6,7},{7,6},{8,9},{9,8},{10,11... | collective-permute-start | bytes 786440 | tf_op jit(solution)/shard_map/ppermute | solution.py:310
  166.2 4.0 %collective-permute-done.13.refs_1_ = bf16[128,128]{1,0:T(8,128)(2,1)S(1)} collective-permute-done((bf16[128,128]{1,0:T(8,128)(2,1)S(1)}, bf16[128,128]{1,0:T(8,128)(2,1)S(1)}, u32[]{:S(2)}, u32[]{:S(2)}) %collective-permute-start.13) | collective-permute-done | bytes 32800 | tf_op jit(solution)/shard_map/ppermute | solution.py:341
  170.3 18.4 %all_to_all.41.refs_0_ = bf16[16,128,256]{2,1,0:T(8,128)(2,1)S(1)} all-to-all(bf16[16,128,256]{2,1,0:T(8,128)(2,1)S(1)} %shard_map.102), channel_id=1, replica_groups={{0,2,4,6,8,10,12,14,16,18,20,22,24,26,28,30},{1,3,5,7,9,11,13,15,17,19,..., dimensions={0} | all-to-all | bytes 2097152 | tf_op jit(solution)/shard_map/all_to_all | solution.py:314
  189.4 2.5 %collective-permute-start.14 = (f32[128,512]{1,0:T(8,128)S(1)}, f32[128,512]{1,0:T(8,128)S(1)}, u32[]{:S(2)}, u32[]{:S(2)}) collective-permute-start(f32[128,512]{1,0:T(8,128)S(1)} %shard_map.104), channel_id=1, source_target_pairs={{0,1},{1,0},{2,3},{3,2},{4,5},{5,4},{6,7},{7,6},{8,9},{9,8},{10,11... | collective-permute-start | bytes 786440 | tf_op jit(solution)/shard_map/ppermute | solution.py:310
  193.1 0.7 shard_map.105
  (46 shorter events, 9.0 us)
Async XLA Ops:
  0.6 0.8 copy-start.1
  20.3 10.5 %collective-permute-start = (bf16[16,128,128]{2,1,0:T(8,128)(2,1)S(1)}, bf16[16,128,128]{2,1,0:T(8,128)(2,1)S(1)}, u32[]{:S(2)}, u32[]{:S(2)}) collective-permute-start(bf16[16,128,128]{2,1,0:T(8,128)(2,1)S(1)} %all_to_all.35.own_ref.refs_0_), channel_id=1, source_target_pairs={{0,1},{1,0},{2,3},{3,2},{4,5},{5,4},{6,7},{7,6},{8,9},{9,8},{10,11... | collective-permute-start | bytes 1572872 | tf_op jit(solution)/shard_map/ppermute | solution.py:310
  26.5 4.4 %copy-start.5 = (bf16[16,128,512]{2,1,0:T(8,128)(2,1)S(1)}, bf16[16,128,512]{2,1,0:T(8,128)(2,1)}, u32[]{:S(2)}) copy-start(bf16[16,128,512]{2,1,0:T(8,128)(2,1)} %get-tuple-element.36.refs_3_) | copy-start | bytes 6291460
  30.8 22.6 %collective-permute-start.2 = (bf16[16,128,512]{2,1,0:T(8,128)(2,1)}, bf16[16,128,512]{2,1,0:T(8,128)(2,1)S(1)}, u32[]{:S(2)}, u32[]{:S(2)}) collective-permute-start(bf16[16,128,512]{2,1,0:T(8,128)(2,1)} %get-tuple-element.35.refs_2_), channel_id=1, source_target_pairs={{0,1},{1,0},{2,3},{3,2},{4,5},{5,4},{6,7},{7,6},{8,9},{9,8},{10,11... | collective-permute-start | bytes 6291464 | tf_op jit(solution)/shard_map/ppermute | solution.py:310
  30.9 22.5 %collective-permute-start.3 = (bf16[16,128,512]{2,1,0:T(8,128)(2,1)S(1)}, bf16[16,128,512]{2,1,0:T(8,128)(2,1)S(1)}, u32[]{:S(2)}, u32[]{:S(2)}) collective-permute-start(bf16[16,128,512]{2,1,0:T(8,128)(2,1)S(1)} %copy-done.5), channel_id=1, source_target_pairs={{0,1},{1,0},{2,3},{3,2},{4,5},{5,4},{6,7},{7,6},{8,9},{9,8},{10,11... | collective-permute-start | bytes 6291464 | tf_op jit(solution)/shard_map/ppermute | solution.py:310
  31.4 5.0 %copy-start.2 = (bf16[1,128,128]{2,1,0:T(8,128)(2,1)S(1)}, bf16[1,128,128]{2,1,0:T(8,128)(2,1)}, u32[]{:S(2)}) copy-start(bf16[1,128,128]{2,1,0:T(8,128)(2,1)} %param.10) | copy-start | bytes 98308
  31.4 5.0 %copy-start.3 = (f32[1,4,128]{2,1,0:T(4,128)S(1)}, f32[1,4,128]{2,1,0:T(4,128)}, u32[]{:S(2)}) copy-start(f32[1,4,128]{2,1,0:T(4,128)} %param.9) | copy-start | bytes 6148
  31.4 5.0 %copy-start.4 = (f32[1,128,128]{2,1,0:T(8,128)S(1)}, f32[1,128,128]{2,1,0:T(8,128)}, u32[]{:S(2)}) copy-start(f32[1,128,128]{2,1,0:T(8,128)} %param.11) | copy-start | bytes 196612
  31.4 22.0 %copy-start = (bf16[4,128,4096]{2,1,0:T(8,128)(2,1)S(1)}, bf16[4,128,4096]{2,1,0:T(8,128)(2,1)}, u32[]{:S(2)}) copy-start(bf16[4,128,4096]{2,1,0:T(8,128)(2,1)} %refs_1_.7) | copy-start | bytes 12582916
  36.4 4.0 %collective-permute-start.1 = (bf16[128,128]{1,0:T(8,128)(2,1)S(1)}, bf16[128,128]{1,0:T(8,128)(2,1)S(1)}, u32[]{:S(2)}, u32[]{:S(2)}) collective-permute-start(bf16[128,128]{1,0:T(8,128)(2,1)S(1)} %get-tuple-element.32.refs_0_.refs_4_.refs_5_), channel_id=1, source_target_pairs={{0,32},{32,64},{64,96},{96,0},{1,33},{33,65},{65,97},{97,1},{2,34}... | collective-permute-start | bytes 98312 | tf_op jit(solution)/shard_map/ppermute | solution.py:341
  54.1 3.6 %collective-permute-start.4 = (f32[128,512]{1,0:T(8,128)S(1)}, f32[128,512]{1,0:T(8,128)S(1)}, u32[]{:S(2)}, u32[]{:S(2)}) collective-permute-start(f32[128,512]{1,0:T(8,128)S(1)} %shard_map.84), channel_id=1, source_target_pairs={{0,1},{1,0},{2,3},{3,2},{4,5},{5,4},{6,7},{7,6},{8,9},{9,8},{10,11... | collective-permute-start | bytes 786440 | tf_op jit(solution)/shard_map/ppermute | solution.py:310
  57.8 4.0 %collective-permute-start.5 = (bf16[128,128]{1,0:T(8,128)(2,1)S(1)}, bf16[128,128]{1,0:T(8,128)(2,1)S(1)}, u32[]{:S(2)}, u32[]{:S(2)}) collective-permute-start(bf16[128,128]{1,0:T(8,128)(2,1)S(1)} %get-tuple-element.38.refs_0_.refs_4_.refs_6_), channel_id=1, source_target_pairs={{0,32},{32,64},{64,96},{96,0},{1,33},{33,65},{65,97},{97,1},{2,34}... | collective-permute-start | bytes 98312 | tf_op jit(solution)/shard_map/ppermute | solution.py:341
  81.0 3.8 %collective-permute-start.6 = (f32[128,512]{1,0:T(8,128)S(1)}, f32[128,512]{1,0:T(8,128)S(1)}, u32[]{:S(2)}, u32[]{:S(2)}) collective-permute-start(f32[128,512]{1,0:T(8,128)S(1)} %shard_map.88), channel_id=1, source_target_pairs={{0,1},{1,0},{2,3},{3,2},{4,5},{5,4},{6,7},{7,6},{8,9},{9,8},{10,11... | collective-permute-start | bytes 786440 | tf_op jit(solution)/shard_map/ppermute | solution.py:310
  84.9 4.0 %collective-permute-start.7 = (bf16[128,128]{1,0:T(8,128)(2,1)S(1)}, bf16[128,128]{1,0:T(8,128)(2,1)S(1)}, u32[]{:S(2)}, u32[]{:S(2)}) collective-permute-start(bf16[128,128]{1,0:T(8,128)(2,1)S(1)} %get-tuple-element.40.refs_0_.refs_4_.refs_7_), channel_id=1, source_target_pairs={{0,32},{32,64},{64,96},{96,0},{1,33},{33,65},{65,97},{97,1},{2,34}... | collective-permute-start | bytes 98312 | tf_op jit(solution)/shard_map/ppermute | solution.py:341
  108.1 3.9 %collective-permute-start.8 = (f32[128,512]{1,0:T(8,128)S(1)}, f32[128,512]{1,0:T(8,128)S(1)}, u32[]{:S(2)}, u32[]{:S(2)}) collective-permute-start(f32[128,512]{1,0:T(8,128)S(1)} %shard_map.92), channel_id=1, source_target_pairs={{0,1},{1,0},{2,3},{3,2},{4,5},{5,4},{6,7},{7,6},{8,9},{9,8},{10,11... | collective-permute-start | bytes 786440 | tf_op jit(solution)/shard_map/ppermute | solution.py:310
  112.1 4.0 %collective-permute-start.9 = (bf16[128,128]{1,0:T(8,128)(2,1)S(1)}, bf16[128,128]{1,0:T(8,128)(2,1)S(1)}, u32[]{:S(2)}, u32[]{:S(2)}) collective-permute-start(bf16[128,128]{1,0:T(8,128)(2,1)S(1)} %get-tuple-element.42.refs_0_.refs_4_.refs_8_), channel_id=1, source_target_pairs={{0,32},{32,64},{64,96},{96,0},{1,33},{33,65},{65,97},{97,1},{2,34}... | collective-permute-start | bytes 98312 | tf_op jit(solution)/shard_map/ppermute | solution.py:341
  135.3 3.7 %collective-permute-start.10 = (f32[128,512]{1,0:T(8,128)S(1)}, f32[128,512]{1,0:T(8,128)S(1)}, u32[]{:S(2)}, u32[]{:S(2)}) collective-permute-start(f32[128,512]{1,0:T(8,128)S(1)} %shard_map.96), channel_id=1, source_target_pairs={{0,1},{1,0},{2,3},{3,2},{4,5},{5,4},{6,7},{7,6},{8,9},{9,8},{10,11... | collective-permute-start | bytes 786440 | tf_op jit(solution)/shard_map/ppermute | solution.py:310
  139.1 4.0 %collective-permute-start.11 = (bf16[128,128]{1,0:T(8,128)(2,1)S(1)}, bf16[128,128]{1,0:T(8,128)(2,1)S(1)}, u32[]{:S(2)}, u32[]{:S(2)}) collective-permute-start(bf16[128,128]{1,0:T(8,128)(2,1)S(1)} %get-tuple-element.44.refs_0_.refs_4_.refs_9_), channel_id=1, source_target_pairs={{0,32},{32,64},{64,96},{96,0},{1,33},{33,65},{65,97},{97,1},{2,34}... | collective-permute-start | bytes 98312 | tf_op jit(solution)/shard_map/ppermute | solution.py:341
  162.3 3.7 %collective-permute-start.12 = (f32[128,512]{1,0:T(8,128)S(1)}, f32[128,512]{1,0:T(8,128)S(1)}, u32[]{:S(2)}, u32[]{:S(2)}) collective-permute-start(f32[128,512]{1,0:T(8,128)S(1)} %shard_map.100), channel_id=1, source_target_pairs={{0,1},{1,0},{2,3},{3,2},{4,5},{5,4},{6,7},{7,6},{8,9},{9,8},{10,11... | collective-permute-start | bytes 786440 | tf_op jit(solution)/shard_map/ppermute | solution.py:310
  166.1 4.0 %collective-permute-start.13 = (bf16[128,128]{1,0:T(8,128)(2,1)S(1)}, bf16[128,128]{1,0:T(8,128)(2,1)S(1)}, u32[]{:S(2)}, u32[]{:S(2)}) collective-permute-start(bf16[128,128]{1,0:T(8,128)(2,1)S(1)} %get-tuple-element.46.refs_0_.refs_4_.refs_10_), channel_id=1, source_target_pairs={{0,32},{32,64},{64,96},{96,0},{1,33},{33,65},{65,97},{97,1},{2,34}... | collective-permute-start | bytes 98312 | tf_op jit(solution)/shard_map/ppermute | solution.py:341
  189.4 3.7 %collective-permute-start.14 = (f32[128,512]{1,0:T(8,128)S(1)}, f32[128,512]{1,0:T(8,128)S(1)}, u32[]{:S(2)}, u32[]{:S(2)}) collective-permute-start(f32[128,512]{1,0:T(8,128)S(1)} %shard_map.104), channel_id=1, source_target_pairs={{0,1},{1,0},{2,3},{3,2},{4,5},{5,4},{6,7},{7,6},{8,9},{9,8},{10,11... | collective-permute-start | bytes 786440 | tf_op jit(solution)/shard_map/ppermute | solution.py:310

commit v6 on v5

--- a/solution.py
+++ b/solution.py
@@ -23,7 +23,13 @@
     return pltpu.CompilerParams(vmem_limit_bytes=mib << 20)
 
 
-def sort_kernel(w_ref, keep_ref, away_ref, natural, ordered, in_sems, out_sems):
+def sort_kernel(fed, *refs):
+    refs = list(refs)
+    w_ref = refs.pop(0)
+    x_ref = refs.pop(0) if fed else None
+    keep_ref, away_ref = refs.pop(0), refs.pop(0)
+    sum_ref = refs.pop(0) if fed else None
+    natural, ordered, in_sems, out_sems = refs[:4]
     blocks, _, depth, wide = ordered.shape
     unit = natural.shape[3]
     gates = wide // unit
@@ -52,6 +58,10 @@
 
     for part in range(parts):
         incoming(part).start()
+        if fed and part == 0:
+            x_held, x_sem = refs[4:]
+            x_copy = pltpu.make_async_copy(x_ref.at[0], x_held, x_sem)
+            x_copy.start()
     for part in range(parts):
         incoming(part).wait()
         for j in range(part * size, (part + 1) * size):
@@ -68,32 +78,47 @@
                         )
         for away in range(2):
             outgoing(part, away).start()
+        if fed:
+            if part == 0:
+                x_copy.wait()
+            for cols in (slice(n, n + 256) for n in range(0, wide, 256)):
+                total = None if part == 0 else sum_ref[:, cols]
+                for j in range(part * size, (part + 1) * size):
+                    left = x_held[:, 2 * j * depth : 2 * (j + 1) * depth]
+                    right = ordered[j, :, :, cols].reshape(2 * depth, 256)
+                    term = jnp.dot(left, right, preferred_element_type=jnp.float32)
+                    total = term if total is None else total + term
+                sum_ref[:, cols] = total
     for part in range(parts):
         for away in range(2):
             outgoing(part, away).wait()
 
 
-def sorted_weights(w, blocks):
+def sorted_weights(w, blocks, x=None):
     gates, unit = w.shape[1:]
     depth = w.shape[0] // (2 * blocks)
     wide = gates * unit
     parts = 4
-    return pl.pallas_call(
-        sort_kernel,
-        out_shape=tuple([pltpu.HBM((blocks, depth, wide), w.dtype)] * 2),
-        in_specs=[HBM],
-        out_specs=(HBM, HBM),
+    fed = x is not None
+    sides = [pltpu.HBM((blocks, depth, wide), w.dtype)] * 2
+    natural = (blocks, 2, depth * gates, unit)
+    return pl.pallas_call(
+        functools.partial(sort_kernel, fed),
+        out_shape=(*sides, *([jax.ShapeDtypeStruct((x.shape[1], wide), jnp.float32)] if fed else [])),
+        in_specs=[HBM] * (1 + fed),
+        out_specs=(HBM, HBM, *([VMEM] if fed else [])),
         scratch_shapes=[
-            pltpu.VMEM((blocks, 2, depth * gates, unit), w.dtype),
+            pltpu.VMEM(natural, w.dtype),
             pltpu.VMEM((blocks, 2, depth, wide), w.dtype),
             pltpu.SemaphoreType.DMA((parts,)),
             pltpu.SemaphoreType.DMA((parts, 2)),
+            *([pltpu.VMEM(x.shape[1:], x.dtype), pltpu.SemaphoreType.DMA] if fed else []),
         ],
         cost_estimate=pl.CostEstimate(
             flops=4_000_000_000, bytes_accessed=8 * blocks * depth * wide, transcendentals=0
         ),
-        compiler_params=limits(10),
-    )(outside(w.reshape(blocks, 2, depth * gates, unit)))
+        compiler_params=limits(12),
+    )(outside(w.reshape(natural)), *([outside(x)] if fed else []))
 
 
 def block_of(x_ref, turn, j, side, unit):
@@ -101,74 +126,80 @@
     return x_ref[turn, :, pl.ds(at, unit)]
 
 
-def first_kernel(own_ref, other_ref, x_ref, *refs):
-    weights, (out_ref, *kept), (*away, x_held, sems, x_sem) = refs[:4], refs[4:7], refs[7:]
-    blocks, unit, width = kept[0].shape
-    core = lax.axis_index("col") & 1
+def first_kernel(acc_ref, own_ref, keep_ref, away_ref, out_ref, kept_ref, held_ref, sems):
+    blocks, unit, width = kept_ref.shape
     parts = sems.shape[1]
     size = blocks // parts
-    places = (*kept, *away)
-
-    def incoming(i, part):
+
+    def incoming(away, part):
         chosen = pl.ds(part * size, size)
-        return pltpu.make_async_copy(
-            weights[i].at[chosen], places[i].at[chosen], sems.at[i, part]
-        )
-
-    def left(i, j):
-        if i == 0:
-            return own_ref[j]
-        if i == 2:
-            return other_ref[j]
-        return block_of(x_held, 0, j, core if i == 1 else 1 - core, unit)
-
-    x_copy = pltpu.make_async_copy(x_ref.at[pl.ds(0, 1)], x_held, x_sem)
-    for i in range(4):
+        from_ref, to_ref = (away_ref, held_ref) if away else (keep_ref, kept_ref)
+        return pltpu.make_async_copy(from_ref.at[chosen], to_ref.at[chosen], sems.at[away, part])
+
+    for away in range(2):
         for part in range(parts):
-            incoming(i, part).start()
-        if i == 0:
-            x_copy.start()
+            incoming(away, part).start()
     wide = 256
-    for i in range(4):
-        if i == 1:
-            x_copy.wait()
-        for part in range(parts):
-            incoming(i, part).wait()
-            for n in range(width // wide):
-                cols = slice(n * wide, (n + 1) * wide)
-                total = None if i + part == 0 else out_ref[:, cols]
-                for j in range(part * size, (part + 1) * size, 2):
-                    pair = jnp.concatenate([left(i, j), left(i, j + 1)], axis=1)
-                    right = places[i][j : j + 2, :, cols].reshape(2 * unit, wide)
-                    term = jnp.dot(pair, right, preferred_element_type=jnp.float32)
-                    total = term if total is None else total + term
-                out_ref[:, cols] = total
-
-
-def first_product(own, other, x, keeps, aways):
-    blocks, unit, width = keeps[0].shape
-    batch = own.shape[1]
-    held = jax.ShapeDtypeStruct(keeps[0].shape, keeps[0].dtype)
+    for part in range(parts):
+        incoming(0, part).wait()
+        for n in range(width // wide):
+            cols = slice(n * wide, (n + 1) * wide)
+            total = out_ref[:, cols] if part else acc_ref[:, cols]
+            for j in range(part * size, (part + 1) * size, 2):
+                pair = jnp.concatenate([own_ref[j], own_ref[j + 1]], axis=1)
+                right = kept_ref[j : j + 2, :, cols].reshape(2 * unit, wide)
+                total = total + jnp.dot(pair, right, preferred_element_type=jnp.float32)
+            out_ref[:, cols] = total
+    for part in range(parts):
+        incoming(1, part).wait()
+
+
+def first_product(acc, own, keep, away):
+    blocks, unit, width = keep.shape
+    held = jax.ShapeDtypeStruct(keep.shape, keep.dtype)
     parts = 2
     return pl.pallas_call(
         first_kernel,
-        out_shape=(jax.ShapeDtypeStruct((batch, width), jnp.float32), held, held),
-        in_specs=[*[VMEM] * 2, *[HBM] * 5],
+        out_shape=(jax.ShapeDtypeStruct(acc.shape, acc.dtype), held, held),
+        in_specs=[VMEM, VMEM, HBM, HBM],
         out_specs=(VMEM, VMEM, VMEM),
-        scratch_shapes=[
-            pltpu.VMEM(keeps[0].shape, keeps[0].dtype),
-            pltpu.VMEM(keeps[0].shape, keeps[0].dtype),
-            pltpu.VMEM((1, *x.shape[1:]), x.dtype),
-            pltpu.SemaphoreType.DMA((4, parts)),
-            pltpu.SemaphoreType.DMA,
-        ],
-        cost_estimate=pl.CostEstimate(
-            flops=8 * blocks * unit * batch * width,
-            bytes_accessed=8 * blocks * unit * width,
+        scratch_shapes=[pltpu.SemaphoreType.DMA((2, parts))],
+        cost_estimate=pl.CostEstimate(
+            flops=2 * blocks * unit * acc.shape[0] * width,
+            bytes_accessed=4 * blocks * unit * width,
             transcendentals=0,
         ),
-        compiler_params=limits(7),
-    )(resident(own), resident(other), *[outside(value) for value in (x, *keeps, *aways)])
+        compiler_params=limits(2),
+    )(resident(acc), resident(own), outside(keep), outside(away))
+
+
+def added_kernel(acc_ref, g_ref, w_ref, out_ref):
+    blocks, unit, width = w_ref.shape
+    wide = 256
+    for n in range(width // wide):
+        cols = slice(n * wide, (n + 1) * wide)
+        total = acc_ref[:, cols]
+        for j in range(0, blocks, 2):
+            pair = jnp.concatenate([g_ref[j], g_ref[j + 1]], axis=1)
+            right = w_ref[j : j + 2, :, cols].reshape(2 * unit, wide)
+            total = total + jnp.dot(pair, right, preferred_element_type=jnp.float32)
+        out_ref[:, cols] = total
+
+
+def added_product(acc, g, w):
+    blocks, unit, width = w.shape
+    return pl.pallas_call(
+        added_kernel,
+        out_shape=jax.ShapeDtypeStruct(acc.shape, acc.dtype),
+        in_specs=[VMEM] * 3,
+        out_specs=VMEM,
+        cost_estimate=pl.CostEstimate(
+            flops=2 * blocks * unit * width * acc.shape[0],
+            bytes_accessed=2 * blocks * unit * width,
+            transcendentals=0,
+        ),
+        compiler_params=limits(2),
+    )(*[resident(value) for value in (acc, g, w)])
 
 
 def product_kernel(turn, stage, fed, *refs):
@@ -317,19 +348,16 @@
     hidden = h_start[0]
     start = gathered((hidden,), 0)
     rec_keep, rec_away = sorted_weights(w_recur[0], chips)
-    in_keep, in_away = sorted_weights(w_input[0], chips)
+    in_keep, in_away, z = sorted_weights(w_input[0], chips, inputs)
     other = across(start)
-    *leaving, other = lax.optimization_barrier((rec_away, in_away, other))
-    rec_send, in_send = (across(away) for away in leaving)
-
+    z, rec_keep, rec_held = first_product(z, start, rec_keep, rec_away)
+    rec_away, in_away, z = lax.optimization_barrier((rec_away, in_away, z))
+    rec_send, in_send = across(rec_away), across(in_away)
     kept = []
     for turn in range(turns):
         fed = inputs if turn < steps else None
         if turn == 0:
-            z, rec_keep, in_keep = first_product(
-                start, other, fed, (rec_keep, in_keep), (rec_away, in_away)
-            )
-            sums = (z,)
+            sums = (added_product(z, other, rec_held),)
         else:
             stage = min(turn, 2)
             came = across(product(blocks, fed, rec_send, in_send, turn, stage))

time: 194 us -> 194 us (level)
  blocking collectives: 123 us -> 106 us
  starting transfers between devices: 19.7 us -> 28.5 us
  waiting for transfers between devices: 25.2 us -> 33.4 us
    all_to_all x7 -> x6, blocking collectives: 123 us -> 106 us  [gathered(): lax.all_to_all(copies, 'col', 0, 0, tiled=True, axis_index_groups=same_core)]
    all_to_all x0 -> x1, starting transfers between devices: none -> 8.59 us  [gathered(): lax.all_to_all(copies, 'col', 0, 0, tiled=True, axis_index_groups=same_core)]
    ppermute x9, waiting for transfers between devices: 2.66 us -> 9.54 us  [across(): return lax.ppermute(x, 'col', partners)]
    pallas_call x3 -> x4, Pallas kernels: 13.4 us -> 11.9 us  [the longest x2 9.13 us: sorted_weights(): pl.pallas_call(functools.partial(sort_kernel, fed), out_shape=(*sides, *(...]
  transfers between devices with their start and end apart: 15 -> 16, of which waited for: 12 -> 14; matrix products, arithmetic and copies ran while one was open for 0% -> 0% of each run, Pallas kernels for 9% -> 7%
where the time goes in v6:
time: 194 us; the launch traced here: 193 us
  blocking collectives  106 us (55%)
  waiting for transfers between devices  33.4 us (17%)
  starting transfers between devices  28.5 us (15%)
  Pallas kernels  23.3 us (12%)
    all_to_all x6, blocking collectives, gathered(): lax.all_to_all(copies, 'col', 0, 0, tiled=True, axis_index_groups=same_core)  106 us
    ppermute x6, waiting for transfers between devices, body(): below = lax.ppermute(hidden, 'layer', upward)  22.6 us
    ppermute x9, starting transfers between devices, across(): return lax.ppermute(x, 'col', partners)  18.3 us
    ppermute x9, waiting for transfers between devices, across(): return lax.ppermute(x, 'col', partners)  9.54 us
    pallas_call x2, Pallas kernels, sorted_weights(): pl.pallas_call(functools.partial(sort_kernel, fed), out_shape=(*sides, *(...  9.13 us
    all_to_all x1, starting transfers between devices, gathered(): lax.all_to_all(copies, 'col', 0, 0, tiled=True, axis_index_groups=same_core)  8.59 us
    pallas_call x12, Pallas kernels, product(): pl.pallas_call(functools.partial(product_kernel, turn, stage, x is not No...  8.57 us
  transfers between devices with their start and end apart: 16, of which 14 were waited for; matrix products, arithmetic and copies ran while one was open for 0% of the time, Pallas kernels for 7%

profile of v6, /device:TPU:1, one launch (start us, length us, event | category | flops | bytes accessed | tf_op | source)
XLA Modules:
  0.0 193.4 jit_solution(5918197342356708826)
XLA Ops:
  0.6 0.7 copy-done.2
  1.4 0.9 shard_map.77
  2.3 8.6 %all-to-all-start = ((bf16[16,128,128]{2,1,0:T(8,128)(2,1)}), bf16[16,128,128]{2,1,0:T(8,128)(2,1)S(1)}, u32[]{:S(2)}, u32[]{:S(2)}) async-start(bf16[16,128,128]{2,1,0:T(8,128)(2,1)} %shard_map.77), calls=%async_computation | async-start | bytes 1048576 | tf_op jit(solution)/shard_map/all_to_all | solution.py:345
  10.9 4.2 %shard_map.78 = (bf16[16,128,512]{2,1,0:T(8,128)(2,1)}, bf16[16,128,512]{2,1,0:T(8,128)(2,1)}) custom-call(bf16[16,2,512,128]{3,2,1,0:T(8,128)(2,1)} %bitcast.17), custom_call_target="tpu_custom_call" | custom-call | flops 4000000000 | bytes 8388608 | tf_op jit(solution)/shard_map/pallas_call | solution.py:105
  15.1 5.0 %shard_map.79 = (bf16[16,128,512]{2,1,0:T(8,128)(2,1)}, bf16[16,128,512]{2,1,0:T(8,128)(2,1)}, f32[128,512]{1,0:T(8,128)S(1)}) custom-call(bf16[16,2,512,128]{3,2,1,0:T(8,128)(2,1)} %bitcast.18, bf16[4,128,4096]{2,1,0:T(8,128)(2,1)} %refs_1_.9), custom_call_target="tpu_custom_call" | custom-call | flops 4000000000 | bytes 8388608 | tf_op jit(solution)/shard_map/pallas_call | solution.py:105
  20.0 1.3 all-to-all-done.own_ref.refs_0_
  21.3 2.4 %shard_map.80 = (f32[128,512]{1,0:T(8,128)S(1)}, bf16[16,128,512]{2,1,0:T(8,128)(2,1)S(1)}, bf16[16,128,512]{2,1,0:T(8,128)(2,1)S(1)}) custom-call(f32[128,512]{1,0:T(8,128)S(1)} %get-tuple-element.29.acc_ref, bf16[16,128,128]{2,1,0:T(8,128)(2,1)S(1)} %all-to-all-done.own_ref.refs_0_, bf16[16,128,512]{2,1,0:T(8,128)(2,1)} %get-tuple-element.30.keep_ref, ...), custom_call_target="tpu_custom_call" | custom-call | flops 268435456 | bytes 4194304 | tf_op jit(solution)/shard_map/pallas_call | solution.py:161
  24.2 2.1 %collective-permute-start.2 = (bf16[16,128,512]{2,1,0:T(8,128)(2,1)S(1)}, bf16[16,128,512]{2,1,0:T(8,128)(2,1)S(1)}, u32[]{:S(2)}, u32[]{:S(2)}) collective-permute-start(bf16[16,128,512]{2,1,0:T(8,128)(2,1)S(1)} %copy-done.6), channel_id=1, source_target_pairs={{0,1},{1,0},{2,3},{3,2},{4,5},{5,4},{6,7},{7,6},{8,9},{9,8},{10,11... | collective-permute-start | bytes 6291464 | tf_op jit(solution)/shard_map/ppermute | solution.py:341
  26.9 6.9 %collective-permute-done.g_ref = bf16[16,128,128]{2,1,0:T(8,128)(2,1)S(1)} collective-permute-done((bf16[16,128,128]{2,1,0:T(8,128)(2,1)S(1)}, bf16[16,128,128]{2,1,0:T(8,128)(2,1)S(1)}, u32[]{:S(2)}, u32[]{:S(2)}) %collective-permute-start) | collective-permute-done | bytes 524320 | tf_op jit(solution)/shard_map/ppermute | solution.py:341
  34.3 1.3 collective-permute-start.1
  35.6 2.8 %collective-permute-done.1.refs_1_ = bf16[128,128]{1,0:T(8,128)(2,1)S(1)} collective-permute-done((bf16[128,128]{1,0:T(8,128)(2,1)S(1)}, bf16[128,128]{1,0:T(8,128)(2,1)S(1)}, u32[]{:S(2)}, u32[]{:S(2)}) %collective-permute-start.1) | collective-permute-done | bytes 32800 | tf_op jit(solution)/shard_map/ppermute | solution.py:369
  38.5 14.4 %all_to_all.35.refs_1_ = bf16[16,128,128]{2,1,0:T(8,128)(2,1)S(1)} all-to-all(bf16[16,128,128]{2,1,0:T(8,128)(2,1)S(1)} %shard_map.83), channel_id=1, replica_groups={{0,2,4,6,8,10,12,14,16,18,20,22,24,26,28,30},{1,3,5,7,9,11,13,15,17,19,..., dimensions={0} | all-to-all | bytes 1048576 | tf_op jit(solution)/shard_map/all_to_all | solution.py:345
  52.9 0.7 shard_map.85
  53.6 2.6 %collective-permute-start.4 = (f32[128,512]{1,0:T(8,128)S(1)}, f32[128,512]{1,0:T(8,128)S(1)}, u32[]{:S(2)}, u32[]{:S(2)}) collective-permute-start(f32[128,512]{1,0:T(8,128)S(1)} %shard_map.85), channel_id=1, source_target_pairs={{0,1},{1,0},{2,3},{3,2},{4,5},{5,4},{6,7},{7,6},{8,9},{9,8},{10,11... | collective-permute-start | bytes 786440 | tf_op jit(solution)/shard_map/ppermute | solution.py:341
  56.2 0.7 shard_map.84.refs_0_
  57.5 4.0 %collective-permute-done.5.refs_1_ = bf16[128,128]{1,0:T(8,128)(2,1)S(1)} collective-permute-done((bf16[128,128]{1,0:T(8,128)(2,1)S(1)}, bf16[128,128]{1,0:T(8,128)(2,1)S(1)}, u32[]{:S(2)}, u32[]{:S(2)}) %collective-permute-start.5) | collective-permute-done | bytes 32800 | tf_op jit(solution)/shard_map/ppermute | solution.py:369
  61.6 18.3 %all_to_all.36.refs_0_ = bf16[16,128,256]{2,1,0:T(8,128)(2,1)S(1)} all-to-all(bf16[16,128,256]{2,1,0:T(8,128)(2,1)S(1)} %shard_map.87), channel_id=1, replica_groups={{0,2,4,6,8,10,12,14,16,18,20,22,24,26,28,30},{1,3,5,7,9,11,13,15,17,19,..., dimensions={0} | all-to-all | bytes 2097152 | tf_op jit(solution)/shard_map/all_to_all | solution.py:345
  80.6 2.6 %collective-permute-start.6 = (f32[128,512]{1,0:T(8,128)S(1)}, f32[128,512]{1,0:T(8,128)S(1)}, u32[]{:S(2)}, u32[]{:S(2)}) collective-permute-start(f32[128,512]{1,0:T(8,128)S(1)} %shard_map.89), channel_id=1, source_target_pairs={{0,1},{1,0},{2,3},{3,2},{4,5},{5,4},{6,7},{7,6},{8,9},{9,8},{10,11... | collective-permute-start | bytes 786440 | tf_op jit(solution)/shard_map/ppermute | solution.py:341
  83.2 0.7 shard_map.88.refs_0_
  84.5 4.0 %collective-permute-done.7.refs_1_ = bf16[128,128]{1,0:T(8,128)(2,1)S(1)} collective-permute-done((bf16[128,128]{1,0:T(8,128)(2,1)S(1)}, bf16[128,128]{1,0:T(8,128)(2,1)S(1)}, u32[]{:S(2)}, u32[]{:S(2)}) %collective-permute-start.7) | collective-permute-done | bytes 32800 | tf_op jit(solution)/shard_map/ppermute | solution.py:369
  88.6 18.3 %all_to_all.37.refs_0_ = bf16[16,128,256]{2,1,0:T(8,128)(2,1)S(1)} all-to-all(bf16[16,128,256]{2,1,0:T(8,128)(2,1)S(1)} %shard_map.91), channel_id=1, replica_groups={{0,2,4,6,8,10,12,14,16,18,20,22,24,26,28,30},{1,3,5,7,9,11,13,15,17,19,..., dimensions={0} | all-to-all | bytes 2097152 | tf_op jit(solution)/shard_map/all_to_all | solution.py:345
  107.7 2.8 %collective-permute-start.8 = (f32[128,512]{1,0:T(8,128)S(1)}, f32[128,512]{1,0:T(8,128)S(1)}, u32[]{:S(2)}, u32[]{:S(2)}) collective-permute-start(f32[128,512]{1,0:T(8,128)S(1)} %shard_map.93), channel_id=1, source_target_pairs={{0,1},{1,0},{2,3},{3,2},{4,5},{5,4},{6,7},{7,6},{8,9},{9,8},{10,11... | collective-permute-start | bytes 786440 | tf_op jit(solution)/shard_map/ppermute | solution.py:341
  111.7 4.0 %collective-permute-done.9.refs_1_ = bf16[128,128]{1,0:T(8,128)(2,1)S(1)} collective-permute-done((bf16[128,128]{1,0:T(8,128)(2,1)S(1)}, bf16[128,128]{1,0:T(8,128)(2,1)S(1)}, u32[]{:S(2)}, u32[]{:S(2)}) %collective-permute-start.9) | collective-permute-done | bytes 32800 | tf_op jit(solution)/shard_map/ppermute | solution.py:369
  115.8 18.4 %all_to_all.38.refs_0_ = bf16[16,128,256]{2,1,0:T(8,128)(2,1)S(1)} all-to-all(bf16[16,128,256]{2,1,0:T(8,128)(2,1)S(1)} %shard_map.95), channel_id=1, replica_groups={{0,2,4,6,8,10,12,14,16,18,20,22,24,26,28,30},{1,3,5,7,9,11,13,15,17,19,..., dimensions={0} | all-to-all | bytes 2097152 | tf_op jit(solution)/shard_map/all_to_all | solution.py:345
  134.9 2.5 %collective-permute-start.10 = (f32[128,512]{1,0:T(8,128)S(1)}, f32[128,512]{1,0:T(8,128)S(1)}, u32[]{:S(2)}, u32[]{:S(2)}) collective-permute-start(f32[128,512]{1,0:T(8,128)S(1)} %shard_map.97), channel_id=1, source_target_pairs={{0,1},{1,0},{2,3},{3,2},{4,5},{5,4},{6,7},{7,6},{8,9},{9,8},{10,11... | collective-permute-start | bytes 786440 | tf_op jit(solution)/shard_map/ppermute | solution.py:341
  138.7 4.0 %collective-permute-done.11.refs_1_ = bf16[128,128]{1,0:T(8,128)(2,1)S(1)} collective-permute-done((bf16[128,128]{1,0:T(8,128)(2,1)S(1)}, bf16[128,128]{1,0:T(8,128)(2,1)S(1)}, u32[]{:S(2)}, u32[]{:S(2)}) %collective-permute-start.11) | collective-permute-done | bytes 32800 | tf_op jit(solution)/shard_map/ppermute | solution.py:369
  142.8 18.4 %all_to_all.39.refs_0_ = bf16[16,128,256]{2,1,0:T(8,128)(2,1)S(1)} all-to-all(bf16[16,128,256]{2,1,0:T(8,128)(2,1)S(1)} %shard_map.99), channel_id=1, replica_groups={{0,2,4,6,8,10,12,14,16,18,20,22,24,26,28,30},{1,3,5,7,9,11,13,15,17,19,..., dimensions={0} | all-to-all | bytes 2097152 | tf_op jit(solution)/shard_map/all_to_all | solution.py:345
  161.9 2.5 %collective-permute-start.12 = (f32[128,512]{1,0:T(8,128)S(1)}, f32[128,512]{1,0:T(8,128)S(1)}, u32[]{:S(2)}, u32[]{:S(2)}) collective-permute-start(f32[128,512]{1,0:T(8,128)S(1)} %shard_map.101), channel_id=1, source_target_pairs={{0,1},{1,0},{2,3},{3,2},{4,5},{5,4},{6,7},{7,6},{8,9},{9,8},{10,11... | collective-permute-start | bytes 786440 | tf_op jit(solution)/shard_map/ppermute | solution.py:341
  165.8 4.0 %collective-permute-done.13.refs_1_ = bf16[128,128]{1,0:T(8,128)(2,1)S(1)} collective-permute-done((bf16[128,128]{1,0:T(8,128)(2,1)S(1)}, bf16[128,128]{1,0:T(8,128)(2,1)S(1)}, u32[]{:S(2)}, u32[]{:S(2)}) %collective-permute-start.13) | collective-permute-done | bytes 32800 | tf_op jit(solution)/shard_map/ppermute | solution.py:369
  169.9 18.4 %all_to_all.40.refs_0_ = bf16[16,128,256]{2,1,0:T(8,128)(2,1)S(1)} all-to-all(bf16[16,128,256]{2,1,0:T(8,128)(2,1)S(1)} %shard_map.103), channel_id=1, replica_groups={{0,2,4,6,8,10,12,14,16,18,20,22,24,26,28,30},{1,3,5,7,9,11,13,15,17,19,..., dimensions={0} | all-to-all | bytes 2097152 | tf_op jit(solution)/shard_map/all_to_all | solution.py:345
  188.9 2.5 %collective-permute-start.14 = (f32[128,512]{1,0:T(8,128)S(1)}, f32[128,512]{1,0:T(8,128)S(1)}, u32[]{:S(2)}, u32[]{:S(2)}) collective-permute-start(f32[128,512]{1,0:T(8,128)S(1)} %shard_map.105), channel_id=1, source_target_pairs={{0,1},{1,0},{2,3},{3,2},{4,5},{5,4},{6,7},{7,6},{8,9},{9,8},{10,11... | collective-permute-start | bytes 786440 | tf_op jit(solution)/shard_map/ppermute | solution.py:341
  192.6 0.8 shard_map.106
  (52 shorter events, 12.1 us)
Async XLA Ops:
  0.6 0.8 copy-start.2
  2.3 19.0 %all-to-all-start = ((bf16[16,128,128]{2,1,0:T(8,128)(2,1)}), bf16[16,128,128]{2,1,0:T(8,128)(2,1)S(1)}, u32[]{:S(2)}, u32[]{:S(2)}) async-start(bf16[16,128,128]{2,1,0:T(8,128)(2,1)} %shard_map.77), calls=%async_computation | async-start | bytes 1048576 | tf_op jit(solution)/shard_map/all_to_all | solution.py:345
  21.3 2.9 %copy-start.6 = (bf16[16,128,512]{2,1,0:T(8,128)(2,1)S(1)}, bf16[16,128,512]{2,1,0:T(8,128)(2,1)}, u32[]{:S(2)}) copy-start(bf16[16,128,512]{2,1,0:T(8,128)(2,1)} %get-tuple-element.37.away_ref) | copy-start | bytes 6291460
  21.3 4.9 %copy-start.7 = (bf16[16,128,512]{2,1,0:T(8,128)(2,1)S(1)}, bf16[16,128,512]{2,1,0:T(8,128)(2,1)}, u32[]{:S(2)}) copy-start(bf16[16,128,512]{2,1,0:T(8,128)(2,1)} %get-tuple-element.38) | copy-start | bytes 6291460
  23.7 10.5 %copy-start.3 = (bf16[1,128,128]{2,1,0:T(8,128)(2,1)S(1)}, bf16[1,128,128]{2,1,0:T(8,128)(2,1)}, u32[]{:S(2)}) copy-start(bf16[1,128,128]{2,1,0:T(8,128)(2,1)} %param.10) | copy-start | bytes 98308
  23.7 10.5 %copy-start.4 = (f32[1,4,128]{2,1,0:T(4,128)S(1)}, f32[1,4,128]{2,1,0:T(4,128)}, u32[]{:S(2)}) copy-start(f32[1,4,128]{2,1,0:T(4,128)} %param.9) | copy-start | bytes 6148
  23.7 10.5 %copy-start.5 = (f32[1,128,128]{2,1,0:T(8,128)S(1)}, f32[1,128,128]{2,1,0:T(8,128)}, u32[]{:S(2)}) copy-start(f32[1,128,128]{2,1,0:T(8,128)} %param.11) | copy-start | bytes 196612
  24.2 28.7 %collective-permute-start.2 = (bf16[16,128,512]{2,1,0:T(8,128)(2,1)S(1)}, bf16[16,128,512]{2,1,0:T(8,128)(2,1)S(1)}, u32[]{:S(2)}, u32[]{:S(2)}) collective-permute-start(bf16[16,128,512]{2,1,0:T(8,128)(2,1)S(1)} %copy-done.6), channel_id=1, source_target_pairs={{0,1},{1,0},{2,3},{3,2},{4,5},{5,4},{6,7},{7,6},{8,9},{9,8},{10,11... | collective-permute-start | bytes 6291464 | tf_op jit(solution)/shard_map/ppermute | solution.py:341
  26.2 26.6 %collective-permute-start.3 = (bf16[16,128,512]{2,1,0:T(8,128)(2,1)S(1)}, bf16[16,128,512]{2,1,0:T(8,128)(2,1)S(1)}, u32[]{:S(2)}, u32[]{:S(2)}) collective-permute-start(bf16[16,128,512]{2,1,0:T(8,128)(2,1)S(1)} %copy-done.7), channel_id=1, source_target_pairs={{0,1},{1,0},{2,3},{3,2},{4,5},{5,4},{6,7},{7,6},{8,9},{9,8},{10,11... | collective-permute-start | bytes 6291464 | tf_op jit(solution)/shard_map/ppermute | solution.py:341
  26.9 6.9 %collective-permute-start = (bf16[16,128,128]{2,1,0:T(8,128)(2,1)S(1)}, bf16[16,128,128]{2,1,0:T(8,128)(2,1)S(1)}, u32[]{:S(2)}, u32[]{:S(2)}) collective-permute-start(bf16[16,128,128]{2,1,0:T(8,128)(2,1)S(1)} %all-to-all-done.own_ref.refs_0_), channel_id=1, source_target_pairs={{0,1},{1,0},{2,3},{3,2},{4,5},{5,4},{6,7},{7,6},{8,9},{9,8},{10,11... | collective-permute-start | bytes 1572872 | tf_op jit(solution)/shard_map/ppermute | solution.py:341
  33.8 19.1 %copy-start = (bf16[4,128,4096]{2,1,0:T(8,128)(2,1)S(1)}, bf16[4,128,4096]{2,1,0:T(8,128)(2,1)}, u32[]{:S(2)}) copy-start(bf16[4,128,4096]{2,1,0:T(8,128)(2,1)} %refs_1_.9) | copy-start | bytes 12582916
  34.3 4.0 %collective-permute-start.1 = (bf16[128,128]{1,0:T(8,128)(2,1)S(1)}, bf16[128,128]{1,0:T(8,128)(2,1)S(1)}, u32[]{:S(2)}, u32[]{:S(2)}) collective-permute-start(bf16[128,128]{1,0:T(8,128)(2,1)S(1)} %get-tuple-element.34.refs_0_.refs_4_.refs_5_), channel_id=1, source_target_pairs={{0,32},{32,64},{64,96},{96,0},{1,33},{33,65},{65,97},{97,1},{2,34}... | collective-permute-start | bytes 98312 | tf_op jit(solution)/shard_map/ppermute | solution.py:369
  52.9 3.3 %copy-start.1 = (bf16[16,128,512]{2,1,0:T(8,128)(2,1)S(1)}, bf16[16,128,512]{2,1,0:T(8,128)(2,1)}, u32[]{:S(2)}) copy-start(bf16[16,128,512]{2,1,0:T(8,128)(2,1)} %get-tuple-element.36.refs_4_.refs_3_.refs_2_) | copy-start | bytes 6291460
  53.6 3.7 %collective-permute-start.4 = (f32[128,512]{1,0:T(8,128)S(1)}, f32[128,512]{1,0:T(8,128)S(1)}, u32[]{:S(2)}, u32[]{:S(2)}) collective-permute-start(f32[128,512]{1,0:T(8,128)S(1)} %shard_map.85), channel_id=1, source_target_pairs={{0,1},{1,0},{2,3},{3,2},{4,5},{5,4},{6,7},{7,6},{8,9},{9,8},{10,11... | collective-permute-start | bytes 786440 | tf_op jit(solution)/shard_map/ppermute | solution.py:341
  57.4 4.0 %collective-permute-start.5 = (bf16[128,128]{1,0:T(8,128)(2,1)S(1)}, bf16[128,128]{1,0:T(8,128)(2,1)S(1)}, u32[]{:S(2)}, u32[]{:S(2)}) collective-permute-start(bf16[128,128]{1,0:T(8,128)(2,1)S(1)} %get-tuple-element.40.refs_0_.refs_4_.refs_6_), channel_id=1, source_target_pairs={{0,32},{32,64},{64,96},{96,0},{1,33},{33,65},{65,97},{97,1},{2,34}... | collective-permute-start | bytes 98312 | tf_op jit(solution)/shard_map/ppermute | solution.py:369
  80.6 3.8 %collective-permute-start.6 = (f32[128,512]{1,0:T(8,128)S(1)}, f32[128,512]{1,0:T(8,128)S(1)}, u32[]{:S(2)}, u32[]{:S(2)}) collective-permute-start(f32[128,512]{1,0:T(8,128)S(1)} %shard_map.89), channel_id=1, source_target_pairs={{0,1},{1,0},{2,3},{3,2},{4,5},{5,4},{6,7},{7,6},{8,9},{9,8},{10,11... | collective-permute-start | bytes 786440 | tf_op jit(solution)/shard_map/ppermute | solution.py:341
  84.4 4.0 %collective-permute-start.7 = (bf16[128,128]{1,0:T(8,128)(2,1)S(1)}, bf16[128,128]{1,0:T(8,128)(2,1)S(1)}, u32[]{:S(2)}, u32[]{:S(2)}) collective-permute-start(bf16[128,128]{1,0:T(8,128)(2,1)S(1)} %get-tuple-element.42.refs_0_.refs_4_.refs_7_), channel_id=1, source_target_pairs={{0,32},{32,64},{64,96},{96,0},{1,33},{33,65},{65,97},{97,1},{2,34}... | collective-permute-start | bytes 98312 | tf_op jit(solution)/shard_map/ppermute | solution.py:369
  107.7 3.9 %collective-permute-start.8 = (f32[128,512]{1,0:T(8,128)S(1)}, f32[128,512]{1,0:T(8,128)S(1)}, u32[]{:S(2)}, u32[]{:S(2)}) collective-permute-start(f32[128,512]{1,0:T(8,128)S(1)} %shard_map.93), channel_id=1, source_target_pairs={{0,1},{1,0},{2,3},{3,2},{4,5},{5,4},{6,7},{7,6},{8,9},{9,8},{10,11... | collective-permute-start | bytes 786440 | tf_op jit(solution)/shard_map/ppermute | solution.py:341
  111.6 4.0 %collective-permute-start.9 = (bf16[128,128]{1,0:T(8,128)(2,1)S(1)}, bf16[128,128]{1,0:T(8,128)(2,1)S(1)}, u32[]{:S(2)}, u32[]{:S(2)}) collective-permute-start(bf16[128,128]{1,0:T(8,128)(2,1)S(1)} %get-tuple-element.44.refs_0_.refs_4_.refs_8_), channel_id=1, source_target_pairs={{0,32},{32,64},{64,96},{96,0},{1,33},{33,65},{65,97},{97,1},{2,34}... | collective-permute-start | bytes 98312 | tf_op jit(solution)/shard_map/ppermute | solution.py:369
  134.9 3.7 %collective-permute-start.10 = (f32[128,512]{1,0:T(8,128)S(1)}, f32[128,512]{1,0:T(8,128)S(1)}, u32[]{:S(2)}, u32[]{:S(2)}) collective-permute-start(f32[128,512]{1,0:T(8,128)S(1)} %shard_map.97), channel_id=1, source_target_pairs={{0,1},{1,0},{2,3},{3,2},{4,5},{5,4},{6,7},{7,6},{8,9},{9,8},{10,11... | collective-permute-start | bytes 786440 | tf_op jit(solution)/shard_map/ppermute | solution.py:341
  138.7 4.0 %collective-permute-start.11 = (bf16[128,128]{1,0:T(8,128)(2,1)S(1)}, bf16[128,128]{1,0:T(8,128)(2,1)S(1)}, u32[]{:S(2)}, u32[]{:S(2)}) collective-permute-start(bf16[128,128]{1,0:T(8,128)(2,1)S(1)} %get-tuple-element.46.refs_0_.refs_4_.refs_9_), channel_id=1, source_target_pairs={{0,32},{32,64},{64,96},{96,0},{1,33},{33,65},{65,97},{97,1},{2,34}... | collective-permute-start | bytes 98312 | tf_op jit(solution)/shard_map/ppermute | solution.py:369
  161.9 3.7 %collective-permute-start.12 = (f32[128,512]{1,0:T(8,128)S(1)}, f32[128,512]{1,0:T(8,128)S(1)}, u32[]{:S(2)}, u32[]{:S(2)}) collective-permute-start(f32[128,512]{1,0:T(8,128)S(1)} %shard_map.101), channel_id=1, source_target_pairs={{0,1},{1,0},{2,3},{3,2},{4,5},{5,4},{6,7},{7,6},{8,9},{9,8},{10,11... | collective-permute-start | bytes 786440 | tf_op jit(solution)/shard_map/ppermute | solution.py:341
  165.7 4.0 %collective-permute-start.13 = (bf16[128,128]{1,0:T(8,128)(2,1)S(1)}, bf16[128,128]{1,0:T(8,128)(2,1)S(1)}, u32[]{:S(2)}, u32[]{:S(2)}) collective-permute-start(bf16[128,128]{1,0:T(8,128)(2,1)S(1)} %get-tuple-element.48.refs_0_.refs_4_.refs_10_), channel_id=1, source_target_pairs={{0,32},{32,64},{64,96},{96,0},{1,33},{33,65},{65,97},{97,1},{2,34}... | collective-permute-start | bytes 98312 | tf_op jit(solution)/shard_map/ppermute | solution.py:369
  188.9 3.7 %collective-permute-start.14 = (f32[128,512]{1,0:T(8,128)S(1)}, f32[128,512]{1,0:T(8,128)S(1)}, u32[]{:S(2)}, u32[]{:S(2)}) collective-permute-start(f32[128,512]{1,0:T(8,128)S(1)} %shard_map.105), channel_id=1, source_target_pairs={{0,1},{1,0},{2,3},{3,2},{4,5},{5,4},{6,7},{7,6},{8,9},{9,8},{10,11... | collective-permute-start | bytes 786440 | tf_op jit(solution)/shard_map/ppermute | solution.py:341
